TPU v7x, 256 devices: a 4x2x16 block of a 4x16x16 slice. The times are simulated.
256 devices in a mesh: rep: 2 (over y), ep: 128 (over x, z, core).
Axes of the slice: x: 4, y: 2, z: 16, core: 2. Of those that a mesh axis runs over, the one named last changes fastest.
The devices are a block of a 4x16x16 slice.
Arguments:
- cache_kv: bfloat16 [512, 2048, 576], P(('rep', 'ep')), parts along dimension 0, may hold values from -6 to 6
- new_kv: bfloat16 [512, 2, 576], P(('rep', 'ep')), parts along dimension 0, may hold values from -6 to 6
- queries: bfloat16 [512, 2, 64, 576], P(('rep', 'ep')), parts along dimension 0, may hold values from -256 to 256
- lengths: int32 [512], P(('rep', 'ep')), parts along dimension 0, may hold values from 256 to 2048
- resid: bfloat16 [512, 2, 7168], P(('rep', 'ep')), parts along dimension 0, may hold values from -18 to 18
- value_up: bfloat16 [512, 8192], P(None, 'ep'), may hold values from -1.5 to 1.5
- out_proj: bfloat16 [8192, 7168], P('ep'), may hold values from -0.09375 to 0.09375
- norm_gain: bfloat16 [7168], replicated, may hold values from 0.25 to 1.75
- router: bfloat16 [7168, 16], replicated, may hold values from -0.0625 to 0.0625
- expert_ids: int32 [512, 2, 8], P(('rep', 'ep')), parts along dimension 0, may hold values from 0 to 15, as said below
- slots: int32 [512, 2, 8], P(('rep', 'ep')), parts along dimension 0, may hold values from 0 to 3, as said below
- w_gate: bfloat16 [7168, 16384], P(None, 'ep'), may hold values from -0.0625 to 0.0625
- w_up: bfloat16 [7168, 16384], P(None, 'ep'), may hold values from -0.0625 to 0.0625
- w_down: bfloat16 [16384, 7168], P('ep'), may hold values from -0.1875 to 0.1875
Outputs:
- mixed: bfloat16 [512, 2, 7168], P(('rep', 'ep')), parts along dimension 0
There are 2 independent parts, one for each index of `rep`. A program takes and returns all parts, laid end to end along the dimension named above; an argument that names none is the same for every part. Nothing has to cross between parts.
Inputs may be any that keep to these rules, and one draw needn't show every extreme that they name: `expert_ids`: each row names 8 different experts. In each aligned block of 4 rows (the rows of one device), the rows that name the same expert carry the distinct slots 0 up to their number minus one for it; in every block some expert is named by all 4 rows.
All inputs are finite; a program needn't handle non-finite values.
Results may differ from a plain program's by a relative error of at most 0.0065.
Values may be sent and summed in bfloat16 or wider, within the bound.
No kernel may reach another device: no remote copies, remote signals or barrier semaphores. Data moves between devices by JAX's collectives and lax.ppermute only.
A program may use at most 128 MiB of HBM per device.

v0:
```python
import functools
import math

import jax
import jax.numpy as jnp
from jax import lax
from jax.experimental import pallas as pl
from jax.experimental.pallas import tpu as pltpu
from jax.sharding import Mesh
from jax.sharding import PartitionSpec as P


D = 7168
LAT = 512
EXPERTS = 16
TOP = 8
CAP = 2
QK = 192

CORES = 2
NEAR = 4
FAR = 4
RING = NEAR * FAR
SLOTS = RING * CAP
LATE = FAR * CAP
EARLY = SLOTS - LATE
EXTRA = 128

route_scale = 2.827
norm_eps = 1e-06


ZAX = ("zb", "j")
f32, bf16 = jnp.float32, jnp.bfloat16
NT = (((1,), (1,)), ((), ()))


def swap_x(a, bits):
    return lax.ppermute(a, "x", [(i, i ^ bits) for i in range(lax.axis_size("x"))])


def swap_x_by_group(a, even, odd):
    nx = lax.axis_size("x")
    bits = [odd if g % 2 and paired() else even for g in range(lax.axis_size("rep"))]
    return lax.ppermute(a, ("rep", "x"), [(g * nx + i, g * nx + (i ^ b)) for g, b in enumerate(bits) for i in range(nx)])


def paired():
    return lax.axis_size("rep") % 2 == 0


def swap_group(a):
    return lax.ppermute(a, "rep", [(i, i ^ 1) for i in range(lax.axis_size("rep"))])


def shift_z(a, step):
    return lax.ppermute(a, ZAX, [(i, (i + step) % RING) for i in range(RING)])


def swap_far(a, bits):
    return lax.ppermute(a, "zb", [(i, i ^ bits) for i in range(FAR)])


def swap_core(a):
    return lax.ppermute(a, "c", [(i, i ^ 1) for i in range(CORES)])


def iota(shape, axis):
    return lax.broadcasted_iota(jnp.int32, shape, axis)


def one_hot(mask):
    return jnp.where(mask, 1.0, 0.0).astype(bf16)


COLUMNS = (0, 1, 3, 2)


def column(index, x):
    return x ^ jnp.where(index == 2, 3, jnp.where(index == 3, 2, index))


STEPS = (0, 1, RING - 1, 2, RING - 2)


def chip_at(place, where_ref):
    group, bits = place // FAR, lax.rem(place, FAR)
    step = 0
    for i, value in enumerate(STEPS):
        step = jnp.where(group == i, value, step)
    chip = lax.rem(NEAR * where_ref[1] + where_ref[2] + step, RING)
    return NEAR * ((chip // NEAR) ^ bits) + lax.rem(chip, NEAR)


def of_tile(rows, n, tiles):
    size = rows.shape[0] // len(STEPS)
    if n < tiles // 2:
        return rows[: 4 * size]
    return jnp.concatenate([rows[: 3 * size], rows[4 * size :]], axis=0)


def smem():
    return pl.BlockSpec(memory_space=pltpu.SMEM)


def vmem():
    return pl.BlockSpec(memory_space=pltpu.VMEM)


def hbm():
    return pl.BlockSpec(memory_space=pltpu.HBM)


def held_in_hbm(a):
    return pltpu.with_memory_space_constraint(a, pltpu.HBM)


def held_in_vmem(a):
    return pltpu.with_memory_space_constraint(a, pltpu.VMEM)


def params(mib):
    return pltpu.CompilerParams(vmem_limit_bytes=mib << 20)


def cost(flops, nbytes):
    return pl.CostEstimate(flops=flops, bytes_accessed=nbytes, transcendentals=0)


def context_kernel(nx, where_ref, keys, queries, new, out, held):
    seq = pl.program_id(0)
    seqs = pl.num_programs(0)
    steps, heads = queries.shape[1], queries.shape[2]
    count = steps * heads
    scale = 1.0 / math.sqrt(QK)
    query = queries[0].reshape(count, queries.shape[3])
    score = jnp.dot(query, keys[0], preferred_element_type=f32) * scale
    score = jnp.where(iota(score.shape, 1) < where_ref[3 + seq], score, -jnp.inf)
    wide = query.astype(f32)
    step_of = iota((count, 1), 0) // heads
    latest = []
    peak = jnp.max(score, axis=1, keepdims=True)
    for t in range(steps):
        key = new[0, t : t + 1, :].astype(f32)
        got = jnp.sum(wide * key, axis=1, keepdims=True) * scale
        got = jnp.where(step_of >= t, got, -jnp.inf)
        latest.append(got)
        peak = jnp.maximum(peak, got)
    probs = jnp.exp(score - peak)
    total = jnp.sum(probs, axis=1, keepdims=True)
    latest = [jnp.exp(got - peak) for got in latest]
    for got in latest:
        total = total + got
    share = 1.0 / total
    probs = (probs * share).astype(bf16)
    context = lax.dot_general(probs, keys[0, :LAT, :], NT, preferred_element_type=f32)
    for t, got in enumerate(latest):
        part = (got * share).astype(bf16).astype(f32)
        context = context + part * new[0, t : t + 1, :LAT].astype(f32)
    held[pl.ds(pl.multiple_of(seq * count, count), count), :] = context.astype(bf16)

    @pl.when(seq == seqs - 1)
    def _():
        rows = held.shape[0]
        tok = rows // heads
        shape = (rows, rows)
        to, source = iota(shape, 0), iota(shape, 1)
        hop = lax.rem(to // tok, nx)
        head = column(hop, where_ref[0]) * RING + to // (tok * nx)
        take = (lax.rem(to, tok) == source // heads) & (head == lax.rem(source, heads))
        out[...] = jnp.dot(one_hot(take), held[...], preferred_element_type=f32).astype(bf16)


def context_rows(where, nx, cache_kv, new_kv, queries):
    seqs, length, width = cache_kv.shape
    steps, heads = queries.shape[1:3]
    rows = seqs * steps * heads
    keys = jnp.swapaxes(cache_kv, 1, 2)
    return pl.pallas_call(
        functools.partial(context_kernel, nx),
        grid=(seqs,),
        out_shape=jax.ShapeDtypeStruct((rows, LAT), bf16),
        in_specs=[
            smem(),
            pl.BlockSpec((1, width, length), lambda b: (b, 0, 0)),
            pl.BlockSpec((1, steps, heads, width), lambda b: (b, 0, 0, 0)),
            pl.BlockSpec((1, steps, width), lambda b: (b, 0, 0)),
        ],
        out_specs=pl.BlockSpec((rows, LAT), lambda b: (0, 0)),
        scratch_shapes=[pltpu.VMEM((rows, LAT), bf16)],
        compiler_params=params(24),
        cost_estimate=cost(2 * rows * length * (width + LAT), 2 * cache_kv.size),
        name="context_rows",
    )(where, held_in_hbm(keys), held_in_hbm(queries), held_in_hbm(new_kv))


def pack_kernel(up, rows, tops, lows, sem):
    half, at = tops.shape[0], up.shape[1]
    copies = []
    for i, out in enumerate((tops, lows)):
        part = pl.ds(i * half, half)
        copies.append(pltpu.make_async_copy(rows.at[part], out.at[:, pl.ds(at, rows.shape[1])], sem.at[i, 0]))
        copies.append(pltpu.make_async_copy(up.at[part], out.at[:, pl.ds(0, at)], sem.at[i, 1]))
    for copy in copies:
        copy.start()
    for copy in copies:
        copy.wait()


def pack(up, rows):
    shape = (rows.shape[0] // 2, up.shape[1] + rows.shape[1])
    return pl.pallas_call(
        pack_kernel,
        out_shape=(jax.ShapeDtypeStruct(shape, bf16),) * 2,
        in_specs=[hbm()] * 2,
        out_specs=[vmem()] * 2,
        scratch_shapes=[pltpu.SemaphoreType.DMA((2, 2))],
        compiler_params=params(12),
        cost_estimate=cost(1, 4 * rows.size),
        name="pack",
    )(held_in_hbm(up), held_in_hbm(rows))


HALVES = 2
TILE = 256


def put_rows(got, outs, n):
    own, right, left, ahead, behind = outs
    size, width = own.shape[0], ahead.shape[1]
    cols = pl.ds(n * TILE, TILE)
    own[:, cols] = got[:size]
    right[:, cols] = got[size : 2 * size].astype(bf16)
    left[:, cols] = got[2 * size : 3 * size].astype(bf16)
    last, at = (ahead, n * TILE) if n * TILE < width else (behind, n * TILE - width)
    last[:, pl.ds(at, TILE)] = got[3 * size :].astype(bf16)


def row_shapes(size, width):
    return (
        jax.ShapeDtypeStruct((size, width), f32),
        jax.ShapeDtypeStruct((size, width), bf16),
        jax.ShapeDtypeStruct((size, width), bf16),
        jax.ShapeDtypeStruct((size, width // 2), bf16),
        jax.ShapeDtypeStruct((size, width // 2), bf16),
    )


def tiles_of(parts, at, n):
    half = (parts[0].shape[1] - at) // HALVES
    got = [p[:, pl.ds(at + c * half + n * TILE, TILE)] for c in range(HALVES) for p in parts]
    return jnp.concatenate(got, axis=0)


def attend_kernel(tok, nx, count, hops, last, where_ref, arrived, *refs):
    pieces, outs = refs[:count], refs[count:]
    if last:
        before, outs = outs[0], outs[1:]
    up = jnp.concatenate([piece[:, pl.ds(0, LAT)] for piece in pieces], axis=0)
    values = lax.dot_general(arrived[...], up, NT, preferred_element_type=f32)
    hop = lax.rem(iota(values.shape, 0) // tok, nx)
    odd = where_ref[where_ref.shape[0] - 1]
    part = iota(values.shape, 1) // (up.shape[0] // len(hops))
    wanted = 0
    for i, (at, step) in enumerate(hops):
        wanted = jnp.where(part == i, at + step * odd, wanted)
    values = jnp.where(hop == wanted, values, 0.0).astype(bf16)
    shape = (len(STEPS) * FAR * HALVES * tok, arrived.shape[0])
    row, source = iota(shape, 0), iota(shape, 1)
    chip = chip_at(row // (HALVES * tok), where_ref)
    take = (source // (tok * nx) == chip) & (lax.rem(source, tok) == lax.rem(row, tok))
    half = lax.rem(row // tok, HALVES)
    taken = [
        jnp.dot(one_hot(take & (half == c)), values, preferred_element_type=f32).astype(bf16)
        for c in range(HALVES)
    ]
    values = jnp.concatenate(taken, axis=1)
    tiles = outs[0].shape[1] // TILE
    for n in range(tiles):
        got = jnp.dot(of_tile(values, n, tiles), tiles_of(pieces, LAT, n), preferred_element_type=f32)
        cols = pl.ds(n * TILE, TILE)
        if last:
            put_rows(before[:, cols] + got, outs, n)
        else:
            outs[0][:, cols] = got


def attend_part(where, nx, arrived, pieces, tok, hops, before):
    depth = sum(p.shape[0] for p in pieces)
    width = (pieces[0].shape[1] - LAT) // HALVES
    count = len(pieces)
    last = before is not None
    part = jax.ShapeDtypeStruct((RING * HALVES * tok, width), f32)
    return pl.pallas_call(
        functools.partial(attend_kernel, tok, nx, count, hops, last),
        out_shape=row_shapes(FAR * HALVES * tok, width) if last else part,
        in_specs=[smem(), vmem()] + [vmem()] * count + [vmem()] * last,
        out_specs=[vmem()] * 5 if last else vmem(),
        compiler_params=params(6),
        cost_estimate=cost(8 * RING * tok * depth * width * HALVES, 4 * depth * width),
        name="attend_part",
    )(where, arrived, *pieces, *([before] if last else []))


SEND_TILE = 512


def dispatch_kernel(tok, nx, where_ref, tokens, *refs):
    outs, (early, late) = refs[:nx], refs[nx:]
    count, width = tokens.shape
    half = width - EXTRA
    table = tokens[:, pl.ds(half, EXTRA)]
    shape = (nx * CAP, EXTRA)
    row, place = iota(shape, 0), iota(shape, 1)
    expert = FAR * column(row // CAP, where_ref[0]) + where_ref[1]
    hot = one_hot(place == lax.rem(row, CAP) * EXPERTS + expert)
    got = lax.dot_general(hot, table, NT, preferred_element_type=f32)
    shape = (SLOTS, count)
    slot, token = iota(shape, 0), iota(shape, 1)
    source = slot // CAP
    chip = NEAR * lax.rem(source, FAR) + lax.rem(where_ref[2] + source // FAR + 1, NEAR)
    parts = []
    for r in range(nx):
        sel = jnp.where(lax.rem(slot, CAP) == 0, got[CAP * r : CAP * r + 1], got[CAP * r + 1 : CAP * r + 2])
        parts.append(jnp.where(chip == token // (HALVES * tok), sel, 0.0))
    of_half = lax.rem(token // tok, HALVES)
    halves = [[jnp.where(of_half == c, sel, 0.0) for sel in parts] for c in range(HALVES)]
    both = jnp.concatenate(sum(halves, []), axis=0).astype(bf16)
    rows = nx * SLOTS
    for n in range(half // SEND_TILE):
        got = jnp.dot(both, tokens[:, pl.ds(n * SEND_TILE, SEND_TILE)], preferred_element_type=f32).astype(bf16)
        for c in range(HALVES):
            for r in range(nx):
                at = c * rows + r * SLOTS
                outs[r][:, pl.ds(c * half + n * SEND_TILE, SEND_TILE)] = got[at : at + SLOTS]
    got = jnp.dot(both[:rows], table, preferred_element_type=f32).astype(bf16)
    for r in range(nx):
        outs[r][:, pl.ds(HALVES * half, EXTRA)] = got[r * SLOTS : (r + 1) * SLOTS]
    for out, group, at, end in ((early, 1, 0, EARLY), (late, 0, EARLY, SLOTS)):
        shape = (out.shape[0], count)
        row, token = iota(shape, 0), iota(shape, 1)
        chip = chip_at(group * FAR + row // (HALVES * tok), where_ref)
        take = (token // (HALVES * tok) == chip) & (lax.rem(token, HALVES * tok) == lax.rem(row, HALVES * tok))
        sel = jnp.concatenate([sel[at:end] for sels in halves for sel in sels], axis=0).astype(bf16)
        out[...] = lax.dot_general(one_hot(take), sel, NT, preferred_element_type=f32).astype(bf16)


def dispatch(where, nx, tokens, tok):
    count, width = tokens.shape
    full = HALVES * (width - EXTRA) + EXTRA
    near = count // NEAR
    return pl.pallas_call(
        functools.partial(dispatch_kernel, tok, nx),
        out_shape=(jax.ShapeDtypeStruct((SLOTS, full), bf16),) * nx
        + (
            jax.ShapeDtypeStruct(((len(STEPS) - 1) * near, HALVES * nx * EARLY), bf16),
            jax.ShapeDtypeStruct((near, HALVES * nx * LATE), bf16),
        ),
        in_specs=[smem(), vmem()],
        out_specs=[vmem()] * (nx + 2),
        compiler_params=params(12),
        cost_estimate=cost(2 * nx * SLOTS * count * full, 4 * count * width),
        name="dispatch",
    )(where, tokens)


CHUNKS = 7


def stage_kernel(gate_a, gate_b, up_a, up_b, down_a, down_b, wide, deep, sem):
    part = gate_a.shape[1]
    copies = [
        pltpu.make_async_copy(ref, wide.at[:, pl.ds(i * part, part)], sem.at[i])
        for i, ref in enumerate((gate_a, gate_b, up_a, up_b))
    ]
    copies += [
        pltpu.make_async_copy(ref, deep.at[pl.ds(i * part, part)], sem.at[4 + i])
        for i, ref in enumerate((down_a, down_b))
    ]
    for copy in copies:
        copy.start()
    for copy in copies:
        copy.wait()


def stage(weights):
    dim, part = weights[0].shape
    return pl.pallas_call(
        stage_kernel,
        out_shape=(
            jax.ShapeDtypeStruct((dim, 4 * part), bf16),
            jax.ShapeDtypeStruct((2 * part, dim), bf16),
        ),
        in_specs=[hbm()] * 6,
        out_specs=[vmem()] * 2,
        scratch_shapes=[pltpu.SemaphoreType.DMA((6,))],
        compiler_params=params(4),
        cost_estimate=cost(4 * 1000 * dim * part, 12 * dim * part),
        name="stage",
    )(*[held_in_hbm(w) for w in weights])


def expert_kernel(groups, where_ref, *refs):
    tokens = refs[:groups]
    wide, deep = refs[groups : groups + 2]
    early, late = refs[groups + 2 : 2 * groups + 2], refs[2 * groups + 2 : 3 * groups + 2]
    held = refs[3 * groups + 2] if groups > 1 else tokens[0]
    dim = wide.shape[0]
    part = wide.shape[1] // 2
    chunk = dim // CHUNKS
    if groups > 1:
        for g, ref in enumerate(tokens):
            held[pl.ds(g * SLOTS, SLOTS)] = ref[...]
    total = jnp.dot(held[:, pl.ds(0, dim)], wide[...], preferred_element_type=f32)
    gate, upward = total[:, :part], total[:, part:]
    act = (gate / (1.0 + jnp.exp(-gate)) * upward).astype(bf16)
    shape = (EXTRA, EXTRA)
    expert = FAR * where_ref[0] + where_ref[1]
    from_share = iota(shape, 0) - CAP * EXPERTS
    hot = (from_share >= 0) & (from_share < 3 * EXPERTS) & (lax.rem(from_share + EXTRA, EXPERTS) == expert)
    share = jnp.dot(held[:, pl.ds(dim, EXTRA)], one_hot(hot), preferred_element_type=f32)[:, :1]
    for k in range(CHUNKS):
        cols = pl.ds(k * chunk, chunk)
        got = jnp.dot(act, deep[:, cols], preferred_element_type=f32) * share
        for g in range(groups):
            rows = got[g * SLOTS : (g + 1) * SLOTS].astype(bf16)
            early[g][:, cols] = rows[:EARLY]
            late[g][:, cols] = rows[EARLY:]


def expert_part(where, tokens, weights):
    wide, deep = weights
    dim = wide.shape[0]
    groups = len(tokens)
    rows = groups * SLOTS
    held = [pltpu.VMEM((rows, dim + EXTRA), bf16)] if groups > 1 else []
    return pl.pallas_call(
        functools.partial(expert_kernel, groups),
        out_shape=(jax.ShapeDtypeStruct((EARLY, dim), bf16),) * groups
        + (jax.ShapeDtypeStruct((LATE, dim), bf16),) * groups,
        in_specs=[smem()] + [vmem()] * (groups + 2),
        out_specs=[vmem()] * (2 * groups),
        scratch_shapes=held,
        compiler_params=params(8),
        cost_estimate=cost(6 * rows * wide.size, 2 * rows * dim),
        name="expert_part",
    )(where, *tokens, held_in_vmem(wide), held_in_vmem(deep))


def collect_kernel(count, spread, *refs):
    parts, (right, left, ahead, behind) = refs[:count], refs[count:]
    size = right.shape[0]
    tiles = right.shape[1] // TILE
    for n in range(tiles):
        cols = pl.ds(n * TILE, TILE)
        rows = spread[...]
        first = n < tiles // 2
        rows = rows[: 3 * size] if first else jnp.concatenate([rows[: 2 * size], rows[3 * size :]], axis=0)
        got = jnp.dot(rows, tiles_of(parts, 0, n), preferred_element_type=f32).astype(bf16)
        right[:, cols] = got[:size]
        left[:, cols] = got[size : 2 * size]
        last, at = (ahead, n * TILE) if first else (behind, (n - tiles // 2) * TILE)
        last[:, pl.ds(at, TILE)] = got[2 * size :]


def collect(spread, parts):
    width = parts[0].shape[1] // HALVES
    count = len(parts)
    return pl.pallas_call(
        functools.partial(collect_kernel, count),
        out_shape=row_shapes(spread.shape[0] // (len(STEPS) - 1), width)[1:],
        in_specs=[vmem()] * (count + 1),
        out_specs=[vmem()] * 4,
        compiler_params=params(12),
        cost_estimate=cost(2 * spread.size * width, 4 * spread.shape[0] * width),
        name="collect",
    )(spread, *parts)


def merge_kernel(count, *refs):
    mine, (right, left, ahead, behind, first), rest = refs[:count], refs[count : count + 5], refs[count + 5 :]
    block = first.shape[0]
    tiles = first.shape[1] // TILE
    for n in range(tiles):
        cols = pl.ds(n * TILE, TILE)
        if count == 1:
            total = mine[0][:, cols]
        else:
            total = jnp.dot(mine[0][...], tiles_of(mine[1:], 0, n), preferred_element_type=f32)
        last, at = (ahead, n * TILE) if n < tiles // 2 else (behind, (n - tiles // 2) * TILE)
        total = total + right[:, cols].astype(f32) + left[:, cols].astype(f32)
        total = total + last[:, pl.ds(at, TILE)].astype(f32)
        first[:, cols] = total[:block]
        for k, out in enumerate(rest):
            out[:, cols] = total[(k + 1) * block : (k + 2) * block].astype(bf16)


def merge(mine, others):
    size, width = others[0].shape
    block = (size // FAR, width)
    return pl.pallas_call(
        functools.partial(merge_kernel, len(mine)),
        out_shape=(jax.ShapeDtypeStruct(block, f32),) + (jax.ShapeDtypeStruct(block, bf16),) * (FAR - 1),
        in_specs=[vmem()] * (len(mine) + 4),
        out_specs=[vmem()] * FAR,
        compiler_params=params(4),
        cost_estimate=cost(4 * size * width, 12 * size * width),
        name="merge",
    )(*mine, *others)


def half_swap(a):
    middle = a.shape[0] // 2
    return jnp.concatenate([a[middle:], a[:middle]], axis=0)


def route_kernel(first, one, two, three, rows, gain, router, ids, slots, hidden, payload):
    count, half = rows.shape
    total = first[...] + one[...].astype(f32) + two[...].astype(f32) + three[...].astype(f32)
    total = rows[...].astype(f32) + total
    hidden[...] = total
    square = jnp.sum(total * total, axis=1, keepdims=True)
    scale = lax.rsqrt((square + half_swap(square)) / D + norm_eps)
    normed = (total * scale * gain[...]).astype(bf16)
    payload[:, pl.ds(0, half)] = normed
    parts = [
        lax.dot_general(normed, router[:, pl.ds(c * half, half)], NT, preferred_element_type=f32)
        for c in range(HALVES)
    ]
    logits = jnp.where(iota(parts[0].shape, 0) < count // 2, parts[0], parts[1])
    logits = logits + half_swap(logits)
    logits = jnp.concatenate([logits] * (EXTRA // EXPERTS), axis=1)
    lane = iota(logits.shape, 1)
    place = jnp.zeros(logits.shape, jnp.int32)
    for k in range(TOP):
        place = jnp.where(lax.rem(lane, EXPERTS) == ids[:, k : k + 1], slots[:, k : k + 1] + 1, place)
    gates = jnp.where(place > 0, 1.0 / (1.0 + jnp.exp(-logits)), 0.0)
    share = route_scale * gates / jnp.sum(jnp.where(lane < EXPERTS, gates, 0.0), axis=1, keepdims=True)
    kind = lane // EXPERTS
    table = jnp.zeros(logits.shape, f32)
    for n in range(CAP):
        table = jnp.where((kind == n) & (place == n + 1), 1.0, table)
    rest = share
    for n in range(3):
        piece = rest.astype(bf16).astype(f32)
        table = jnp.where(kind == CAP + n, piece, table)
        rest = rest - piece
    payload[:, pl.ds(half, EXTRA)] = table.astype(bf16)


def route(added, rows, gain, router, ids, slots):
    count, half = rows.shape
    return pl.pallas_call(
        route_kernel,
        out_shape=(
            jax.ShapeDtypeStruct((count, half), f32),
            jax.ShapeDtypeStruct((count, half + EXTRA), bf16),
        ),
        in_specs=[vmem()] * 9,
        out_specs=[vmem()] * 2,
        compiler_params=params(4),
        cost_estimate=cost(4 * count * half * EXPERTS, 20 * count * half),
        name="route",
    )(*added, rows, gain, router, ids, slots)


def finish_kernel(hidden, first, one, two, three, out):
    seqs, steps, _ = out.shape
    half = hidden.shape[1]
    total = first[...] + one[...].astype(f32) + two[...].astype(f32) + three[...].astype(f32)
    total = (hidden[...] + total).astype(bf16)
    for c in range(HALVES):
        for b in range(seqs):
            at = (c * seqs + b) * steps
            out[b, :, pl.ds(c * half, half)] = total[at : at + steps]


def finish(hidden, added, shape):
    return pl.pallas_call(
        finish_kernel,
        out_shape=jax.ShapeDtypeStruct(shape, bf16),
        in_specs=[vmem()] * 5,
        out_specs=vmem(),
        compiler_params=params(4),
        cost_estimate=cost(5 * hidden.size, 14 * hidden.size),
        name="finish",
    )(hidden, *added)


def reduce_z(mine, right, left, ahead, behind):
    others = shift_z(right, 1), shift_z(left, -1), shift_z(ahead, 2), shift_z(behind, -2)
    first, *sent = merge(mine, others)
    others = [swap_far(rows, k + 1) for k, rows in enumerate(sent)]
    return first, *others


def layer(
    cache_kv,
    new_kv,
    queries,
    lengths,
    resid,
    value_up,
    out_proj,
    norm_gain,
    router,
    expert_ids,
    slots,
    w_gate,
    w_up,
    w_down,
):
    nx = lax.axis_size("x")
    seqs, steps = queries.shape[:2]
    tok = seqs * steps
    where = jnp.stack([lax.axis_index(a) for a in ("x", "zb", "j")]).astype(jnp.int32)
    odd = lax.rem(lax.axis_index("rep"), 2) if paired() else jnp.int32(0)
    where = jnp.concatenate([where, lengths.astype(jnp.int32), odd.astype(jnp.int32).reshape(1)])

    tops, lows = pack(value_up.T, out_proj)
    top_near, low_near = swap_x_by_group(tops, 1, 3), swap_x_by_group(lows, 3, 1)
    outgoing = context_rows(where, nx, cache_kv, new_kv, queries)
    arrived = lax.all_to_all(
        outgoing.reshape(RING, nx * tok, LAT), ZAX, split_axis=0, concat_axis=0, tiled=True
    )
    if paired():
        top_other, low_other = swap_group(top_near), swap_group(low_near)
    else:
        top_other, low_other = swap_x(tops, 3), swap_x(lows, 1)
    top_far, low_far = swap_x_by_group(top_near, 3, 1), swap_x_by_group(low_near, 1, 3)
    near = [top_near, swap_core(top_near), low_near, swap_core(low_near)]
    near += [top_far, low_far, swap_core(top_far), swap_core(low_far)]
    near += [tops, lows, swap_core(tops), swap_core(lows)]
    beyond = [top_other, swap_core(top_other), low_other, swap_core(low_other)]
    others = [swap_core(w) for w in (w_gate, w_up, w_down)]
    weights = stage((w_gate, others[0], w_up, others[1], w_down, others[2]))
    arrived = arrived.reshape(RING * nx * tok, LAT)
    most = attend_part(where, nx, arrived, near, tok, ((1, 1), (2, -1), (3, 0), (3, 0), (0, 0), (0, 0)), None)
    own, *rows = attend_part(where, nx, arrived, beyond, tok, ((2, -1), (1, 1)), most)
    added = reduce_z((own,), *rows)

    half = D // HALVES
    rows = resid.reshape(tok, HALVES, half).swapaxes(0, 1).reshape(HALVES * tok, half)
    gain = jnp.repeat(norm_gain.astype(f32).reshape(HALVES, half), tok, axis=0)
    ids, places = [
        jnp.tile(a.reshape(tok, TOP).astype(jnp.int32), (HALVES, 1)) for a in (expert_ids, slots)
    ]
    hidden, payload = route(added, rows, gain, router.T, ids, places)

    ring = lax.all_gather(payload, ZAX, axis=0, tiled=True)
    *sent, early, late = dispatch(where, nx, ring, tok)
    got = [swap_x(sent[i], COLUMNS[i]) for i in range(1, nx)]
    done = expert_part(where, (sent[0], *got[: nx - 2]), weights)
    done = [list(done[: nx - 1]), list(done[nx - 1 :])]
    for rows, last in zip(done, expert_part(where, got[nx - 2 :], weights)):
        rows.append(last)
    first = [done[0][0]] + [swap_x(done[0][i], COLUMNS[i]) for i in range(1, nx)]
    second = [done[1][0]] + [swap_x(done[1][i], COLUMNS[i]) for i in range(1, nx)]
    added = reduce_z((late, *second), *collect(early, first))
    return finish(hidden, added, resid.shape)


def solution(mesh):
    chips = mesh.shape["ep"] // (RING * CORES)
    grid = mesh.devices.reshape(mesh.shape["rep"], chips, FAR, NEAR, CORES)
    fine = Mesh(grid, ("rep", "x", "zb", "j", "c"))
    ep = ("x", "zb", "j", "c")
    both = ("rep",) + ep
    return jax.shard_map(
        layer,
        mesh=fine,
        in_specs=(
            P(both, None, None),
            P(both, None, None),
            P(both, None, None, None),
            P(both),
            P(both, None, None),
            P(None, ep),
            P(ep, None),
            P(),
            P(),
            P(both, None, None),
            P(both, None, None),
            P(None, ep),
            P(None, ep),
            P(ep, None),
        ),
        out_specs=P(both, None, None),
        check_vma=False,
    )
```

profile of v0, /device:TPU:34, one launch (start us, length us, event | category | flops | bytes accessed | tf_op | source)
XLA Modules:
  0.0 232.7 jit_solution(9065530113633848586)
XLA Ops:
  0.0 1.2 pack.1
  1.2 19.5 %collective-permute-start = (bf16[32,7680]{1,0:T(8,128)(2,1)S(1)}, bf16[32,7680]{1,0:T(8,128)(2,1)S(1)}, u32[]{:S(2)}, u32[]{:S(2)}) collective-permute-start(bf16[32,7680]{1,0:T(8,128)(2,1)S(1)} %get-tuple-element.42.refs_8_), channel_id=1, source_target_pairs={{0,32},{32,0},{64,96},{96,64},{128,224},{160,192},{192,160},{224,1... | collective-permute-start | bytes 1474568 | tf_op jit(solution)/shard_map/ppermute | solution.py:45
  20.7 0.5 collective-permute-start.13
  21.2 6.3 %collective-permute-done.refs_0_ = bf16[32,7680]{1,0:T(8,128)(2,1)S(1)} collective-permute-done((bf16[32,7680]{1,0:T(8,128)(2,1)S(1)}, bf16[32,7680]{1,0:T(8,128)(2,1)S(1)}, u32[]{:S(2)}, u32[]{:S(2)}) %collective-permute-start) | collective-permute-done | bytes 491552 | tf_op jit(solution)/shard_map/ppermute | solution.py:45
  27.6 7.1 %collective-permute-done.3.refs_2_ = bf16[32,7680]{1,0:T(8,128)(2,1)S(1)} collective-permute-done((bf16[32,7680]{1,0:T(8,128)(2,1)S(1)}, bf16[32,7680]{1,0:T(8,128)(2,1)S(1)}, u32[]{:S(2)}, u32[]{:S(2)}) %collective-permute-start.3) | collective-permute-done | bytes 491552 | tf_op jit(solution)/shard_map/ppermute | solution.py:45
  34.7 1.4 collective-permute-start.9
  36.2 3.7 %collective-permute-done.8.refs_4_ = bf16[32,7680]{1,0:T(8,128)(2,1)S(1)} collective-permute-done((bf16[32,7680]{1,0:T(8,128)(2,1)S(1)}, bf16[32,7680]{1,0:T(8,128)(2,1)S(1)}, u32[]{:S(2)}, u32[]{:S(2)}) %collective-permute-start.8) | collective-permute-done | bytes 491552 | tf_op jit(solution)/shard_map/ppermute | solution.py:45
  39.9 0.8 copy-done
  40.8 0.7 concatenate.3.where_ref
  41.5 5.9 %context_rows.1 = bf16[256,512]{1,0:T(8,128)(2,1)} custom-call(s32[6]{0:T(128)S(1)} %concatenate.3.where_ref, bf16[2,576,2048]{2,1,0:T(8,128)(2,1)} %bitcast.21, bf16[2,2,64,576]{3,2,1,0:T(8,128)(2,1)} %queries.1, bf16[2,2,576]{2,1,0:T(2,128)(2,1)} %new.1), custom_call_target="tpu_custom_call" | custom-call | flops 1140850688 | bytes 4718592 | tf_op jit(solution)/shard_map/context_rows/pallas_call | solution.py:179
  47.4 13.0 %all-to-all-start = ((bf16[16,16,512]{2,1,0:T(8,128)(2,1)}), bf16[16,16,512]{2,1,0:T(8,128)(2,1)S(1)}, u32[]{:S(2)}, u32[]{:S(2)}) async-start(bf16[16,16,512]{2,1,0:T(8,128)(2,1)} %bitcast.5), calls=%async_computation | async-start | bytes 524288 | tf_op jit(solution)/shard_map/all_to_all | solution.py:623
  60.6 0.5 collective-permute-start.11
  61.2 0.4 collective-permute-start.24
  61.7 0.9 collective-permute-done.10.refs_6_
  62.6 0.8 copy-done.2
  63.6 0.8 copy-done.4
  64.4 0.4 collective-permute-start.5
  64.8 12.7 %all-to-all-done = bf16[16,16,512]{2,1,0:T(8,128)(2,1)S(1)} async-done(((bf16[16,16,512]{2,1,0:T(8,128)(2,1)}), bf16[16,16,512]{2,1,0:T(8,128)(2,1)S(1)}, u32[]{:S(2)}, u32[]{:S(2)}) %all-to-all-start) | async-done | bytes 262176 | tf_op jit(solution)/shard_map/all_to_all | solution.py:623
  77.4 1.0 copy-done.1
  78.5 1.0 copy-done.3
  79.5 1.0 copy-done.5
  80.5 2.7 %attend_part.2.refs_4_ = f32[128,3584]{1,0:T(8,128)S(1)} custom-call(s32[6]{0:T(128)S(1)} %concatenate.3.where_ref, bf16[256,512]{1,0:T(8,128)(2,1)S(1)} %bitcast.16, bf16[32,7680]{1,0:T(8,128)(2,1)S(1)} %collective-permute-done.refs_0_, bf16[32,7680]{1,0:T(8,128)(2,1)} %collective-permute-done.6.refs_1_, ...), custom_call_target="tpu_custom_call" | custom-call | flops 1409286144 | bytes 5505024 | tf_op jit(solution)/shard_map/attend_part/pallas_call | solution.py:294
  83.3 2.4 %attend_part.3 = (f32[32,3584]{1,0:T(8,128)S(1)}, bf16[32,3584]{1,0:T(8,128)(2,1)S(1)}, bf16[32,3584]{1,0:T(8,128)(2,1)S(1)}, bf16[32,1792]{1,0:T(8,128)(2,1)S(1)}, bf16[32,1792]{1,0:T(8,128)(2,1)S(1)}) custom-call(s32[6]{0:T(128)S(1)} %concatenate.3.where_ref, bf16[256,512]{1,0:T(8,128)(2,1)S(1)} %bitcast.17, ...), custom_call_target="tpu_custom_call" | custom-call | flops 469762048 | bytes 1835008 | tf_op jit(solution)/shard_map/attend_part/pallas_call | solution.py:294
  85.7 2.6 %collective-permute-start.16 = (bf16[32,1792]{1,0:T(8,128)(2,1)S(1)}, bf16[32,1792]{1,0:T(8,128)(2,1)S(1)}, u32[]{:S(2)}, u32[]{:S(2)}) collective-permute-start(bf16[32,1792]{1,0:T(8,128)(2,1)S(1)} %get-tuple-element.47), channel_id=1, source_target_pairs={{0,4},{2,6},{4,8},{6,10},{8,12},{10,14},{12,16},{14,18},{16,20},{1... | collective-permute-start | bytes 344072 | tf_op jit(solution)/shard_map/ppermute | solution.py:57
  88.2 1.7 collective-permute-start.17
  89.9 4.9 %collective-permute-done.16.refs_3_ = bf16[32,1792]{1,0:T(8,128)(2,1)S(1)} collective-permute-done((bf16[32,1792]{1,0:T(8,128)(2,1)S(1)}, bf16[32,1792]{1,0:T(8,128)(2,1)S(1)}, u32[]{:S(2)}, u32[]{:S(2)}) %collective-permute-start.16) | collective-permute-done | bytes 114720 | tf_op jit(solution)/shard_map/ppermute | solution.py:57
  94.8 1.8 collective-permute-start.14
  96.6 2.7 %collective-permute-start.15 = (bf16[32,3584]{1,0:T(8,128)(2,1)S(1)}, bf16[32,3584]{1,0:T(8,128)(2,1)S(1)}, u32[]{:S(2)}, u32[]{:S(2)}) collective-permute-start(bf16[32,3584]{1,0:T(8,128)(2,1)S(1)} %get-tuple-element.46), channel_id=1, source_target_pairs={{0,30},{2,0},{4,2},{6,4},{8,6},{10,8},{12,10},{14,12},{16,14},{18,... | collective-permute-start | bytes 688136 | tf_op jit(solution)/shard_map/ppermute | solution.py:57
  99.3 2.8 %collective-permute-done.14.refs_1_ = bf16[32,3584]{1,0:T(8,128)(2,1)S(1)} collective-permute-done((bf16[32,3584]{1,0:T(8,128)(2,1)S(1)}, bf16[32,3584]{1,0:T(8,128)(2,1)S(1)}, u32[]{:S(2)}, u32[]{:S(2)}) %collective-permute-start.14) | collective-permute-done | bytes 229408 | tf_op jit(solution)/shard_map/ppermute | solution.py:57
  102.0 0.8 collective-permute-done.15.refs_2_
  102.9 4.9 %collective-permute-start.18 = (bf16[8,3584]{1,0:T(8,128)(2,1)S(1)}, bf16[8,3584]{1,0:T(8,128)(2,1)S(1)}, u32[]{:S(2)}, u32[]{:S(2)}) collective-permute-start(bf16[8,3584]{1,0:T(8,128)(2,1)S(1)} %get-tuple-element.50), channel_id=1, source_target_pairs={{0,8},{8,0},{16,24},{24,16},{1,9},{9,1},{17,25},{25,17},{2,10},{10... | collective-permute-start | bytes 172040 | tf_op jit(solution)/shard_map/ppermute | solution.py:61
  107.8 4.9 %collective-permute-start.19 = (bf16[8,3584]{1,0:T(8,128)(2,1)S(1)}, bf16[8,3584]{1,0:T(8,128)(2,1)S(1)}, u32[]{:S(2)}, u32[]{:S(2)}) collective-permute-start(bf16[8,3584]{1,0:T(8,128)(2,1)S(1)} %get-tuple-element.51), channel_id=1, source_target_pairs={{0,16},{8,24},{16,0},{24,8},{1,17},{9,25},{17,1},{25,9},{2,18},{10... | collective-permute-start | bytes 172040 | tf_op jit(solution)/shard_map/ppermute | solution.py:61
  112.7 1.4 collective-permute-done.18.one
  114.1 1.6 collective-permute-start.20
  115.9 4.9 %collective-permute-done.19.two = bf16[8,3584]{1,0:T(8,128)(2,1)S(1)} collective-permute-done((bf16[8,3584]{1,0:T(8,128)(2,1)S(1)}, bf16[8,3584]{1,0:T(8,128)(2,1)S(1)}, u32[]{:S(2)}, u32[]{:S(2)}) %collective-permute-start.19) | collective-permute-done | bytes 57376 | tf_op jit(solution)/shard_map/ppermute | solution.py:61
  120.8 1.5 collective-permute-done.20.three
  122.3 0.6 route.1
  122.9 35.0 %all_gather.3.tokens = bf16[128,3712]{1,0:T(8,128)(2,1)S(1)} all-gather(bf16[8,3712]{1,0:T(8,128)(2,1)S(1)} %get-tuple-element.54), channel_id=1, replica_groups=mesh['rep'=2,'x'=4,'zb'=4,'j'=4,'c'=2] {'zb','j'}, dimensions={0}, use_global_device_ids=true | all-gather | bytes 1009664 | tf_op jit(solution)/shard_map/all_gather | solution.py:650
  157.9 1.4 dispatch.1
  159.2 2.2 collective-permute-start.21
  161.4 3.0 %collective-permute-start.22 = (bf16[32,7296]{1,0:T(8,128)(2,1)S(1)}, bf16[32,7296]{1,0:T(8,128)(2,1)S(1)}, u32[]{:S(2)}, u32[]{:S(2)}) collective-permute-start(bf16[32,7296]{1,0:T(8,128)(2,1)S(1)} %get-tuple-element.58), channel_id=1, source_target_pairs={{0,96},{32,64},{64,32},{96,0},{1,97},{33,65},{65,33},{97,1},{2,98}... | collective-permute-start | bytes 1400840 | tf_op jit(solution)/shard_map/ppermute | solution.py:39
  164.4 4.3 %stage.1 = (bf16[7168,512]{1,0:T(8,128)(2,1)S(1)}, bf16[256,7168]{1,0:T(8,128)(2,1)S(1)}) custom-call(bf16[7168,128]{1,0:T(8,128)(2,1)} %gate_a.1, bf16[7168,128]{1,0:T(8,128)(2,1)} %collective-permute-done.23.gate_b, bf16[7168,128]{1,0:T(8,128)(2,1)} %up_a.1, bf16[7168,128]{1,0:T(8,128)(2,1)} %collective-permute-done.24.up_b, bf16[128,7168]{1,0:T(8,128)(2,1)} %down_a.1, ...), custom_call_target="tpu_custom_call" | custom-call | flops 3670016000 | bytes 11010048 | tf_op jit(solution)/shard_map/stage/pallas_call | solution.py:388
  168.7 3.3 %collective-permute-done.21.refs_1_ = bf16[32,7296]{1,0:T(8,128)(2,1)S(1)} collective-permute-done((bf16[32,7296]{1,0:T(8,128)(2,1)S(1)}, bf16[32,7296]{1,0:T(8,128)(2,1)S(1)}, u32[]{:S(2)}, u32[]{:S(2)}) %collective-permute-start.21) | collective-permute-done | bytes 466976 | tf_op jit(solution)/shard_map/ppermute | solution.py:39
  172.0 12.3 %collective-permute-done.22.refs_2_ = bf16[32,7296]{1,0:T(8,128)(2,1)S(1)} collective-permute-done((bf16[32,7296]{1,0:T(8,128)(2,1)S(1)}, bf16[32,7296]{1,0:T(8,128)(2,1)S(1)}, u32[]{:S(2)}, u32[]{:S(2)}) %collective-permute-start.22) | collective-permute-done | bytes 466976 | tf_op jit(solution)/shard_map/ppermute | solution.py:39
  184.3 2.5 %expert_part.2 = (bf16[24,7168]{1,0:T(8,128)(2,1)S(1)}, bf16[24,7168]{1,0:T(8,128)(2,1)S(1)}, bf16[24,7168]{1,0:T(8,128)(2,1)S(1)}, bf16[8,7168]{1,0:T(8,128)(2,...) custom-call(s32[6]{0:T(128)S(1)} %concatenate.3.where_ref, ...), custom_call_target="tpu_custom_call" | custom-call | flops 2113929216 | bytes 1376256 | tf_op jit(solution)/shard_map/expert_part/pallas_call | solution.py:437
  187.1 3.1 %collective-permute-start.31 = (bf16[24,7168]{1,0:T(8,128)(2,1)S(1)}, bf16[24,7168]{1,0:T(8,128)(2,1)S(1)}, u32[]{:S(2)}, u32[]{:S(2)}) collective-permute-start(bf16[24,7168]{1,0:T(8,128)(2,1)S(1)} %get-tuple-element.69), channel_id=1, source_target_pairs={{0,96},{32,64},{64,32},{96,0},{1,97},{33,65},{65,33},{97,1},{2,98}... | collective-permute-start | bytes 1032200 | tf_op jit(solution)/shard_map/ppermute | solution.py:39
  190.1 2.6 %expert_part.3 = (bf16[24,7168]{1,0:T(8,128)(2,1)S(1)}, bf16[8,7168]{1,0:T(8,128)(2,1)S(1)}) custom-call(s32[6]{0:T(128)S(1)} %concatenate.3.where_ref, bf16[32,7296]{1,0:T(8,128)(2,1)S(1)} %collective-permute-done.28.refs_0_, bf16[7168,512]{1,0:T(8,128)(2,1)S(1)} %get-tuple-element.59.refs_3_.refs_1_, bf16[256,7168]{1,0:T(8,128)(2,1)S(1)} %get-tuple-element.60.refs_4_.refs_2_), custom_call_target="tpu_custom_call" | custom-call | flops 704643072 | bytes 458752 | tf_op jit(solution)/shard_map/expert_part/pallas_call | solution.py:437
  192.8 1.0 collective-permute-start.32
  193.8 1.1 collective-permute-start.26
  194.9 2.0 collective-permute-start.27
  197.0 4.8 %collective-permute-done.32.refs_3_ = bf16[24,7168]{1,0:T(8,128)(2,1)S(1)} collective-permute-done((bf16[24,7168]{1,0:T(8,128)(2,1)S(1)}, bf16[24,7168]{1,0:T(8,128)(2,1)S(1)}, u32[]{:S(2)}, u32[]{:S(2)}) %collective-permute-start.32) | collective-permute-done | bytes 344096 | tf_op jit(solution)/shard_map/ppermute | solution.py:39
  202.2 3.2 %collective-permute-start.34 = (bf16[32,3584]{1,0:T(8,128)(2,1)S(1)}, bf16[32,3584]{1,0:T(8,128)(2,1)S(1)}, u32[]{:S(2)}, u32[]{:S(2)}) collective-permute-start(bf16[32,3584]{1,0:T(8,128)(2,1)S(1)} %get-tuple-element.72), channel_id=1, source_target_pairs={{0,30},{2,0},{4,2},{6,4},{8,6},{10,8},{12,10},{14,12},{16,14},{18,... | collective-permute-start | bytes 688136 | tf_op jit(solution)/shard_map/ppermute | solution.py:57
  205.4 1.1 collective-permute-start.29
  206.6 4.1 %collective-permute-start.36 = (bf16[32,1792]{1,0:T(8,128)(2,1)S(1)}, bf16[32,1792]{1,0:T(8,128)(2,1)S(1)}, u32[]{:S(2)}, u32[]{:S(2)}) collective-permute-start(bf16[32,1792]{1,0:T(8,128)(2,1)S(1)} %get-tuple-element.74), channel_id=1, source_target_pairs={{0,28},{2,30},{4,0},{6,2},{8,4},{10,6},{12,8},{14,10},{16,12},{18,... | collective-permute-start | bytes 344072 | tf_op jit(solution)/shard_map/ppermute | solution.py:57
  210.7 1.0 collective-permute-done.29.refs_4_
  211.7 1.9 collective-permute-done.35.refs_7_
  213.6 0.5 collective-permute-done.36.refs_8_
  214.1 0.7 collective-permute-done.33.refs_5_
  215.1 2.8 %collective-permute-start.37 = (bf16[8,3584]{1,0:T(8,128)(2,1)S(1)}, bf16[8,3584]{1,0:T(8,128)(2,1)S(1)}, u32[]{:S(2)}, u32[]{:S(2)}) collective-permute-start(bf16[8,3584]{1,0:T(8,128)(2,1)S(1)} %get-tuple-element.76), channel_id=1, source_target_pairs={{0,8},{8,0},{16,24},{24,16},{1,9},{9,1},{17,25},{25,17},{2,10},{10... | collective-permute-start | bytes 172040 | tf_op jit(solution)/shard_map/ppermute | solution.py:61
  217.8 5.3 %collective-permute-start.38 = (bf16[8,3584]{1,0:T(8,128)(2,1)S(1)}, bf16[8,3584]{1,0:T(8,128)(2,1)S(1)}, u32[]{:S(2)}, u32[]{:S(2)}) collective-permute-start(bf16[8,3584]{1,0:T(8,128)(2,1)S(1)} %get-tuple-element.77), channel_id=1, source_target_pairs={{0,16},{8,24},{16,0},{24,8},{1,17},{9,25},{17,1},{25,9},{2,18},{10... | collective-permute-start | bytes 172040 | tf_op jit(solution)/shard_map/ppermute | solution.py:61
  223.1 3.3 %collective-permute-start.39 = (bf16[8,3584]{1,0:T(8,128)(2,1)S(1)}, bf16[8,3584]{1,0:T(8,128)(2,1)S(1)}, u32[]{:S(2)}, u32[]{:S(2)}) collective-permute-start(bf16[8,3584]{1,0:T(8,128)(2,1)S(1)} %get-tuple-element.78), channel_id=1, source_target_pairs={{0,24},{8,16},{16,8},{24,0},{1,25},{9,17},{17,9},{25,1},{2,26},{10... | collective-permute-start | bytes 172040 | tf_op jit(solution)/shard_map/ppermute | solution.py:61
  226.5 4.3 %collective-permute-done.38.two = bf16[8,3584]{1,0:T(8,128)(2,1)S(1)} collective-permute-done((bf16[8,3584]{1,0:T(8,128)(2,1)S(1)}, bf16[8,3584]{1,0:T(8,128)(2,1)S(1)}, u32[]{:S(2)}, u32[]{:S(2)}) %collective-permute-start.38) | collective-permute-done | bytes 57376 | tf_op jit(solution)/shard_map/ppermute | solution.py:61
  230.8 1.3 collective-permute-done.39.three
  232.1 0.7 finish.1
  (63 shorter events, 2.0 us)
Async XLA Ops:
  1.2 26.3 %collective-permute-start = (bf16[32,7680]{1,0:T(8,128)(2,1)S(1)}, bf16[32,7680]{1,0:T(8,128)(2,1)S(1)}, u32[]{:S(2)}, u32[]{:S(2)}) collective-permute-start(bf16[32,7680]{1,0:T(8,128)(2,1)S(1)} %get-tuple-element.42.refs_8_), channel_id=1, source_target_pairs={{0,32},{32,0},{64,96},{96,64},{128,224},{160,192},{192,160},{224,1... | collective-permute-start | bytes 1474568 | tf_op jit(solution)/shard_map/ppermute | solution.py:45
  20.7 13.9 %collective-permute-start.3 = (bf16[32,7680]{1,0:T(8,128)(2,1)S(1)}, bf16[32,7680]{1,0:T(8,128)(2,1)S(1)}, u32[]{:S(2)}, u32[]{:S(2)}) collective-permute-start(bf16[32,7680]{1,0:T(8,128)(2,1)S(1)} %get-tuple-element.43.refs_9_), channel_id=1, source_target_pairs={{0,96},{32,64},{64,32},{96,0},{128,160},{160,128},{192,224},{224,1... | collective-permute-start | bytes 1474568 | tf_op jit(solution)/shard_map/ppermute | solution.py:45
  20.7 15.3 %collective-permute-start.12 = (bf16[32,7680]{1,0:T(8,128)(2,1)S(1)}, bf16[32,7680]{1,0:T(8,128)(2,1)S(1)}, u32[]{:S(2)}, u32[]{:S(2)}) collective-permute-start(bf16[32,7680]{1,0:T(8,128)(2,1)S(1)} %get-tuple-element.42.refs_8_), channel_id=1, source_target_pairs={{0,1},{1,0},{2,3},{3,2},{4,5},{5,4},{6,7},{7,6},{8,9},{9,8},{10,11... | collective-permute-start | bytes 1474568 | tf_op jit(solution)/shard_map/ppermute | solution.py:65
  20.7 15.3 %collective-permute-start.13 = (bf16[32,7680]{1,0:T(8,128)(2,1)S(1)}, bf16[32,7680]{1,0:T(8,128)(2,1)S(1)}, u32[]{:S(2)}, u32[]{:S(2)}) collective-permute-start(bf16[32,7680]{1,0:T(8,128)(2,1)S(1)} %get-tuple-element.43.refs_9_), channel_id=1, source_target_pairs={{0,1},{1,0},{2,3},{3,2},{4,5},{5,4},{6,7},{7,6},{8,9},{9,8},{10,11... | collective-permute-start | bytes 1474568 | tf_op jit(solution)/shard_map/ppermute | solution.py:65
  27.5 12.4 %collective-permute-start.8 = (bf16[32,7680]{1,0:T(8,128)(2,1)S(1)}, bf16[32,7680]{1,0:T(8,128)(2,1)S(1)}, u32[]{:S(2)}, u32[]{:S(2)}) collective-permute-start(bf16[32,7680]{1,0:T(8,128)(2,1)S(1)} %collective-permute-done.refs_0_), channel_id=1, source_target_pairs={{0,96},{32,64},{64,32},{96,0},{128,160},{160,128},{192,224},{224,1... | collective-permute-start | bytes 1474568 | tf_op jit(solution)/shard_map/ppermute | solution.py:45
  27.6 32.9 %collective-permute-start.6 = (bf16[32,7680]{1,0:T(8,128)(2,1)S(1)}, bf16[32,7680]{1,0:T(8,128)(2,1)}, u32[]{:S(2)}, u32[]{:S(2)}) collective-permute-start(bf16[32,7680]{1,0:T(8,128)(2,1)S(1)} %collective-permute-done.refs_0_), channel_id=1, source_target_pairs={{0,1},{1,0},{2,3},{3,2},{4,5},{5,4},{6,7},{7,6},{8,9},{9,8},{10,11... | collective-permute-start | bytes 1474568 | tf_op jit(solution)/shard_map/ppermute | solution.py:65
  34.7 25.9 %collective-permute-start.9 = (bf16[32,7680]{1,0:T(8,128)(2,1)S(1)}, bf16[32,7680]{1,0:T(8,128)(2,1)}, u32[]{:S(2)}, u32[]{:S(2)}) collective-permute-start(bf16[32,7680]{1,0:T(8,128)(2,1)S(1)} %collective-permute-done.3.refs_2_), channel_id=1, source_target_pairs={{0,32},{32,0},{64,96},{96,64},{128,224},{160,192},{192,160},{224,1... | collective-permute-start | bytes 1474568 | tf_op jit(solution)/shard_map/ppermute | solution.py:45
  36.0 25.0 %collective-permute-start.1 = (bf16[32,7680]{1,0:T(8,128)(2,1)S(1)}, bf16[32,7680]{1,0:T(8,128)(2,1)}, u32[]{:S(2)}, u32[]{:S(2)}) collective-permute-start(bf16[32,7680]{1,0:T(8,128)(2,1)S(1)} %collective-permute-done.refs_0_), channel_id=1, source_target_pairs={{0,128},{128,0},{1,129},{129,1},{2,130},{130,2},{3,131},{131,3},{4... | collective-permute-start | bytes 1474568 | tf_op jit(solution)/shard_map/ppermute | solution.py:53
  36.0 25.2 %collective-permute-start.7 = (bf16[32,7680]{1,0:T(8,128)(2,1)S(1)}, bf16[32,7680]{1,0:T(8,128)(2,1)}, u32[]{:S(2)}, u32[]{:S(2)}) collective-permute-start(bf16[32,7680]{1,0:T(8,128)(2,1)S(1)} %collective-permute-done.3.refs_2_), channel_id=1, source_target_pairs={{0,1},{1,0},{2,3},{3,2},{4,5},{5,4},{6,7},{7,6},{8,9},{9,8},{10,11... | collective-permute-start | bytes 1474568 | tf_op jit(solution)/shard_map/ppermute | solution.py:65
  39.9 0.8 copy-start
  40.8 20.8 %collective-permute-start.4 = (bf16[32,7680]{1,0:T(8,128)(2,1)S(1)}, bf16[32,7680]{1,0:T(8,128)(2,1)}, u32[]{:S(2)}, u32[]{:S(2)}) collective-permute-start(bf16[32,7680]{1,0:T(8,128)(2,1)S(1)} %collective-permute-done.3.refs_2_), channel_id=1, source_target_pairs={{0,128},{128,0},{1,129},{129,1},{2,130},{130,2},{3,131},{131,3},{4... | collective-permute-start | bytes 1474568 | tf_op jit(solution)/shard_map/ppermute | solution.py:53
  47.4 30.0 %all-to-all-start = ((bf16[16,16,512]{2,1,0:T(8,128)(2,1)}), bf16[16,16,512]{2,1,0:T(8,128)(2,1)S(1)}, u32[]{:S(2)}, u32[]{:S(2)}) async-start(bf16[16,16,512]{2,1,0:T(8,128)(2,1)} %bitcast.5), calls=%async_computation | async-start | bytes 524288 | tf_op jit(solution)/shard_map/all_to_all | solution.py:623
  60.4 2.2 collective-permute-start.10
  60.6 3.0 %collective-permute-start.11 = (bf16[32,7680]{1,0:T(8,128)(2,1)}, bf16[32,7680]{1,0:T(8,128)(2,1)S(1)}, u32[]{:S(2)}, u32[]{:S(2)}) collective-permute-start(bf16[32,7680]{1,0:T(8,128)(2,1)} %collective-permute-done.9.refs_5_), channel_id=1, source_target_pairs={{0,1},{1,0},{2,3},{3,2},{4,5},{5,4},{6,7},{7,6},{8,9},{9,8},{10,11... | collective-permute-start | bytes 1474568 | tf_op jit(solution)/shard_map/ppermute | solution.py:65
  61.1 103.3 %collective-permute-start.23 = (bf16[7168,128]{1,0:T(8,128)(2,1)}, bf16[7168,128]{1,0:T(8,128)(2,1)}, u32[]{:S(2)}, u32[]{:S(2)}) collective-permute-start(bf16[7168,128]{1,0:T(8,128)(2,1)} %gate_a.1), channel_id=1, source_target_pairs={{0,1},{1,0},{2,3},{3,2},{4,5},{5,4},{6,7},{7,6},{8,9},{9,8},{10,11... | collective-permute-start | bytes 5505032 | tf_op jit(solution)/shard_map/ppermute | solution.py:65
  61.2 103.2 %collective-permute-start.24 = (bf16[7168,128]{1,0:T(8,128)(2,1)}, bf16[7168,128]{1,0:T(8,128)(2,1)}, u32[]{:S(2)}, u32[]{:S(2)}) collective-permute-start(bf16[7168,128]{1,0:T(8,128)(2,1)} %up_a.1), channel_id=1, source_target_pairs={{0,1},{1,0},{2,3},{3,2},{4,5},{5,4},{6,7},{7,6},{8,9},{9,8},{10,11... | collective-permute-start | bytes 5505032 | tf_op jit(solution)/shard_map/ppermute | solution.py:65
  61.6 102.8 %collective-permute-start.25 = (bf16[128,7168]{1,0:T(8,128)(2,1)}, bf16[128,7168]{1,0:T(8,128)(2,1)}, u32[]{:S(2)}, u32[]{:S(2)}) collective-permute-start(bf16[128,7168]{1,0:T(8,128)(2,1)} %down_a.1), channel_id=1, source_target_pairs={{0,1},{1,0},{2,3},{3,2},{4,5},{5,4},{6,7},{7,6},{8,9},{9,8},{10,11... | collective-permute-start | bytes 5505032 | tf_op jit(solution)/shard_map/ppermute | solution.py:65
  62.6 0.8 copy-start.2
  63.4 19.8 %collective-permute-start.2 = (bf16[32,7680]{1,0:T(8,128)(2,1)}, bf16[32,7680]{1,0:T(8,128)(2,1)}, u32[]{:S(2)}, u32[]{:S(2)}) collective-permute-start(bf16[32,7680]{1,0:T(8,128)(2,1)} %collective-permute-done.1.refs_0_), channel_id=1, source_target_pairs={{0,1},{1,0},{2,3},{3,2},{4,5},{5,4},{6,7},{7,6},{8,9},{9,8},{10,11... | collective-permute-start | bytes 1474568 | tf_op jit(solution)/shard_map/ppermute | solution.py:65
  63.6 0.8 copy-start.4
  64.4 18.9 %collective-permute-start.5 = (bf16[32,7680]{1,0:T(8,128)(2,1)}, bf16[32,7680]{1,0:T(8,128)(2,1)}, u32[]{:S(2)}, u32[]{:S(2)}) collective-permute-start(bf16[32,7680]{1,0:T(8,128)(2,1)} %collective-permute-done.4.refs_2_), channel_id=1, source_target_pairs={{0,1},{1,0},{2,3},{3,2},{4,5},{5,4},{6,7},{7,6},{8,9},{9,8},{10,11... | collective-permute-start | bytes 1474568 | tf_op jit(solution)/shard_map/ppermute | solution.py:65
  77.4 1.0 copy-start.1
  78.5 1.0 copy-start.3
  79.5 1.0 copy-start.5
  83.2 32.5 %copy-start.8 = (bf16[7168]{0:T(1024)(128)(2,1)S(1)}, bf16[7168]{0:T(1024)(128)(2,1)}, u32[]{:S(2)}) copy-start(bf16[7168]{0:T(1024)(128)(2,1)} %param.21) | copy-start | bytes 43012
  83.2 32.5 %copy-start.7 = (bf16[2,2,7168]{2,1,0:T(2,128)(2,1)S(1)}, bf16[2,2,7168]{2,1,0:T(2,128)(2,1)}, u32[]{:S(2)}) copy-start(bf16[2,2,7168]{2,1,0:T(2,128)(2,1)} %param.18) | copy-start | bytes 172036
  85.6 36.6 %copy-start.9 = (s32[2,2,8]{2,1,0:T(2,128)S(1)}, s32[2,2,8]{2,1,0:T(2,128)}, u32[]{:S(2)}) copy-start(s32[2,2,8]{2,1,0:T(2,128)} %param.23) | copy-start | bytes 388
  85.7 36.6 %copy-start.10 = (s32[2,2,8]{2,1,0:T(2,128)S(1)}, s32[2,2,8]{2,1,0:T(2,128)}, u32[]{:S(2)}) copy-start(s32[2,2,8]{2,1,0:T(2,128)} %param.24) | copy-start | bytes 388
  85.7 36.6 %copy-start.6 = (bf16[7168,16]{0,1:T(8,128)(2,1)S(1)}, bf16[7168,16]{0,1:T(8,128)(2,1)}, u32[]{:S(2)}) copy-start(bf16[7168,16]{0,1:T(8,128)(2,1)} %param.22) | copy-start | bytes 688132
  85.7 9.1 %collective-permute-start.16 = (bf16[32,1792]{1,0:T(8,128)(2,1)S(1)}, bf16[32,1792]{1,0:T(8,128)(2,1)S(1)}, u32[]{:S(2)}, u32[]{:S(2)}) collective-permute-start(bf16[32,1792]{1,0:T(8,128)(2,1)S(1)} %get-tuple-element.47), channel_id=1, source_target_pairs={{0,4},{2,6},{4,8},{6,10},{8,12},{10,14},{12,16},{14,18},{16,20},{1... | collective-permute-start | bytes 344072 | tf_op jit(solution)/shard_map/ppermute | solution.py:57
  88.2 8.4 %collective-permute-start.17 = (bf16[32,1792]{1,0:T(8,128)(2,1)S(1)}, bf16[32,1792]{1,0:T(8,128)(2,1)S(1)}, u32[]{:S(2)}, u32[]{:S(2)}) collective-permute-start(bf16[32,1792]{1,0:T(8,128)(2,1)S(1)} %get-tuple-element.48), channel_id=1, source_target_pairs={{0,28},{2,30},{4,0},{6,2},{8,4},{10,6},{12,8},{14,10},{16,12},{18,... | collective-permute-start | bytes 344072 | tf_op jit(solution)/shard_map/ppermute | solution.py:57
  94.8 7.2 %collective-permute-start.14 = (bf16[32,3584]{1,0:T(8,128)(2,1)S(1)}, bf16[32,3584]{1,0:T(8,128)(2,1)S(1)}, u32[]{:S(2)}, u32[]{:S(2)}) collective-permute-start(bf16[32,3584]{1,0:T(8,128)(2,1)S(1)} %get-tuple-element.45), channel_id=1, source_target_pairs={{0,2},{2,4},{4,6},{6,8},{8,10},{10,12},{12,14},{14,16},{16,18},{18... | collective-permute-start | bytes 688136 | tf_op jit(solution)/shard_map/ppermute | solution.py:57
  96.6 6.2 %collective-permute-start.15 = (bf16[32,3584]{1,0:T(8,128)(2,1)S(1)}, bf16[32,3584]{1,0:T(8,128)(2,1)S(1)}, u32[]{:S(2)}, u32[]{:S(2)}) collective-permute-start(bf16[32,3584]{1,0:T(8,128)(2,1)S(1)} %get-tuple-element.46), channel_id=1, source_target_pairs={{0,30},{2,0},{4,2},{6,4},{8,6},{10,8},{12,10},{14,12},{16,14},{18,... | collective-permute-start | bytes 688136 | tf_op jit(solution)/shard_map/ppermute | solution.py:57
  102.9 11.2 %collective-permute-start.18 = (bf16[8,3584]{1,0:T(8,128)(2,1)S(1)}, bf16[8,3584]{1,0:T(8,128)(2,1)S(1)}, u32[]{:S(2)}, u32[]{:S(2)}) collective-permute-start(bf16[8,3584]{1,0:T(8,128)(2,1)S(1)} %get-tuple-element.50), channel_id=1, source_target_pairs={{0,8},{8,0},{16,24},{24,16},{1,9},{9,1},{17,25},{25,17},{2,10},{10... | collective-permute-start | bytes 172040 | tf_op jit(solution)/shard_map/ppermute | solution.py:61
  107.8 12.9 %collective-permute-start.19 = (bf16[8,3584]{1,0:T(8,128)(2,1)S(1)}, bf16[8,3584]{1,0:T(8,128)(2,1)S(1)}, u32[]{:S(2)}, u32[]{:S(2)}) collective-permute-start(bf16[8,3584]{1,0:T(8,128)(2,1)S(1)} %get-tuple-element.51), channel_id=1, source_target_pairs={{0,16},{8,24},{16,0},{24,8},{1,17},{9,25},{17,1},{25,9},{2,18},{10... | collective-permute-start | bytes 172040 | tf_op jit(solution)/shard_map/ppermute | solution.py:61
  114.1 8.1 %collective-permute-start.20 = (bf16[8,3584]{1,0:T(8,128)(2,1)S(1)}, bf16[8,3584]{1,0:T(8,128)(2,1)S(1)}, u32[]{:S(2)}, u32[]{:S(2)}) collective-permute-start(bf16[8,3584]{1,0:T(8,128)(2,1)S(1)} %get-tuple-element.52), channel_id=1, source_target_pairs={{0,24},{8,16},{16,8},{24,0},{1,25},{9,17},{17,9},{25,1},{2,26},{10... | collective-permute-start | bytes 172040 | tf_op jit(solution)/shard_map/ppermute | solution.py:61
  159.2 12.8 %collective-permute-start.21 = (bf16[32,7296]{1,0:T(8,128)(2,1)S(1)}, bf16[32,7296]{1,0:T(8,128)(2,1)S(1)}, u32[]{:S(2)}, u32[]{:S(2)}) collective-permute-start(bf16[32,7296]{1,0:T(8,128)(2,1)S(1)} %get-tuple-element.57), channel_id=1, source_target_pairs={{0,32},{32,0},{64,96},{96,64},{1,33},{33,1},{65,97},{97,65},{2,34}... | collective-permute-start | bytes 1400840 | tf_op jit(solution)/shard_map/ppermute | solution.py:39
  161.4 22.9 %collective-permute-start.22 = (bf16[32,7296]{1,0:T(8,128)(2,1)S(1)}, bf16[32,7296]{1,0:T(8,128)(2,1)S(1)}, u32[]{:S(2)}, u32[]{:S(2)}) collective-permute-start(bf16[32,7296]{1,0:T(8,128)(2,1)S(1)} %get-tuple-element.58), channel_id=1, source_target_pairs={{0,96},{32,64},{64,32},{96,0},{1,97},{33,65},{65,33},{97,1},{2,98}... | collective-permute-start | bytes 1400840 | tf_op jit(solution)/shard_map/ppermute | solution.py:39
  164.4 25.7 %collective-permute-start.28 = (bf16[32,7296]{1,0:T(8,128)(2,1)S(1)}, bf16[32,7296]{1,0:T(8,128)(2,1)S(1)}, u32[]{:S(2)}, u32[]{:S(2)}) collective-permute-start(bf16[32,7296]{1,0:T(8,128)(2,1)S(1)} %get-tuple-element.64), channel_id=1, source_target_pairs={{0,64},{32,96},{64,0},{96,32},{1,65},{33,97},{65,1},{97,33},{2,66}... | collective-permute-start | bytes 1400840 | tf_op jit(solution)/shard_map/ppermute | solution.py:39
  186.9 10.1 %collective-permute-start.30 = (bf16[24,7168]{1,0:T(8,128)(2,1)S(1)}, bf16[24,7168]{1,0:T(8,128)(2,1)S(1)}, u32[]{:S(2)}, u32[]{:S(2)}) collective-permute-start(bf16[24,7168]{1,0:T(8,128)(2,1)S(1)} %get-tuple-element.68), channel_id=1, source_target_pairs={{0,32},{32,0},{64,96},{96,64},{1,33},{33,1},{65,97},{97,65},{2,34}... | collective-permute-start | bytes 1032200 | tf_op jit(solution)/shard_map/ppermute | solution.py:39
  187.1 9.9 %collective-permute-start.31 = (bf16[24,7168]{1,0:T(8,128)(2,1)S(1)}, bf16[24,7168]{1,0:T(8,128)(2,1)S(1)}, u32[]{:S(2)}, u32[]{:S(2)}) collective-permute-start(bf16[24,7168]{1,0:T(8,128)(2,1)S(1)} %get-tuple-element.69), channel_id=1, source_target_pairs={{0,96},{32,64},{64,32},{96,0},{1,97},{33,65},{65,33},{97,1},{2,98}... | collective-permute-start | bytes 1032200 | tf_op jit(solution)/shard_map/ppermute | solution.py:39
  192.8 9.0 %collective-permute-start.32 = (bf16[24,7168]{1,0:T(8,128)(2,1)S(1)}, bf16[24,7168]{1,0:T(8,128)(2,1)S(1)}, u32[]{:S(2)}, u32[]{:S(2)}) collective-permute-start(bf16[24,7168]{1,0:T(8,128)(2,1)S(1)} %get-tuple-element.70), channel_id=1, source_target_pairs={{0,64},{32,96},{64,0},{96,32},{1,65},{33,97},{65,1},{97,33},{2,66}... | collective-permute-start | bytes 1032200 | tf_op jit(solution)/shard_map/ppermute | solution.py:39
  193.8 12.8 %collective-permute-start.26 = (bf16[8,7168]{1,0:T(8,128)(2,1)S(1)}, bf16[8,7168]{1,0:T(8,128)(2,1)S(1)}, u32[]{:S(2)}, u32[]{:S(2)}) collective-permute-start(bf16[8,7168]{1,0:T(8,128)(2,1)S(1)} %get-tuple-element.62), channel_id=1, source_target_pairs={{0,32},{32,0},{64,96},{96,64},{1,33},{33,1},{65,97},{97,65},{2,34}... | collective-permute-start | bytes 344072 | tf_op jit(solution)/shard_map/ppermute | solution.py:39
  194.9 11.6 %collective-permute-start.27 = (bf16[8,7168]{1,0:T(8,128)(2,1)S(1)}, bf16[8,7168]{1,0:T(8,128)(2,1)S(1)}, u32[]{:S(2)}, u32[]{:S(2)}) collective-permute-start(bf16[8,7168]{1,0:T(8,128)(2,1)S(1)} %get-tuple-element.63), channel_id=1, source_target_pairs={{0,96},{32,64},{64,32},{96,0},{1,97},{33,65},{65,33},{97,1},{2,98}... | collective-permute-start | bytes 344072 | tf_op jit(solution)/shard_map/ppermute | solution.py:39
  202.1 12.7 %collective-permute-start.33 = (bf16[32,3584]{1,0:T(8,128)(2,1)S(1)}, bf16[32,3584]{1,0:T(8,128)(2,1)S(1)}, u32[]{:S(2)}, u32[]{:S(2)}) collective-permute-start(bf16[32,3584]{1,0:T(8,128)(2,1)S(1)} %get-tuple-element.71), channel_id=1, source_target_pairs={{0,2},{2,4},{4,6},{6,8},{8,10},{10,12},{12,14},{14,16},{16,18},{18... | collective-permute-start | bytes 688136 | tf_op jit(solution)/shard_map/ppermute | solution.py:57
  202.2 12.6 %collective-permute-start.34 = (bf16[32,3584]{1,0:T(8,128)(2,1)S(1)}, bf16[32,3584]{1,0:T(8,128)(2,1)S(1)}, u32[]{:S(2)}, u32[]{:S(2)}) collective-permute-start(bf16[32,3584]{1,0:T(8,128)(2,1)S(1)} %get-tuple-element.72), channel_id=1, source_target_pairs={{0,30},{2,0},{4,2},{6,4},{8,6},{10,8},{12,10},{14,12},{16,14},{18,... | collective-permute-start | bytes 688136 | tf_op jit(solution)/shard_map/ppermute | solution.py:57
  205.4 6.3 %collective-permute-start.29 = (bf16[8,7168]{1,0:T(8,128)(2,1)S(1)}, bf16[8,7168]{1,0:T(8,128)(2,1)S(1)}, u32[]{:S(2)}, u32[]{:S(2)}) collective-permute-start(bf16[8,7168]{1,0:T(8,128)(2,1)S(1)} %get-tuple-element.65), channel_id=1, source_target_pairs={{0,64},{32,96},{64,0},{96,32},{1,65},{33,97},{65,1},{97,33},{2,66}... | collective-permute-start | bytes 344072 | tf_op jit(solution)/shard_map/ppermute | solution.py:39
  206.6 7.1 %collective-permute-start.35 = (bf16[32,1792]{1,0:T(8,128)(2,1)S(1)}, bf16[32,1792]{1,0:T(8,128)(2,1)S(1)}, u32[]{:S(2)}, u32[]{:S(2)}) collective-permute-start(bf16[32,1792]{1,0:T(8,128)(2,1)S(1)} %get-tuple-element.73), channel_id=1, source_target_pairs={{0,4},{2,6},{4,8},{6,10},{8,12},{10,14},{12,16},{14,18},{16,20},{1... | collective-permute-start | bytes 344072 | tf_op jit(solution)/shard_map/ppermute | solution.py:57
  206.6 7.6 %collective-permute-start.36 = (bf16[32,1792]{1,0:T(8,128)(2,1)S(1)}, bf16[32,1792]{1,0:T(8,128)(2,1)S(1)}, u32[]{:S(2)}, u32[]{:S(2)}) collective-permute-start(bf16[32,1792]{1,0:T(8,128)(2,1)S(1)} %get-tuple-element.74), channel_id=1, source_target_pairs={{0,28},{2,30},{4,0},{6,2},{8,4},{10,6},{12,8},{14,10},{16,12},{18,... | collective-permute-start | bytes 344072 | tf_op jit(solution)/shard_map/ppermute | solution.py:57
  215.1 11.4 %collective-permute-start.37 = (bf16[8,3584]{1,0:T(8,128)(2,1)S(1)}, bf16[8,3584]{1,0:T(8,128)(2,1)S(1)}, u32[]{:S(2)}, u32[]{:S(2)}) collective-permute-start(bf16[8,3584]{1,0:T(8,128)(2,1)S(1)} %get-tuple-element.76), channel_id=1, source_target_pairs={{0,8},{8,0},{16,24},{24,16},{1,9},{9,1},{17,25},{25,17},{2,10},{10... | collective-permute-start | bytes 172040 | tf_op jit(solution)/shard_map/ppermute | solution.py:61
  217.8 12.9 %collective-permute-start.38 = (bf16[8,3584]{1,0:T(8,128)(2,1)S(1)}, bf16[8,3584]{1,0:T(8,128)(2,1)S(1)}, u32[]{:S(2)}, u32[]{:S(2)}) collective-permute-start(bf16[8,3584]{1,0:T(8,128)(2,1)S(1)} %get-tuple-element.77), channel_id=1, source_target_pairs={{0,16},{8,24},{16,0},{24,8},{1,17},{9,25},{17,1},{25,9},{2,18},{10... | collective-permute-start | bytes 172040 | tf_op jit(solution)/shard_map/ppermute | solution.py:61
  223.1 8.9 %collective-permute-start.39 = (bf16[8,3584]{1,0:T(8,128)(2,1)S(1)}, bf16[8,3584]{1,0:T(8,128)(2,1)S(1)}, u32[]{:S(2)}, u32[]{:S(2)}) collective-permute-start(bf16[8,3584]{1,0:T(8,128)(2,1)S(1)} %get-tuple-element.78), channel_id=1, source_target_pairs={{0,24},{8,16},{16,8},{24,0},{1,25},{9,17},{17,9},{25,1},{2,26},{10... | collective-permute-start | bytes 172040 | tf_op jit(solution)/shard_map/ppermute | solution.py:61
where the time goes:
time: 233 us
  starting transfers between devices  89.1 us (38%)
  waiting for transfers between devices  77 us (33%)
  blocking collectives  35 us (15%)
  Pallas kernels  24.9 us (11%)
  local copies, waits for them, and re-layouts  6.46 us (3%)
    all_gather x1, blocking collectives, layer(): ring = lax.all_gather(payload, ZAX, axis=0, tiled=True)  35 us
    ppermute x6, starting transfers between devices, swap_far(): return lax.ppermute(a, 'zb', [(i, i ^ bits) for i in range(FAR)])  22.8 us
    ppermute x9, waiting for transfers between devices, swap_x(): lax.ppermute(a, 'x', [(i, i ^ bits) for i in range(lax.axis_size('x'))])  21.4 us
    ppermute x4, starting transfers between devices, swap_x_by_group(): lax.ppermute(a, ('rep', 'x'), [(g * nx + i, g * nx + (i ^ b)) for g, b in...  20.9 us
    ppermute x4, waiting for transfers between devices, swap_x_by_group(): lax.ppermute(a, ('rep', 'x'), [(g * nx + i, g * nx + (i ^ b)) for g, b in...  17.2 us
    ppermute x8, starting transfers between devices, shift_z(): return lax.ppermute(a, ZAX, [(i, (i + step) % RING) for i in range(RING)])  16.2 us
    ppermute x9, starting transfers between devices, swap_x(): lax.ppermute(a, 'x', [(i, i ^ bits) for i in range(lax.axis_size('x'))])  13.8 us
    ppermute x6, waiting for transfers between devices, swap_far(): return lax.ppermute(a, 'zb', [(i, i ^ bits) for i in range(FAR)])  13.4 us
  transfers between devices with their start and end apart: 41, of which 20 were waited for; matrix products, arithmetic and copies ran while one was open for 0% of the time, Pallas kernels for 10%

commit v1 on v0

--- a/solution.py
+++ b/solution.py
@@ -12,6 +12,7 @@
 
 D = 7168
 LAT = 512
+VH = 128
 EXPERTS = 16
 TOP = 8
 CAP = 2
@@ -37,20 +38,6 @@
 
 def swap_x(a, bits):
     return lax.ppermute(a, "x", [(i, i ^ bits) for i in range(lax.axis_size("x"))])
-
-
-def swap_x_by_group(a, even, odd):
-    nx = lax.axis_size("x")
-    bits = [odd if g % 2 and paired() else even for g in range(lax.axis_size("rep"))]
-    return lax.ppermute(a, ("rep", "x"), [(g * nx + i, g * nx + (i ^ b)) for g, b in enumerate(bits) for i in range(nx)])
-
-
-def paired():
-    return lax.axis_size("rep") % 2 == 0
-
-
-def swap_group(a):
-    return lax.ppermute(a, "rep", [(i, i ^ 1) for i in range(lax.axis_size("rep"))])
 
 
 def shift_z(a, step):
@@ -252,19 +239,14 @@
     return jnp.concatenate(got, axis=0)
 
 
-def attend_kernel(tok, nx, count, hops, last, where_ref, arrived, *refs):
+def attend_kernel(tok, nx, count, first, last, where_ref, arrived, *refs):
     pieces, outs = refs[:count], refs[count:]
     if last:
         before, outs = outs[0], outs[1:]
     up = jnp.concatenate([piece[:, pl.ds(0, LAT)] for piece in pieces], axis=0)
     values = lax.dot_general(arrived[...], up, NT, preferred_element_type=f32)
     hop = lax.rem(iota(values.shape, 0) // tok, nx)
-    odd = where_ref[where_ref.shape[0] - 1]
-    part = iota(values.shape, 1) // (up.shape[0] // len(hops))
-    wanted = 0
-    for i, (at, step) in enumerate(hops):
-        wanted = jnp.where(part == i, at + step * odd, wanted)
-    values = jnp.where(hop == wanted, values, 0.0).astype(bf16)
+    values = jnp.where(hop == first + iota(values.shape, 1) // VH, values, 0.0).astype(bf16)
     shape = (len(STEPS) * FAR * HALVES * tok, arrived.shape[0])
     row, source = iota(shape, 0), iota(shape, 1)
     chip = chip_at(row // (HALVES * tok), where_ref)
@@ -285,14 +267,14 @@
             outs[0][:, cols] = got
 
 
-def attend_part(where, nx, arrived, pieces, tok, hops, before):
+def attend_part(where, nx, arrived, pieces, tok, first, before):
     depth = sum(p.shape[0] for p in pieces)
     width = (pieces[0].shape[1] - LAT) // HALVES
     count = len(pieces)
     last = before is not None
     part = jax.ShapeDtypeStruct((RING * HALVES * tok, width), f32)
     return pl.pallas_call(
-        functools.partial(attend_kernel, tok, nx, count, hops, last),
+        functools.partial(attend_kernel, tok, nx, count, first, last),
         out_shape=row_shapes(FAR * HALVES * tok, width) if last else part,
         in_specs=[smem(), vmem()] + [vmem()] * count + [vmem()] * last,
         out_specs=[vmem()] * 5 if last else vmem(),
@@ -614,29 +596,29 @@
     seqs, steps = queries.shape[:2]
     tok = seqs * steps
     where = jnp.stack([lax.axis_index(a) for a in ("x", "zb", "j")]).astype(jnp.int32)
-    odd = lax.rem(lax.axis_index("rep"), 2) if paired() else jnp.int32(0)
-    where = jnp.concatenate([where, lengths.astype(jnp.int32), odd.astype(jnp.int32).reshape(1)])
+    where = jnp.concatenate([where, lengths.astype(jnp.int32)])
 
     tops, lows = pack(value_up.T, out_proj)
-    top_near, low_near = swap_x_by_group(tops, 1, 3), swap_x_by_group(lows, 3, 1)
+    top_left = swap_x(tops, 1)
+    low_right = swap_x(lows, 3)
+    low_left = swap_x(lows, 1)
+    top_right = swap_x(tops, 3)
+
     outgoing = context_rows(where, nx, cache_kv, new_kv, queries)
     arrived = lax.all_to_all(
         outgoing.reshape(RING, nx * tok, LAT), ZAX, split_axis=0, concat_axis=0, tiled=True
     )
-    if paired():
-        top_other, low_other = swap_group(top_near), swap_group(low_near)
-    else:
-        top_other, low_other = swap_x(tops, 3), swap_x(lows, 1)
-    top_far, low_far = swap_x_by_group(top_near, 3, 1), swap_x_by_group(low_near, 1, 3)
-    near = [top_near, swap_core(top_near), low_near, swap_core(low_near)]
-    near += [top_far, low_far, swap_core(top_far), swap_core(low_far)]
-    near += [tops, lows, swap_core(tops), swap_core(lows)]
-    beyond = [top_other, swap_core(top_other), low_other, swap_core(low_other)]
+    top_far = swap_x(top_left, 3)
+    low_far = swap_x(low_right, 1)
+    near = [tops, lows, swap_core(tops), swap_core(lows)]
+    for pair in ((top_left, low_left), (top_right, low_right)):
+        near += [*pair, *map(swap_core, pair)]
+    beyond = [top_far, low_far, swap_core(top_far), swap_core(low_far)]
     others = [swap_core(w) for w in (w_gate, w_up, w_down)]
     weights = stage((w_gate, others[0], w_up, others[1], w_down, others[2]))
     arrived = arrived.reshape(RING * nx * tok, LAT)
-    most = attend_part(where, nx, arrived, near, tok, ((1, 1), (2, -1), (3, 0), (3, 0), (0, 0), (0, 0)), None)
-    own, *rows = attend_part(where, nx, arrived, beyond, tok, ((2, -1), (1, 1)), most)
+    most = attend_part(where, nx, arrived, near, tok, 0, None)
+    own, *rows = attend_part(where, nx, arrived, beyond, tok, nx - 1, most)
     added = reduce_z((own,), *rows)
 
     half = D // HALVES

time: 233 us -> 232 us (level)
  local copies, waits for them, and re-layouts: 6.46 us -> 2.03 us
    ppermute x9 -> x15, starting transfers between devices: 13.8 us -> 40.8 us  [swap_x(): lax.ppermute(a, 'x', [(i, i ^ bits) for i in range(lax.axis_size('x'))])]
    ppermute x9 -> x15, waiting for transfers between devices: 21.4 us -> 45.5 us  [swap_x(): lax.ppermute(a, 'x', [(i, i ^ bits) for i in range(lax.axis_size('x'))])]
    ppermute x6 -> x0, starting transfers between devices: 20.9 us -> none  [the longest x4 20.9 us: swap_x_by_group(): lax.ppermute(a, ('rep', 'x'), [(g * nx + i, g * nx + (i ^ b)) for g, b in...]
    ppermute x6 -> x0, waiting for transfers between devices: 17.2 us -> none  [the longest x4 17.2 us: swap_x_by_group(): lax.ppermute(a, ('rep', 'x'), [(g * nx + i, g * nx + (i ^ b)) for g, b in...]
    all_to_all x1, waiting for transfers between devices: 12.7 us -> 4.54 us  [layer(): lax.all_to_all(outgoing.reshape(RING, nx * tok, LAT), ZAX, split_axis=0,...]
    all_to_all x1, starting transfers between devices: 13 us -> 5.74 us  [layer(): lax.all_to_all(outgoing.reshape(RING, nx * tok, LAT), ZAX, split_axis=0,...]
    ppermute x8, waiting for transfers between devices: 11.5 us -> 15.5 us  [shift_z(): return lax.ppermute(a, ZAX, [(i, (i + step) % RING) for i in range(RING)])]
    unnamed x22 -> x14, local copies, waits for them, and re-layouts: 5.56 us -> 1.86 us
  transfers between devices with their start and end apart: 41 -> 41, of which waited for: 20 -> 15; matrix products, arithmetic and copies ran while one was open for 0% -> 0% of each run, Pallas kernels for 10% -> 10%
where the time goes in v1:
time: 232 us
  starting transfers between devices  88.7 us (38%)
  waiting for transfers between devices  78.3 us (34%)
  blocking collectives  36.9 us (16%)
  Pallas kernels  25.2 us (11%)
    ppermute x15, waiting for transfers between devices, swap_x(): lax.ppermute(a, 'x', [(i, i ^ bits) for i in range(lax.axis_size('x'))])  45.5 us
    ppermute x15, starting transfers between devices, swap_x(): lax.ppermute(a, 'x', [(i, i ^ bits) for i in range(lax.axis_size('x'))])  40.8 us
    all_gather x1, blocking collectives, layer(): ring = lax.all_gather(payload, ZAX, axis=0, tiled=True)  36.9 us
    ppermute x6, starting transfers between devices, swap_far(): return lax.ppermute(a, 'zb', [(i, i ^ bits) for i in range(FAR)])  24.1 us
    ppermute x8, starting transfers between devices, shift_z(): return lax.ppermute(a, ZAX, [(i, (i + step) % RING) for i in range(RING)])  16.6 us
    ppermute x8, waiting for transfers between devices, shift_z(): return lax.ppermute(a, ZAX, [(i, (i + step) % RING) for i in range(RING)])  15.5 us
    ppermute x6, waiting for transfers between devices, swap_far(): return lax.ppermute(a, 'zb', [(i, i ^ bits) for i in range(FAR)])  12.7 us
    pallas_call x1, Pallas kernels, context_rows(): pl.pallas_call(functools.partial(context_kernel, nx), grid=(seqs,), out_s...  5.88 us
  transfers between devices with their start and end apart: 41, of which 15 were waited for; matrix products, arithmetic and copies ran while one was open for 0% of the time, Pallas kernels for 10%

profile of v1, /device:TPU:34, one launch (start us, length us, event | category | flops | bytes accessed | tf_op | source)
XLA Modules:
  0.0 232.1 jit_solution(3683899834835212806)
XLA Ops:
  0.0 1.2 pack.1
  1.2 1.7 collective-permute-start.11
  3.0 18.1 %collective-permute-start = (bf16[32,7680]{1,0:T(8,128)(2,1)S(1)}, bf16[32,7680]{1,0:T(8,128)(2,1)S(1)}, u32[]{:S(2)}, u32[]{:S(2)}) collective-permute-start(bf16[32,7680]{1,0:T(8,128)(2,1)S(1)} %get-tuple-element.42.refs_0_), channel_id=1, source_target_pairs={{0,32},{32,0},{64,96},{96,64},{1,33},{33,1},{65,97},{97,65},{2,34}... | collective-permute-start | bytes 1474568 | tf_op jit(solution)/shard_map/ppermute | solution.py:40
  21.0 0.1 collective-permute-start.8
  21.2 2.4 %collective-permute-start.2 = (bf16[32,7680]{1,0:T(8,128)(2,1)S(1)}, bf16[32,7680]{1,0:T(8,128)(2,1)}, u32[]{:S(2)}, u32[]{:S(2)}) collective-permute-start(bf16[32,7680]{1,0:T(8,128)(2,1)S(1)} %get-tuple-element.43.refs_1_), channel_id=1, source_target_pairs={{0,96},{32,64},{64,32},{96,0},{1,97},{33,65},{65,33},{97,1},{2,98}... | collective-permute-start | bytes 1474568 | tf_op jit(solution)/shard_map/ppermute | solution.py:40
  23.6 9.5 %collective-permute-done.refs_4_ = bf16[32,7680]{1,0:T(8,128)(2,1)S(1)} collective-permute-done((bf16[32,7680]{1,0:T(8,128)(2,1)S(1)}, bf16[32,7680]{1,0:T(8,128)(2,1)S(1)}, u32[]{:S(2)}, u32[]{:S(2)}) %collective-permute-start) | collective-permute-done | bytes 491552 | tf_op jit(solution)/shard_map/ppermute | solution.py:40
  33.1 10.2 %collective-permute-done.8.refs_5_ = bf16[32,7680]{1,0:T(8,128)(2,1)S(1)} collective-permute-done((bf16[32,7680]{1,0:T(8,128)(2,1)S(1)}, bf16[32,7680]{1,0:T(8,128)(2,1)S(1)}, u32[]{:S(2)}, u32[]{:S(2)}) %collective-permute-start.8) | collective-permute-done | bytes 491552 | tf_op jit(solution)/shard_map/ppermute | solution.py:40
  43.3 2.5 %collective-permute-start.1 = (bf16[32,7680]{1,0:T(8,128)(2,1)S(1)}, bf16[32,7680]{1,0:T(8,128)(2,1)}, u32[]{:S(2)}, u32[]{:S(2)}) collective-permute-start(bf16[32,7680]{1,0:T(8,128)(2,1)S(1)} %collective-permute-done.refs_4_), channel_id=1, source_target_pairs={{0,96},{32,64},{64,32},{96,0},{1,97},{33,65},{65,33},{97,1},{2,98}... | collective-permute-start | bytes 1474568 | tf_op jit(solution)/shard_map/ppermute | solution.py:40
  45.8 0.7 pad_add_fusion.where_ref
  46.5 5.9 %context_rows.1 = bf16[256,512]{1,0:T(8,128)(2,1)} custom-call(s32[5]{0:T(128)S(1)} %pad_add_fusion.where_ref, bf16[2,576,2048]{2,1,0:T(8,128)(2,1)} %bitcast.20, bf16[2,2,64,576]{3,2,1,0:T(8,128)(2,1)} %queries.1, bf16[2,2,576]{2,1,0:T(2,128)(2,1)} %new.1), custom_call_target="tpu_custom_call" | custom-call | flops 1140850688 | bytes 4718592 | tf_op jit(solution)/shard_map/context_rows/pallas_call | solution.py:166
  52.4 5.7 %all-to-all-start = ((bf16[16,16,512]{2,1,0:T(8,128)(2,1)}), bf16[16,16,512]{2,1,0:T(8,128)(2,1)S(1)}, u32[]{:S(2)}, u32[]{:S(2)}) async-start(bf16[16,16,512]{2,1,0:T(8,128)(2,1)} %bitcast.4), calls=%async_computation | async-start | bytes 524288 | tf_op jit(solution)/shard_map/all_to_all | solution.py:608
  58.2 0.3 collective-permute-start.13
  58.5 1.7 collective-permute-start.3
  60.2 0.5 collective-permute-start.24
  60.7 0.1 collective-permute-start.25
  60.9 0.8 copy-done
  61.6 0.4 collective-permute-start.4
  62.0 10.2 %collective-permute-done.3.refs_1_ = bf16[32,7680]{1,0:T(8,128)(2,1)} collective-permute-done((bf16[32,7680]{1,0:T(8,128)(2,1)}, bf16[32,7680]{1,0:T(8,128)(2,1)}, u32[]{:S(2)}, u32[]{:S(2)}) %collective-permute-start.3) | collective-permute-done | bytes 491552 | tf_op jit(solution)/shard_map/ppermute | solution.py:40
  72.2 4.5 %all-to-all-done = bf16[16,16,512]{2,1,0:T(8,128)(2,1)S(1)} async-done(((bf16[16,16,512]{2,1,0:T(8,128)(2,1)}), bf16[16,16,512]{2,1,0:T(8,128)(2,1)S(1)}, u32[]{:S(2)}, u32[]{:S(2)}) %all-to-all-start) | async-done | bytes 262176 | tf_op jit(solution)/shard_map/all_to_all | solution.py:608
  76.8 1.0 copy-done.1
  77.8 3.0 %attend_part.2.refs_4_ = f32[128,3584]{1,0:T(8,128)S(1)} custom-call(s32[5]{0:T(128)S(1)} %pad_add_fusion.where_ref, bf16[256,512]{1,0:T(8,128)(2,1)S(1)} %bitcast.15, bf16[32,7680]{1,0:T(8,128)(2,1)S(1)} %get-tuple-element.42.refs_0_, bf16[32,7680]{1,0:T(8,128)(2,1)S(1)} %get-tuple-element.43.refs_1_, bf16[32,7680]{1,0:T(8,128)(2,1)S(1)} %collective-permute-done.6.refs_2_, ...), custom_call_target="tpu_custom_call" | custom-call | flops 1409286144 | bytes 5505024 | tf_op jit(solution)/shard_map/attend_part/pallas_call | solution.py:276
  80.9 2.4 %attend_part.3 = (f32[32,3584]{1,0:T(8,128)S(1)}, bf16[32,3584]{1,0:T(8,128)(2,1)S(1)}, bf16[32,3584]{1,0:T(8,128)(2,1)S(1)}, bf16[32,1792]{1,0:T(8,128)(2,1)S(1)}, bf16[32,1792]{1,0:T(8,128)(2,1)S(1)}) custom-call(s32[5]{0:T(128)S(1)} %pad_add_fusion.where_ref, bf16[256,512]{1,0:T(8,128)(2,1)S(1)} %bitcast.16, ...), custom_call_target="tpu_custom_call" | custom-call | flops 469762048 | bytes 1835008 | tf_op jit(solution)/shard_map/attend_part/pallas_call | solution.py:276
  83.3 0.6 collective-permute-start.16
  83.9 3.7 %collective-permute-start.17 = (bf16[32,1792]{1,0:T(8,128)(2,1)S(1)}, bf16[32,1792]{1,0:T(8,128)(2,1)S(1)}, u32[]{:S(2)}, u32[]{:S(2)}) collective-permute-start(bf16[32,1792]{1,0:T(8,128)(2,1)S(1)} %get-tuple-element.48), channel_id=1, source_target_pairs={{0,28},{2,30},{4,0},{6,2},{8,4},{10,6},{12,8},{14,10},{16,12},{18,... | collective-permute-start | bytes 344072 | tf_op jit(solution)/shard_map/ppermute | solution.py:44
  87.6 2.8 %collective-permute-done.16.refs_3_ = bf16[32,1792]{1,0:T(8,128)(2,1)S(1)} collective-permute-done((bf16[32,1792]{1,0:T(8,128)(2,1)S(1)}, bf16[32,1792]{1,0:T(8,128)(2,1)S(1)}, u32[]{:S(2)}, u32[]{:S(2)}) %collective-permute-start.16) | collective-permute-done | bytes 114720 | tf_op jit(solution)/shard_map/ppermute | solution.py:44
  90.4 3.0 %collective-permute-start.14 = (bf16[32,3584]{1,0:T(8,128)(2,1)S(1)}, bf16[32,3584]{1,0:T(8,128)(2,1)S(1)}, u32[]{:S(2)}, u32[]{:S(2)}) collective-permute-start(bf16[32,3584]{1,0:T(8,128)(2,1)S(1)} %get-tuple-element.45), channel_id=1, source_target_pairs={{0,2},{2,4},{4,6},{6,8},{8,10},{10,12},{12,14},{14,16},{16,18},{18... | collective-permute-start | bytes 688136 | tf_op jit(solution)/shard_map/ppermute | solution.py:44
  93.4 1.6 collective-permute-start.15
  95.0 3.4 %collective-permute-done.14.refs_1_ = bf16[32,3584]{1,0:T(8,128)(2,1)S(1)} collective-permute-done((bf16[32,3584]{1,0:T(8,128)(2,1)S(1)}, bf16[32,3584]{1,0:T(8,128)(2,1)S(1)}, u32[]{:S(2)}, u32[]{:S(2)}) %collective-permute-start.14) | collective-permute-done | bytes 229408 | tf_op jit(solution)/shard_map/ppermute | solution.py:44
  98.3 1.5 collective-permute-done.15.refs_2_
  99.8 0.1 merge.2
  99.9 4.2 %collective-permute-start.18 = (bf16[8,3584]{1,0:T(8,128)(2,1)S(1)}, bf16[8,3584]{1,0:T(8,128)(2,1)S(1)}, u32[]{:S(2)}, u32[]{:S(2)}) collective-permute-start(bf16[8,3584]{1,0:T(8,128)(2,1)S(1)} %get-tuple-element.50), channel_id=1, source_target_pairs={{0,8},{8,0},{16,24},{24,16},{1,9},{9,1},{17,25},{25,17},{2,10},{10... | collective-permute-start | bytes 172040 | tf_op jit(solution)/shard_map/ppermute | solution.py:48
  104.1 5.8 %collective-permute-start.19 = (bf16[8,3584]{1,0:T(8,128)(2,1)S(1)}, bf16[8,3584]{1,0:T(8,128)(2,1)S(1)}, u32[]{:S(2)}, u32[]{:S(2)}) collective-permute-start(bf16[8,3584]{1,0:T(8,128)(2,1)S(1)} %get-tuple-element.51), channel_id=1, source_target_pairs={{0,16},{8,24},{16,0},{24,8},{1,17},{9,25},{17,1},{25,9},{2,18},{10... | collective-permute-start | bytes 172040 | tf_op jit(solution)/shard_map/ppermute | solution.py:48
  109.9 2.7 %collective-permute-start.20 = (bf16[8,3584]{1,0:T(8,128)(2,1)S(1)}, bf16[8,3584]{1,0:T(8,128)(2,1)S(1)}, u32[]{:S(2)}, u32[]{:S(2)}) collective-permute-start(bf16[8,3584]{1,0:T(8,128)(2,1)S(1)} %get-tuple-element.52), channel_id=1, source_target_pairs={{0,24},{8,16},{16,8},{24,0},{1,25},{9,17},{17,9},{25,1},{2,26},{10... | collective-permute-start | bytes 172040 | tf_op jit(solution)/shard_map/ppermute | solution.py:48
  112.8 5.6 %collective-permute-done.19.two = bf16[8,3584]{1,0:T(8,128)(2,1)S(1)} collective-permute-done((bf16[8,3584]{1,0:T(8,128)(2,1)S(1)}, bf16[8,3584]{1,0:T(8,128)(2,1)S(1)}, u32[]{:S(2)}, u32[]{:S(2)}) %collective-permute-start.19) | collective-permute-done | bytes 57376 | tf_op jit(solution)/shard_map/ppermute | solution.py:48
  118.4 0.6 collective-permute-done.20.three
  119.1 0.6 route.1
  119.7 36.9 %all_gather.3.tokens = bf16[128,3712]{1,0:T(8,128)(2,1)S(1)} all-gather(bf16[8,3712]{1,0:T(8,128)(2,1)S(1)} %get-tuple-element.54), channel_id=1, replica_groups=mesh['rep'=2,'x'=4,'zb'=4,'j'=4,'c'=2] {'zb','j'}, dimensions={0}, use_global_device_ids=true | all-gather | bytes 1009664 | tf_op jit(solution)/shard_map/all_gather | solution.py:632
  156.6 1.4 dispatch.1
  158.0 1.7 collective-permute-start.21
  159.7 2.5 %collective-permute-start.22 = (bf16[32,7296]{1,0:T(8,128)(2,1)S(1)}, bf16[32,7296]{1,0:T(8,128)(2,1)S(1)}, u32[]{:S(2)}, u32[]{:S(2)}) collective-permute-start(bf16[32,7296]{1,0:T(8,128)(2,1)S(1)} %get-tuple-element.58), channel_id=1, source_target_pairs={{0,96},{32,64},{64,32},{96,0},{1,97},{33,65},{65,33},{97,1},{2,98}... | collective-permute-start | bytes 1400840 | tf_op jit(solution)/shard_map/ppermute | solution.py:40
  162.2 4.3 %stage.1 = (bf16[7168,512]{1,0:T(8,128)(2,1)S(1)}, bf16[256,7168]{1,0:T(8,128)(2,1)S(1)}) custom-call(bf16[7168,128]{1,0:T(8,128)(2,1)} %gate_a.1, bf16[7168,128]{1,0:T(8,128)(2,1)} %collective-permute-done.23.gate_b, bf16[7168,128]{1,0:T(8,128)(2,1)} %up_a.1, bf16[7168,128]{1,0:T(8,128)(2,1)} %collective-permute-done.24.up_b, bf16[128,7168]{1,0:T(8,128)(2,1)} %down_a.1, ...), custom_call_target="tpu_custom_call" | custom-call | flops 3670016000 | bytes 11010048 | tf_op jit(solution)/shard_map/stage/pallas_call | solution.py:370
  166.4 2.2 collective-permute-done.21.refs_1_
  168.6 7.4 %collective-permute-done.22.refs_2_ = bf16[32,7296]{1,0:T(8,128)(2,1)S(1)} collective-permute-done((bf16[32,7296]{1,0:T(8,128)(2,1)S(1)}, bf16[32,7296]{1,0:T(8,128)(2,1)S(1)}, u32[]{:S(2)}, u32[]{:S(2)}) %collective-permute-start.22) | collective-permute-done | bytes 466976 | tf_op jit(solution)/shard_map/ppermute | solution.py:40
  176.1 2.5 %expert_part.2 = (bf16[24,7168]{1,0:T(8,128)(2,1)S(1)}, bf16[24,7168]{1,0:T(8,128)(2,1)S(1)}, bf16[24,7168]{1,0:T(8,128)(2,1)S(1)}, bf16[8,7168]{1,0:T(8,128)(2,...) custom-call(s32[5]{0:T(128)S(1)} %pad_add_fusion.where_ref, ...), custom_call_target="tpu_custom_call" | custom-call | flops 2113929216 | bytes 1376256 | tf_op jit(solution)/shard_map/expert_part/pallas_call | solution.py:419
  178.6 0.1 collective-permute-start.30
  178.7 2.8 %collective-permute-start.31 = (bf16[24,7168]{1,0:T(8,128)(2,1)S(1)}, bf16[24,7168]{1,0:T(8,128)(2,1)S(1)}, u32[]{:S(2)}, u32[]{:S(2)}) collective-permute-start(bf16[24,7168]{1,0:T(8,128)(2,1)S(1)} %get-tuple-element.69), channel_id=1, source_target_pairs={{0,96},{32,64},{64,32},{96,0},{1,97},{33,65},{65,33},{97,1},{2,98}... | collective-permute-start | bytes 1032200 | tf_op jit(solution)/shard_map/ppermute | solution.py:40
  181.6 2.6 %expert_part.3 = (bf16[24,7168]{1,0:T(8,128)(2,1)S(1)}, bf16[8,7168]{1,0:T(8,128)(2,1)S(1)}) custom-call(s32[5]{0:T(128)S(1)} %pad_add_fusion.where_ref, bf16[32,7296]{1,0:T(8,128)(2,1)S(1)} %collective-permute-done.28.refs_0_, bf16[7168,512]{1,0:T(8,128)(2,1)S(1)} %get-tuple-element.59.refs_3_.refs_1_, bf16[256,7168]{1,0:T(8,128)(2,1)S(1)} %get-tuple-element.60.refs_4_.refs_2_), custom_call_target="tpu_custom_call" | custom-call | flops 704643072 | bytes 458752 | tf_op jit(solution)/shard_map/expert_part/pallas_call | solution.py:419
  184.2 1.3 collective-permute-start.32
  185.5 1.2 collective-permute-start.26
  186.7 1.7 collective-permute-start.27
  188.4 6.0 %collective-permute-done.32.refs_3_ = bf16[24,7168]{1,0:T(8,128)(2,1)S(1)} collective-permute-done((bf16[24,7168]{1,0:T(8,128)(2,1)S(1)}, bf16[24,7168]{1,0:T(8,128)(2,1)S(1)}, u32[]{:S(2)}, u32[]{:S(2)}) %collective-permute-start.32) | collective-permute-done | bytes 344096 | tf_op jit(solution)/shard_map/ppermute | solution.py:40
  194.4 0.4 collect.1
  194.7 0.8 collective-permute-start.33
  195.5 2.9 %collective-permute-start.34 = (bf16[32,3584]{1,0:T(8,128)(2,1)S(1)}, bf16[32,3584]{1,0:T(8,128)(2,1)S(1)}, u32[]{:S(2)}, u32[]{:S(2)}) collective-permute-start(bf16[32,3584]{1,0:T(8,128)(2,1)S(1)} %get-tuple-element.72), channel_id=1, source_target_pairs={{0,30},{2,0},{4,2},{6,4},{8,6},{10,8},{12,10},{14,12},{16,14},{18,... | collective-permute-start | bytes 688136 | tf_op jit(solution)/shard_map/ppermute | solution.py:44
  198.4 2.9 %collective-permute-start.29 = (bf16[8,7168]{1,0:T(8,128)(2,1)S(1)}, bf16[8,7168]{1,0:T(8,128)(2,1)S(1)}, u32[]{:S(2)}, u32[]{:S(2)}) collective-permute-start(bf16[8,7168]{1,0:T(8,128)(2,1)S(1)} %get-tuple-element.65), channel_id=1, source_target_pairs={{0,64},{32,96},{64,0},{96,32},{1,65},{33,97},{65,1},{97,33},{2,66}... | collective-permute-start | bytes 344072 | tf_op jit(solution)/shard_map/ppermute | solution.py:40
  201.3 4.1 %collective-permute-start.36 = (bf16[32,1792]{1,0:T(8,128)(2,1)S(1)}, bf16[32,1792]{1,0:T(8,128)(2,1)S(1)}, u32[]{:S(2)}, u32[]{:S(2)}) collective-permute-start(bf16[32,1792]{1,0:T(8,128)(2,1)S(1)} %get-tuple-element.74), channel_id=1, source_target_pairs={{0,28},{2,30},{4,0},{6,2},{8,4},{10,6},{12,8},{14,10},{16,12},{18,... | collective-permute-start | bytes 344072 | tf_op jit(solution)/shard_map/ppermute | solution.py:44
  205.4 7.8 %collective-permute-done.35.refs_7_ = bf16[32,1792]{1,0:T(8,128)(2,1)S(1)} collective-permute-done((bf16[32,1792]{1,0:T(8,128)(2,1)S(1)}, bf16[32,1792]{1,0:T(8,128)(2,1)S(1)}, u32[]{:S(2)}, u32[]{:S(2)}) %collective-permute-start.35) | collective-permute-done | bytes 114720 | tf_op jit(solution)/shard_map/ppermute | solution.py:44
  213.3 0.2 merge.3
  213.5 3.4 %collective-permute-start.37 = (bf16[8,3584]{1,0:T(8,128)(2,1)S(1)}, bf16[8,3584]{1,0:T(8,128)(2,1)S(1)}, u32[]{:S(2)}, u32[]{:S(2)}) collective-permute-start(bf16[8,3584]{1,0:T(8,128)(2,1)S(1)} %get-tuple-element.76), channel_id=1, source_target_pairs={{0,8},{8,0},{16,24},{24,16},{1,9},{9,1},{17,25},{25,17},{2,10},{10... | collective-permute-start | bytes 172040 | tf_op jit(solution)/shard_map/ppermute | solution.py:48
  216.9 4.5 %collective-permute-start.38 = (bf16[8,3584]{1,0:T(8,128)(2,1)S(1)}, bf16[8,3584]{1,0:T(8,128)(2,1)S(1)}, u32[]{:S(2)}, u32[]{:S(2)}) collective-permute-start(bf16[8,3584]{1,0:T(8,128)(2,1)S(1)} %get-tuple-element.77), channel_id=1, source_target_pairs={{0,16},{8,24},{16,0},{24,8},{1,17},{9,25},{17,1},{25,9},{2,18},{10... | collective-permute-start | bytes 172040 | tf_op jit(solution)/shard_map/ppermute | solution.py:48
  221.4 3.5 %collective-permute-start.39 = (bf16[8,3584]{1,0:T(8,128)(2,1)S(1)}, bf16[8,3584]{1,0:T(8,128)(2,1)S(1)}, u32[]{:S(2)}, u32[]{:S(2)}) collective-permute-start(bf16[8,3584]{1,0:T(8,128)(2,1)S(1)} %get-tuple-element.78), channel_id=1, source_target_pairs={{0,24},{8,16},{16,8},{24,0},{1,25},{9,17},{17,9},{25,1},{2,26},{10... | collective-permute-start | bytes 172040 | tf_op jit(solution)/shard_map/ppermute | solution.py:48
  225.0 5.7 %collective-permute-done.38.two = bf16[8,3584]{1,0:T(8,128)(2,1)S(1)} collective-permute-done((bf16[8,3584]{1,0:T(8,128)(2,1)S(1)}, bf16[8,3584]{1,0:T(8,128)(2,1)S(1)}, u32[]{:S(2)}, u32[]{:S(2)}) %collective-permute-start.38) | collective-permute-done | bytes 57376 | tf_op jit(solution)/shard_map/ppermute | solution.py:48
  230.7 0.8 collective-permute-done.39.three
  231.5 0.7 finish.1
  (55 shorter events, 0.3 us)
Async XLA Ops:
  1.2 20.0 %collective-permute-start.11 = (bf16[32,7680]{1,0:T(8,128)(2,1)S(1)}, bf16[32,7680]{1,0:T(8,128)(2,1)S(1)}, u32[]{:S(2)}, u32[]{:S(2)}) collective-permute-start(bf16[32,7680]{1,0:T(8,128)(2,1)S(1)} %get-tuple-element.42.refs_0_), channel_id=1, source_target_pairs={{0,96},{32,64},{64,32},{96,0},{1,97},{33,65},{65,33},{97,1},{2,98}... | collective-permute-start | bytes 1474568 | tf_op jit(solution)/shard_map/ppermute | solution.py:40
  3.0 20.6 %collective-permute-start.6 = (bf16[32,7680]{1,0:T(8,128)(2,1)S(1)}, bf16[32,7680]{1,0:T(8,128)(2,1)S(1)}, u32[]{:S(2)}, u32[]{:S(2)}) collective-permute-start(bf16[32,7680]{1,0:T(8,128)(2,1)S(1)} %get-tuple-element.42.refs_0_), channel_id=1, source_target_pairs={{0,1},{1,0},{2,3},{3,2},{4,5},{5,4},{6,7},{7,6},{8,9},{9,8},{10,11... | collective-permute-start | bytes 1474568 | tf_op jit(solution)/shard_map/ppermute | solution.py:52
  3.0 30.1 %collective-permute-start = (bf16[32,7680]{1,0:T(8,128)(2,1)S(1)}, bf16[32,7680]{1,0:T(8,128)(2,1)S(1)}, u32[]{:S(2)}, u32[]{:S(2)}) collective-permute-start(bf16[32,7680]{1,0:T(8,128)(2,1)S(1)} %get-tuple-element.42.refs_0_), channel_id=1, source_target_pairs={{0,32},{32,0},{64,96},{96,64},{1,33},{33,1},{65,97},{97,65},{2,34}... | collective-permute-start | bytes 1474568 | tf_op jit(solution)/shard_map/ppermute | solution.py:40
  21.0 22.3 %collective-permute-start.8 = (bf16[32,7680]{1,0:T(8,128)(2,1)S(1)}, bf16[32,7680]{1,0:T(8,128)(2,1)S(1)}, u32[]{:S(2)}, u32[]{:S(2)}) collective-permute-start(bf16[32,7680]{1,0:T(8,128)(2,1)S(1)} %get-tuple-element.43.refs_1_), channel_id=1, source_target_pairs={{0,32},{32,0},{64,96},{96,64},{1,33},{33,1},{65,97},{97,65},{2,34}... | collective-permute-start | bytes 1474568 | tf_op jit(solution)/shard_map/ppermute | solution.py:40
  21.2 24.6 %collective-permute-start.7 = (bf16[32,7680]{1,0:T(8,128)(2,1)S(1)}, bf16[32,7680]{1,0:T(8,128)(2,1)}, u32[]{:S(2)}, u32[]{:S(2)}) collective-permute-start(bf16[32,7680]{1,0:T(8,128)(2,1)S(1)} %get-tuple-element.43.refs_1_), channel_id=1, source_target_pairs={{0,1},{1,0},{2,3},{3,2},{4,5},{5,4},{6,7},{7,6},{8,9},{9,8},{10,11... | collective-permute-start | bytes 1474568 | tf_op jit(solution)/shard_map/ppermute | solution.py:52
  21.2 37.0 %collective-permute-start.2 = (bf16[32,7680]{1,0:T(8,128)(2,1)S(1)}, bf16[32,7680]{1,0:T(8,128)(2,1)}, u32[]{:S(2)}, u32[]{:S(2)}) collective-permute-start(bf16[32,7680]{1,0:T(8,128)(2,1)S(1)} %get-tuple-element.43.refs_1_), channel_id=1, source_target_pairs={{0,96},{32,64},{64,32},{96,0},{1,97},{33,65},{65,33},{97,1},{2,98}... | collective-permute-start | bytes 1474568 | tf_op jit(solution)/shard_map/ppermute | solution.py:40
  23.6 34.9 %collective-permute-start.12 = (bf16[32,7680]{1,0:T(8,128)(2,1)S(1)}, bf16[32,7680]{1,0:T(8,128)(2,1)}, u32[]{:S(2)}, u32[]{:S(2)}) collective-permute-start(bf16[32,7680]{1,0:T(8,128)(2,1)S(1)} %collective-permute-done.11.refs_8_), channel_id=1, source_target_pairs={{0,1},{1,0},{2,3},{3,2},{4,5},{5,4},{6,7},{7,6},{8,9},{9,8},{10,11... | collective-permute-start | bytes 1474568 | tf_op jit(solution)/shard_map/ppermute | solution.py:52
  33.1 27.1 %collective-permute-start.9 = (bf16[32,7680]{1,0:T(8,128)(2,1)S(1)}, bf16[32,7680]{1,0:T(8,128)(2,1)}, u32[]{:S(2)}, u32[]{:S(2)}) collective-permute-start(bf16[32,7680]{1,0:T(8,128)(2,1)S(1)} %collective-permute-done.refs_4_), channel_id=1, source_target_pairs={{0,1},{1,0},{2,3},{3,2},{4,5},{5,4},{6,7},{7,6},{8,9},{9,8},{10,11... | collective-permute-start | bytes 1474568 | tf_op jit(solution)/shard_map/ppermute | solution.py:52
  43.3 16.9 %collective-permute-start.1 = (bf16[32,7680]{1,0:T(8,128)(2,1)S(1)}, bf16[32,7680]{1,0:T(8,128)(2,1)}, u32[]{:S(2)}, u32[]{:S(2)}) collective-permute-start(bf16[32,7680]{1,0:T(8,128)(2,1)S(1)} %collective-permute-done.refs_4_), channel_id=1, source_target_pairs={{0,96},{32,64},{64,32},{96,0},{1,97},{33,65},{65,33},{97,1},{2,98}... | collective-permute-start | bytes 1474568 | tf_op jit(solution)/shard_map/ppermute | solution.py:40
  45.8 14.9 %collective-permute-start.10 = (bf16[32,7680]{1,0:T(8,128)(2,1)S(1)}, bf16[32,7680]{1,0:T(8,128)(2,1)}, u32[]{:S(2)}, u32[]{:S(2)}) collective-permute-start(bf16[32,7680]{1,0:T(8,128)(2,1)S(1)} %collective-permute-done.8.refs_5_), channel_id=1, source_target_pairs={{0,1},{1,0},{2,3},{3,2},{4,5},{5,4},{6,7},{7,6},{8,9},{9,8},{10,11... | collective-permute-start | bytes 1474568 | tf_op jit(solution)/shard_map/ppermute | solution.py:52
  52.4 24.4 %all-to-all-start = ((bf16[16,16,512]{2,1,0:T(8,128)(2,1)}), bf16[16,16,512]{2,1,0:T(8,128)(2,1)S(1)}, u32[]{:S(2)}, u32[]{:S(2)}) async-start(bf16[16,16,512]{2,1,0:T(8,128)(2,1)} %bitcast.4), calls=%async_computation | async-start | bytes 524288 | tf_op jit(solution)/shard_map/all_to_all | solution.py:608
  58.2 2.7 %collective-permute-start.13 = (bf16[32,7680]{1,0:T(8,128)(2,1)}, bf16[32,7680]{1,0:T(8,128)(2,1)S(1)}, u32[]{:S(2)}, u32[]{:S(2)}) collective-permute-start(bf16[32,7680]{1,0:T(8,128)(2,1)} %collective-permute-done.2.refs_9_), channel_id=1, source_target_pairs={{0,1},{1,0},{2,3},{3,2},{4,5},{5,4},{6,7},{7,6},{8,9},{9,8},{10,11... | collective-permute-start | bytes 1474568 | tf_op jit(solution)/shard_map/ppermute | solution.py:52
  58.5 13.7 %collective-permute-start.3 = (bf16[32,7680]{1,0:T(8,128)(2,1)}, bf16[32,7680]{1,0:T(8,128)(2,1)}, u32[]{:S(2)}, u32[]{:S(2)}) collective-permute-start(bf16[32,7680]{1,0:T(8,128)(2,1)} %collective-permute-done.2.refs_9_), channel_id=1, source_target_pairs={{0,32},{32,0},{64,96},{96,64},{1,33},{33,1},{65,97},{97,65},{2,34}... | collective-permute-start | bytes 1474568 | tf_op jit(solution)/shard_map/ppermute | solution.py:40
  60.2 102.0 %collective-permute-start.23 = (bf16[7168,128]{1,0:T(8,128)(2,1)}, bf16[7168,128]{1,0:T(8,128)(2,1)}, u32[]{:S(2)}, u32[]{:S(2)}) collective-permute-start(bf16[7168,128]{1,0:T(8,128)(2,1)} %gate_a.1), channel_id=1, source_target_pairs={{0,1},{1,0},{2,3},{3,2},{4,5},{5,4},{6,7},{7,6},{8,9},{9,8},{10,11... | collective-permute-start | bytes 5505032 | tf_op jit(solution)/shard_map/ppermute | solution.py:52
  60.2 102.0 %collective-permute-start.24 = (bf16[7168,128]{1,0:T(8,128)(2,1)}, bf16[7168,128]{1,0:T(8,128)(2,1)}, u32[]{:S(2)}, u32[]{:S(2)}) collective-permute-start(bf16[7168,128]{1,0:T(8,128)(2,1)} %up_a.1), channel_id=1, source_target_pairs={{0,1},{1,0},{2,3},{3,2},{4,5},{5,4},{6,7},{7,6},{8,9},{9,8},{10,11... | collective-permute-start | bytes 5505032 | tf_op jit(solution)/shard_map/ppermute | solution.py:52
  60.7 101.5 %collective-permute-start.25 = (bf16[128,7168]{1,0:T(8,128)(2,1)}, bf16[128,7168]{1,0:T(8,128)(2,1)}, u32[]{:S(2)}, u32[]{:S(2)}) collective-permute-start(bf16[128,7168]{1,0:T(8,128)(2,1)} %down_a.1), channel_id=1, source_target_pairs={{0,1},{1,0},{2,3},{3,2},{4,5},{5,4},{6,7},{7,6},{8,9},{9,8},{10,11... | collective-permute-start | bytes 5505032 | tf_op jit(solution)/shard_map/ppermute | solution.py:52
  60.9 0.8 copy-start
  61.6 19.2 %collective-permute-start.4 = (bf16[32,7680]{1,0:T(8,128)(2,1)}, bf16[32,7680]{1,0:T(8,128)(2,1)}, u32[]{:S(2)}, u32[]{:S(2)}) collective-permute-start(bf16[32,7680]{1,0:T(8,128)(2,1)} %collective-permute-done.1.refs_0_), channel_id=1, source_target_pairs={{0,1},{1,0},{2,3},{3,2},{4,5},{5,4},{6,7},{7,6},{8,9},{9,8},{10,11... | collective-permute-start | bytes 1474568 | tf_op jit(solution)/shard_map/ppermute | solution.py:52
  72.2 8.6 %collective-permute-start.5 = (bf16[32,7680]{1,0:T(8,128)(2,1)}, bf16[32,7680]{1,0:T(8,128)(2,1)}, u32[]{:S(2)}, u32[]{:S(2)}) collective-permute-start(bf16[32,7680]{1,0:T(8,128)(2,1)} %collective-permute-done.3.refs_1_), channel_id=1, source_target_pairs={{0,1},{1,0},{2,3},{3,2},{4,5},{5,4},{6,7},{7,6},{8,9},{9,8},{10,11... | collective-permute-start | bytes 1474568 | tf_op jit(solution)/shard_map/ppermute | solution.py:52
  76.8 1.0 copy-start.1
  80.9 31.8 %copy-start.4 = (bf16[7168]{0:T(1024)(128)(2,1)S(1)}, bf16[7168]{0:T(1024)(128)(2,1)}, u32[]{:S(2)}) copy-start(bf16[7168]{0:T(1024)(128)(2,1)} %param.21) | copy-start | bytes 43012
  80.9 31.8 %copy-start.3 = (bf16[2,2,7168]{2,1,0:T(2,128)(2,1)S(1)}, bf16[2,2,7168]{2,1,0:T(2,128)(2,1)}, u32[]{:S(2)}) copy-start(bf16[2,2,7168]{2,1,0:T(2,128)(2,1)} %param.18) | copy-start | bytes 172036
  83.3 35.7 %copy-start.5 = (s32[2,2,8]{2,1,0:T(2,128)S(1)}, s32[2,2,8]{2,1,0:T(2,128)}, u32[]{:S(2)}) copy-start(s32[2,2,8]{2,1,0:T(2,128)} %param.23) | copy-start | bytes 388
  83.3 35.7 %copy-start.6 = (s32[2,2,8]{2,1,0:T(2,128)S(1)}, s32[2,2,8]{2,1,0:T(2,128)}, u32[]{:S(2)}) copy-start(s32[2,2,8]{2,1,0:T(2,128)} %param.24) | copy-start | bytes 388
  83.3 35.7 %copy-start.2 = (bf16[7168,16]{0,1:T(8,128)(2,1)S(1)}, bf16[7168,16]{0,1:T(8,128)(2,1)}, u32[]{:S(2)}) copy-start(bf16[7168,16]{0,1:T(8,128)(2,1)} %param.22) | copy-start | bytes 688132
  83.3 7.0 %collective-permute-start.16 = (bf16[32,1792]{1,0:T(8,128)(2,1)S(1)}, bf16[32,1792]{1,0:T(8,128)(2,1)S(1)}, u32[]{:S(2)}, u32[]{:S(2)}) collective-permute-start(bf16[32,1792]{1,0:T(8,128)(2,1)S(1)} %get-tuple-element.47), channel_id=1, source_target_pairs={{0,4},{2,6},{4,8},{6,10},{8,12},{10,14},{12,16},{14,18},{16,20},{1... | collective-permute-start | bytes 344072 | tf_op jit(solution)/shard_map/ppermute | solution.py:44
  83.9 9.4 %collective-permute-start.17 = (bf16[32,1792]{1,0:T(8,128)(2,1)S(1)}, bf16[32,1792]{1,0:T(8,128)(2,1)S(1)}, u32[]{:S(2)}, u32[]{:S(2)}) collective-permute-start(bf16[32,1792]{1,0:T(8,128)(2,1)S(1)} %get-tuple-element.48), channel_id=1, source_target_pairs={{0,28},{2,30},{4,0},{6,2},{8,4},{10,6},{12,8},{14,10},{16,12},{18,... | collective-permute-start | bytes 344072 | tf_op jit(solution)/shard_map/ppermute | solution.py:44
  90.4 7.9 %collective-permute-start.14 = (bf16[32,3584]{1,0:T(8,128)(2,1)S(1)}, bf16[32,3584]{1,0:T(8,128)(2,1)S(1)}, u32[]{:S(2)}, u32[]{:S(2)}) collective-permute-start(bf16[32,3584]{1,0:T(8,128)(2,1)S(1)} %get-tuple-element.45), channel_id=1, source_target_pairs={{0,2},{2,4},{4,6},{6,8},{8,10},{10,12},{12,14},{14,16},{16,18},{18... | collective-permute-start | bytes 688136 | tf_op jit(solution)/shard_map/ppermute | solution.py:44
  93.4 6.4 %collective-permute-start.15 = (bf16[32,3584]{1,0:T(8,128)(2,1)S(1)}, bf16[32,3584]{1,0:T(8,128)(2,1)S(1)}, u32[]{:S(2)}, u32[]{:S(2)}) collective-permute-start(bf16[32,3584]{1,0:T(8,128)(2,1)S(1)} %get-tuple-element.46), channel_id=1, source_target_pairs={{0,30},{2,0},{4,2},{6,4},{8,6},{10,8},{12,10},{14,12},{16,14},{18,... | collective-permute-start | bytes 688136 | tf_op jit(solution)/shard_map/ppermute | solution.py:44
  99.9 10.0 %collective-permute-start.18 = (bf16[8,3584]{1,0:T(8,128)(2,1)S(1)}, bf16[8,3584]{1,0:T(8,128)(2,1)S(1)}, u32[]{:S(2)}, u32[]{:S(2)}) collective-permute-start(bf16[8,3584]{1,0:T(8,128)(2,1)S(1)} %get-tuple-element.50), channel_id=1, source_target_pairs={{0,8},{8,0},{16,24},{24,16},{1,9},{9,1},{17,25},{25,17},{2,10},{10... | collective-permute-start | bytes 172040 | tf_op jit(solution)/shard_map/ppermute | solution.py:48
  104.1 14.4 %collective-permute-start.19 = (bf16[8,3584]{1,0:T(8,128)(2,1)S(1)}, bf16[8,3584]{1,0:T(8,128)(2,1)S(1)}, u32[]{:S(2)}, u32[]{:S(2)}) collective-permute-start(bf16[8,3584]{1,0:T(8,128)(2,1)S(1)} %get-tuple-element.51), channel_id=1, source_target_pairs={{0,16},{8,24},{16,0},{24,8},{1,17},{9,25},{17,1},{25,9},{2,18},{10... | collective-permute-start | bytes 172040 | tf_op jit(solution)/shard_map/ppermute | solution.py:48
  109.9 9.1 %collective-permute-start.20 = (bf16[8,3584]{1,0:T(8,128)(2,1)S(1)}, bf16[8,3584]{1,0:T(8,128)(2,1)S(1)}, u32[]{:S(2)}, u32[]{:S(2)}) collective-permute-start(bf16[8,3584]{1,0:T(8,128)(2,1)S(1)} %get-tuple-element.52), channel_id=1, source_target_pairs={{0,24},{8,16},{16,8},{24,0},{1,25},{9,17},{17,9},{25,1},{2,26},{10... | collective-permute-start | bytes 172040 | tf_op jit(solution)/shard_map/ppermute | solution.py:48
  158.0 10.7 %collective-permute-start.21 = (bf16[32,7296]{1,0:T(8,128)(2,1)S(1)}, bf16[32,7296]{1,0:T(8,128)(2,1)S(1)}, u32[]{:S(2)}, u32[]{:S(2)}) collective-permute-start(bf16[32,7296]{1,0:T(8,128)(2,1)S(1)} %get-tuple-element.57), channel_id=1, source_target_pairs={{0,32},{32,0},{64,96},{96,64},{1,33},{33,1},{65,97},{97,65},{2,34}... | collective-permute-start | bytes 1400840 | tf_op jit(solution)/shard_map/ppermute | solution.py:40
  159.7 16.4 %collective-permute-start.22 = (bf16[32,7296]{1,0:T(8,128)(2,1)S(1)}, bf16[32,7296]{1,0:T(8,128)(2,1)S(1)}, u32[]{:S(2)}, u32[]{:S(2)}) collective-permute-start(bf16[32,7296]{1,0:T(8,128)(2,1)S(1)} %get-tuple-element.58), channel_id=1, source_target_pairs={{0,96},{32,64},{64,32},{96,0},{1,97},{33,65},{65,33},{97,1},{2,98}... | collective-permute-start | bytes 1400840 | tf_op jit(solution)/shard_map/ppermute | solution.py:40
  162.2 19.4 %collective-permute-start.28 = (bf16[32,7296]{1,0:T(8,128)(2,1)S(1)}, bf16[32,7296]{1,0:T(8,128)(2,1)S(1)}, u32[]{:S(2)}, u32[]{:S(2)}) collective-permute-start(bf16[32,7296]{1,0:T(8,128)(2,1)S(1)} %get-tuple-element.64), channel_id=1, source_target_pairs={{0,64},{32,96},{64,0},{96,32},{1,65},{33,97},{65,1},{97,33},{2,66}... | collective-permute-start | bytes 1400840 | tf_op jit(solution)/shard_map/ppermute | solution.py:40
  178.6 9.8 %collective-permute-start.30 = (bf16[24,7168]{1,0:T(8,128)(2,1)S(1)}, bf16[24,7168]{1,0:T(8,128)(2,1)S(1)}, u32[]{:S(2)}, u32[]{:S(2)}) collective-permute-start(bf16[24,7168]{1,0:T(8,128)(2,1)S(1)} %get-tuple-element.68), channel_id=1, source_target_pairs={{0,32},{32,0},{64,96},{96,64},{1,33},{33,1},{65,97},{97,65},{2,34}... | collective-permute-start | bytes 1032200 | tf_op jit(solution)/shard_map/ppermute | solution.py:40
  178.7 9.7 %collective-permute-start.31 = (bf16[24,7168]{1,0:T(8,128)(2,1)S(1)}, bf16[24,7168]{1,0:T(8,128)(2,1)S(1)}, u32[]{:S(2)}, u32[]{:S(2)}) collective-permute-start(bf16[24,7168]{1,0:T(8,128)(2,1)S(1)} %get-tuple-element.69), channel_id=1, source_target_pairs={{0,96},{32,64},{64,32},{96,0},{1,97},{33,65},{65,33},{97,1},{2,98}... | collective-permute-start | bytes 1032200 | tf_op jit(solution)/shard_map/ppermute | solution.py:40
  184.2 10.2 %collective-permute-start.32 = (bf16[24,7168]{1,0:T(8,128)(2,1)S(1)}, bf16[24,7168]{1,0:T(8,128)(2,1)S(1)}, u32[]{:S(2)}, u32[]{:S(2)}) collective-permute-start(bf16[24,7168]{1,0:T(8,128)(2,1)S(1)} %get-tuple-element.70), channel_id=1, source_target_pairs={{0,64},{32,96},{64,0},{96,32},{1,65},{33,97},{65,1},{97,33},{2,66}... | collective-permute-start | bytes 1032200 | tf_op jit(solution)/shard_map/ppermute | solution.py:40
  185.5 15.7 %collective-permute-start.26 = (bf16[8,7168]{1,0:T(8,128)(2,1)S(1)}, bf16[8,7168]{1,0:T(8,128)(2,1)S(1)}, u32[]{:S(2)}, u32[]{:S(2)}) collective-permute-start(bf16[8,7168]{1,0:T(8,128)(2,1)S(1)} %get-tuple-element.62), channel_id=1, source_target_pairs={{0,32},{32,0},{64,96},{96,64},{1,33},{33,1},{65,97},{97,65},{2,34}... | collective-permute-start | bytes 344072 | tf_op jit(solution)/shard_map/ppermute | solution.py:40
  186.7 14.6 %collective-permute-start.27 = (bf16[8,7168]{1,0:T(8,128)(2,1)S(1)}, bf16[8,7168]{1,0:T(8,128)(2,1)S(1)}, u32[]{:S(2)}, u32[]{:S(2)}) collective-permute-start(bf16[8,7168]{1,0:T(8,128)(2,1)S(1)} %get-tuple-element.63), channel_id=1, source_target_pairs={{0,96},{32,64},{64,32},{96,0},{1,97},{33,65},{65,33},{97,1},{2,98}... | collective-permute-start | bytes 344072 | tf_op jit(solution)/shard_map/ppermute | solution.py:40
  194.7 18.5 %collective-permute-start.33 = (bf16[32,3584]{1,0:T(8,128)(2,1)S(1)}, bf16[32,3584]{1,0:T(8,128)(2,1)S(1)}, u32[]{:S(2)}, u32[]{:S(2)}) collective-permute-start(bf16[32,3584]{1,0:T(8,128)(2,1)S(1)} %get-tuple-element.71), channel_id=1, source_target_pairs={{0,2},{2,4},{4,6},{6,8},{8,10},{10,12},{12,14},{14,16},{16,18},{18... | collective-permute-start | bytes 688136 | tf_op jit(solution)/shard_map/ppermute | solution.py:44
  195.5 17.8 %collective-permute-start.34 = (bf16[32,3584]{1,0:T(8,128)(2,1)S(1)}, bf16[32,3584]{1,0:T(8,128)(2,1)S(1)}, u32[]{:S(2)}, u32[]{:S(2)}) collective-permute-start(bf16[32,3584]{1,0:T(8,128)(2,1)S(1)} %get-tuple-element.72), channel_id=1, source_target_pairs={{0,30},{2,0},{4,2},{6,4},{8,6},{10,8},{12,10},{14,12},{16,14},{18,... | collective-permute-start | bytes 688136 | tf_op jit(solution)/shard_map/ppermute | solution.py:44
  198.4 7.0 %collective-permute-start.29 = (bf16[8,7168]{1,0:T(8,128)(2,1)S(1)}, bf16[8,7168]{1,0:T(8,128)(2,1)S(1)}, u32[]{:S(2)}, u32[]{:S(2)}) collective-permute-start(bf16[8,7168]{1,0:T(8,128)(2,1)S(1)} %get-tuple-element.65), channel_id=1, source_target_pairs={{0,64},{32,96},{64,0},{96,32},{1,65},{33,97},{65,1},{97,33},{2,66}... | collective-permute-start | bytes 344072 | tf_op jit(solution)/shard_map/ppermute | solution.py:40
  201.3 12.0 %collective-permute-start.35 = (bf16[32,1792]{1,0:T(8,128)(2,1)S(1)}, bf16[32,1792]{1,0:T(8,128)(2,1)S(1)}, u32[]{:S(2)}, u32[]{:S(2)}) collective-permute-start(bf16[32,1792]{1,0:T(8,128)(2,1)S(1)} %get-tuple-element.73), channel_id=1, source_target_pairs={{0,4},{2,6},{4,8},{6,10},{8,12},{10,14},{12,16},{14,18},{16,20},{1... | collective-permute-start | bytes 344072 | tf_op jit(solution)/shard_map/ppermute | solution.py:44
  201.3 12.0 %collective-permute-start.36 = (bf16[32,1792]{1,0:T(8,128)(2,1)S(1)}, bf16[32,1792]{1,0:T(8,128)(2,1)S(1)}, u32[]{:S(2)}, u32[]{:S(2)}) collective-permute-start(bf16[32,1792]{1,0:T(8,128)(2,1)S(1)} %get-tuple-element.74), channel_id=1, source_target_pairs={{0,28},{2,30},{4,0},{6,2},{8,4},{10,6},{12,8},{14,10},{16,12},{18,... | collective-permute-start | bytes 344072 | tf_op jit(solution)/shard_map/ppermute | solution.py:44
  213.5 11.4 %collective-permute-start.37 = (bf16[8,3584]{1,0:T(8,128)(2,1)S(1)}, bf16[8,3584]{1,0:T(8,128)(2,1)S(1)}, u32[]{:S(2)}, u32[]{:S(2)}) collective-permute-start(bf16[8,3584]{1,0:T(8,128)(2,1)S(1)} %get-tuple-element.76), channel_id=1, source_target_pairs={{0,8},{8,0},{16,24},{24,16},{1,9},{9,1},{17,25},{25,17},{2,10},{10... | collective-permute-start | bytes 172040 | tf_op jit(solution)/shard_map/ppermute | solution.py:48
  216.9 13.8 %collective-permute-start.38 = (bf16[8,3584]{1,0:T(8,128)(2,1)S(1)}, bf16[8,3584]{1,0:T(8,128)(2,1)S(1)}, u32[]{:S(2)}, u32[]{:S(2)}) collective-permute-start(bf16[8,3584]{1,0:T(8,128)(2,1)S(1)} %get-tuple-element.77), channel_id=1, source_target_pairs={{0,16},{8,24},{16,0},{24,8},{1,17},{9,25},{17,1},{25,9},{2,18},{10... | collective-permute-start | bytes 172040 | tf_op jit(solution)/shard_map/ppermute | solution.py:48
  221.4 10.0 %collective-permute-start.39 = (bf16[8,3584]{1,0:T(8,128)(2,1)S(1)}, bf16[8,3584]{1,0:T(8,128)(2,1)S(1)}, u32[]{:S(2)}, u32[]{:S(2)}) collective-permute-start(bf16[8,3584]{1,0:T(8,128)(2,1)S(1)} %get-tuple-element.78), channel_id=1, source_target_pairs={{0,24},{8,16},{16,8},{24,0},{1,25},{9,17},{17,9},{25,1},{2,26},{10... | collective-permute-start | bytes 172040 | tf_op jit(solution)/shard_map/ppermute | solution.py:48

commit v2 on v1

--- a/solution.py
+++ b/solution.py
@@ -60,11 +60,15 @@
     return jnp.where(mask, 1.0, 0.0).astype(bf16)
 
 
-COLUMNS = (0, 1, 3, 2)
-
-
 def column(index, x):
     return x ^ jnp.where(index == 2, 3, jnp.where(index == 3, 2, index))
+
+
+EXPERT_COLUMNS = (0, 2, 1, 3)
+
+
+def expert_column(index, x):
+    return x ^ jnp.where(index == 1, 2, jnp.where(index == 2, 1, index))
 
 
 STEPS = (0, 1, RING - 1, 2, RING - 2)
@@ -181,29 +185,27 @@
     )(where, held_in_hbm(keys), held_in_hbm(queries), held_in_hbm(new_kv))
 
 
-def pack_kernel(up, rows, tops, lows, sem):
-    half, at = tops.shape[0], up.shape[1]
-    copies = []
-    for i, out in enumerate((tops, lows)):
-        part = pl.ds(i * half, half)
-        copies.append(pltpu.make_async_copy(rows.at[part], out.at[:, pl.ds(at, rows.shape[1])], sem.at[i, 0]))
-        copies.append(pltpu.make_async_copy(up.at[part], out.at[:, pl.ds(0, at)], sem.at[i, 1]))
+def pack_kernel(first, up, rows, out, sem):
+    part, at = pl.ds(first, out.shape[0]), up.shape[1]
+    copies = [
+        pltpu.make_async_copy(rows.at[part], out.at[:, pl.ds(at, rows.shape[1])], sem.at[0]),
+        pltpu.make_async_copy(up.at[part], out.at[:, pl.ds(0, at)], sem.at[1]),
+    ]
     for copy in copies:
         copy.start()
     for copy in copies:
         copy.wait()
 
 
-def pack(up, rows):
-    shape = (rows.shape[0] // 2, up.shape[1] + rows.shape[1])
-    return pl.pallas_call(
-        pack_kernel,
-        out_shape=(jax.ShapeDtypeStruct(shape, bf16),) * 2,
+def pack(up, rows, first, count):
+    return pl.pallas_call(
+        functools.partial(pack_kernel, first),
+        out_shape=jax.ShapeDtypeStruct((count, up.shape[1] + rows.shape[1]), bf16),
         in_specs=[hbm()] * 2,
-        out_specs=[vmem()] * 2,
-        scratch_shapes=[pltpu.SemaphoreType.DMA((2, 2))],
+        out_specs=vmem(),
+        scratch_shapes=[pltpu.SemaphoreType.DMA((2,))],
         compiler_params=params(12),
-        cost_estimate=cost(1, 4 * rows.size),
+        cost_estimate=cost(1, 4 * count * rows.shape[1]),
         name="pack",
     )(held_in_hbm(up), held_in_hbm(rows))
 
@@ -287,27 +289,30 @@
 SEND_TILE = 512
 
 
-def dispatch_kernel(tok, nx, where_ref, tokens, *refs):
-    outs, (early, late) = refs[:nx], refs[nx:]
-    count, width = tokens.shape
-    half = width - EXTRA
-    table = tokens[:, pl.ds(half, EXTRA)]
+def slot_rows(tok, nx, where_ref, table):
+    count = table.shape[0]
     shape = (nx * CAP, EXTRA)
     row, place = iota(shape, 0), iota(shape, 1)
-    expert = FAR * column(row // CAP, where_ref[0]) + where_ref[1]
+    expert = FAR * expert_column(row // CAP, where_ref[0]) + where_ref[1]
     hot = one_hot(place == lax.rem(row, CAP) * EXPERTS + expert)
     got = lax.dot_general(hot, table, NT, preferred_element_type=f32)
     shape = (SLOTS, count)
     slot, token = iota(shape, 0), iota(shape, 1)
     source = slot // CAP
     chip = NEAR * lax.rem(source, FAR) + lax.rem(where_ref[2] + source // FAR + 1, NEAR)
-    parts = []
+    same = chip == token // (HALVES * tok)
+    half = lax.rem(token // tok, HALVES)
+    rows = []
     for r in range(nx):
         sel = jnp.where(lax.rem(slot, CAP) == 0, got[CAP * r : CAP * r + 1], got[CAP * r + 1 : CAP * r + 2])
-        parts.append(jnp.where(chip == token // (HALVES * tok), sel, 0.0))
-    of_half = lax.rem(token // tok, HALVES)
-    halves = [[jnp.where(of_half == c, sel, 0.0) for sel in parts] for c in range(HALVES)]
-    both = jnp.concatenate(sum(halves, []), axis=0).astype(bf16)
+        rows.append(jnp.where(same, sel, 0.0))
+    return [[jnp.where(half == c, sel, 0.0) for sel in rows] for c in range(HALVES)]
+
+
+def dispatch_kernel(tok, nx, where_ref, tokens, *outs):
+    half = tokens.shape[1] - EXTRA
+    table = tokens[:, pl.ds(half, EXTRA)]
+    both = jnp.concatenate(sum(slot_rows(tok, nx, where_ref, table), []), axis=0).astype(bf16)
     rows = nx * SLOTS
     for n in range(half // SEND_TILE):
         got = jnp.dot(both, tokens[:, pl.ds(n * SEND_TILE, SEND_TILE)], preferred_element_type=f32).astype(bf16)
@@ -318,31 +323,49 @@
     got = jnp.dot(both[:rows], table, preferred_element_type=f32).astype(bf16)
     for r in range(nx):
         outs[r][:, pl.ds(HALVES * half, EXTRA)] = got[r * SLOTS : (r + 1) * SLOTS]
+
+
+def dispatch(where, nx, tokens, tok):
+    count, width = tokens.shape
+    full = HALVES * (width - EXTRA) + EXTRA
+    return pl.pallas_call(
+        functools.partial(dispatch_kernel, tok, nx),
+        out_shape=(jax.ShapeDtypeStruct((SLOTS, full), bf16),) * nx,
+        in_specs=[smem(), vmem()],
+        out_specs=[vmem()] * nx,
+        compiler_params=params(12),
+        cost_estimate=cost(2 * nx * SLOTS * count * full, 4 * count * width),
+        name="dispatch",
+    )(where, tokens)
+
+
+def plan_kernel(tok, nx, where_ref, tokens, early, late):
+    count, width = tokens.shape
+    halves = slot_rows(tok, nx, where_ref, tokens[:, pl.ds(width - EXTRA, EXTRA)])
+    unit = HALVES * tok
     for out, group, at, end in ((early, 1, 0, EARLY), (late, 0, EARLY, SLOTS)):
         shape = (out.shape[0], count)
         row, token = iota(shape, 0), iota(shape, 1)
-        chip = chip_at(group * FAR + row // (HALVES * tok), where_ref)
-        take = (token // (HALVES * tok) == chip) & (lax.rem(token, HALVES * tok) == lax.rem(row, HALVES * tok))
-        sel = jnp.concatenate([sel[at:end] for sels in halves for sel in sels], axis=0).astype(bf16)
+        take = token // unit == chip_at(group * FAR + row // unit, where_ref)
+        take = take & (lax.rem(token, unit) == lax.rem(row, unit))
+        sel = jnp.concatenate([sel[at:end] for rows in halves for sel in rows], axis=0).astype(bf16)
         out[...] = lax.dot_general(one_hot(take), sel, NT, preferred_element_type=f32).astype(bf16)
 
 
-def dispatch(where, nx, tokens, tok):
-    count, width = tokens.shape
-    full = HALVES * (width - EXTRA) + EXTRA
+def plan(where, nx, tokens, tok):
+    count = tokens.shape[0]
     near = count // NEAR
     return pl.pallas_call(
-        functools.partial(dispatch_kernel, tok, nx),
-        out_shape=(jax.ShapeDtypeStruct((SLOTS, full), bf16),) * nx
-        + (
+        functools.partial(plan_kernel, tok, nx),
+        out_shape=(
             jax.ShapeDtypeStruct(((len(STEPS) - 1) * near, HALVES * nx * EARLY), bf16),
             jax.ShapeDtypeStruct((near, HALVES * nx * LATE), bf16),
         ),
         in_specs=[smem(), vmem()],
-        out_specs=[vmem()] * (nx + 2),
-        compiler_params=params(12),
-        cost_estimate=cost(2 * nx * SLOTS * count * full, 4 * count * width),
-        name="dispatch",
+        out_specs=[vmem()] * 2,
+        compiler_params=params(6),
+        cost_estimate=cost(2 * count * SLOTS * count, 4 * count * SLOTS),
+        name="plan",
     )(where, tokens)
 
 
@@ -598,8 +621,10 @@
     where = jnp.stack([lax.axis_index(a) for a in ("x", "zb", "j")]).astype(jnp.int32)
     where = jnp.concatenate([where, lengths.astype(jnp.int32)])
 
-    tops, lows = pack(value_up.T, out_proj)
+    half = out_proj.shape[0] // 2
+    tops = pack(value_up.T, out_proj, 0, half)
     top_left = swap_x(tops, 1)
+    lows = pack(value_up.T, out_proj, half, half)
     low_right = swap_x(lows, 3)
     low_left = swap_x(lows, 1)
     top_right = swap_x(tops, 3)
@@ -630,14 +655,18 @@
     hidden, payload = route(added, rows, gain, router.T, ids, places)
 
     ring = lax.all_gather(payload, ZAX, axis=0, tiled=True)
-    *sent, early, late = dispatch(where, nx, ring, tok)
-    got = [swap_x(sent[i], COLUMNS[i]) for i in range(1, nx)]
-    done = expert_part(where, (sent[0], *got[: nx - 2]), weights)
-    done = [list(done[: nx - 1]), list(done[nx - 1 :])]
-    for rows, last in zip(done, expert_part(where, got[nx - 2 :], weights)):
-        rows.append(last)
-    first = [done[0][0]] + [swap_x(done[0][i], COLUMNS[i]) for i in range(1, nx)]
-    second = [done[1][0]] + [swap_x(done[1][i], COLUMNS[i]) for i in range(1, nx)]
+    sent = dispatch(where, nx, ring, tok)
+    far = swap_x(sent[1], EXPERT_COLUMNS[1])
+    near = [swap_x(sent[i], EXPERT_COLUMNS[i]) for i in range(2, nx)]
+    early, late = plan(where, nx, ring, tok)
+    done = [[], []]
+    for groups in ((sent[0], far), tuple(near)):
+        rows = expert_part(where, groups, weights)
+        done[0] += rows[: len(groups)]
+        done[1] += rows[len(groups) :]
+    first = [done[0][0], swap_x(done[0][1], EXPERT_COLUMNS[1])]
+    first += [swap_x(done[0][i], EXPERT_COLUMNS[i]) for i in range(2, nx)]
+    second = [done[1][0]] + [swap_x(done[1][i], EXPERT_COLUMNS[i]) for i in range(1, nx)]
     added = reduce_z((late, *second), *collect(early, first))
     return finish(hidden, added, resid.shape)
 

time: 232 us -> 229 us (0.987)
  the two profiles are of different devices: /device:TPU:34 before, /device:TPU:164 now
where the time goes in v2:
time: 229 us; the launch traced here: 227 us
  starting transfers between devices  85.5 us (37%)
  waiting for transfers between devices  78.7 us (34%)
  blocking collectives  33.2 us (14%)
  Pallas kernels  27.2 us (12%)
    ppermute x15, waiting for transfers between devices, swap_x(): lax.ppermute(a, 'x', [(i, i ^ bits) for i in range(lax.axis_size('x'))])  44 us
    all_gather x1, blocking collectives, layer(): ring = lax.all_gather(payload, ZAX, axis=0, tiled=True)  33.2 us
    ppermute x6, starting transfers between devices, swap_far(): return lax.ppermute(a, 'zb', [(i, i ^ bits) for i in range(FAR)])  25.7 us
    ppermute x15, starting transfers between devices, swap_x(): lax.ppermute(a, 'x', [(i, i ^ bits) for i in range(lax.axis_size('x'))])  23.2 us
    all_to_all x1, starting transfers between devices, layer(): lax.all_to_all(outgoing.reshape(RING, nx * tok, LAT), ZAX, split_axis=0,...  22.9 us
    ppermute x6, waiting for transfers between devices, swap_far(): return lax.ppermute(a, 'zb', [(i, i ^ bits) for i in range(FAR)])  16.5 us
    ppermute x8, waiting for transfers between devices, shift_z(): return lax.ppermute(a, ZAX, [(i, (i + step) % RING) for i in range(RING)])  14.1 us
    ppermute x8, starting transfers between devices, shift_z(): return lax.ppermute(a, ZAX, [(i, (i + step) % RING) for i in range(RING)])  12.6 us
  transfers between devices with their start and end apart: 41, of which 15 were waited for; matrix products, arithmetic and copies ran while one was open for 0% of the time, Pallas kernels for 11%

profile of v2, /device:TPU:164, one launch (start us, length us, event | category | flops | bytes accessed | tf_op | source)
XLA Modules:
  0.0 227.0 jit_solution(2513558720767673435)
XLA Ops:
  0.0 1.1 pack.2.refs_0_
  1.1 0.5 collective-permute-start.11
  1.6 1.2 collective-permute-start
  2.8 1.0 pack.3.refs_1_
  3.9 0.9 collective-permute-start.8
  4.8 9.4 %collective-permute-done.11.refs_8_ = bf16[32,7680]{1,0:T(8,128)(2,1)S(1)} collective-permute-done((bf16[32,7680]{1,0:T(8,128)(2,1)S(1)}, bf16[32,7680]{1,0:T(8,128)(2,1)S(1)}, u32[]{:S(2)}, u32[]{:S(2)}) %collective-permute-start.11) | collective-permute-done | bytes 491552 | tf_op jit(solution)/shard_map/ppermute | solution.py:40
  14.2 0.4 collective-permute-start.2
  14.6 1.1 collective-permute-done.refs_4_
  15.7 10.1 %collective-permute-done.8.refs_5_ = bf16[32,7680]{1,0:T(8,128)(2,1)S(1)} collective-permute-done((bf16[32,7680]{1,0:T(8,128)(2,1)S(1)}, bf16[32,7680]{1,0:T(8,128)(2,1)S(1)}, u32[]{:S(2)}, u32[]{:S(2)}) %collective-permute-start.8) | collective-permute-done | bytes 491552 | tf_op jit(solution)/shard_map/ppermute | solution.py:40
  25.8 1.8 collective-permute-start.1
  27.7 5.9 %context_rows.1 = bf16[256,512]{1,0:T(8,128)(2,1)} custom-call(s32[5]{0:T(128)S(1)} %pad_add_fusion.where_ref, bf16[2,576,2048]{2,1,0:T(8,128)(2,1)} %bitcast.20, bf16[2,2,64,576]{3,2,1,0:T(8,128)(2,1)} %queries.1, bf16[2,2,576]{2,1,0:T(2,128)(2,1)} %new.1), custom_call_target="tpu_custom_call" | custom-call | flops 1140850688 | bytes 4718592 | tf_op jit(solution)/shard_map/context_rows/pallas_call | solution.py:170
  33.6 22.9 %all-to-all-start = ((bf16[16,16,512]{2,1,0:T(8,128)(2,1)}), bf16[16,16,512]{2,1,0:T(8,128)(2,1)S(1)}, u32[]{:S(2)}, u32[]{:S(2)}) async-start(bf16[16,16,512]{2,1,0:T(8,128)(2,1)} %bitcast.4), calls=%async_computation | async-start | bytes 524288 | tf_op jit(solution)/shard_map/all_to_all | solution.py:633
  56.5 0.1 collective-permute-start.13
  56.7 2.5 %collective-permute-start.3 = (bf16[32,7680]{1,0:T(8,128)(2,1)}, bf16[32,7680]{1,0:T(8,128)(2,1)}, u32[]{:S(2)}, u32[]{:S(2)}) collective-permute-start(bf16[32,7680]{1,0:T(8,128)(2,1)} %collective-permute-done.2.refs_9_), channel_id=1, source_target_pairs={{0,32},{32,0},{64,96},{96,64},{1,33},{33,1},{65,97},{97,65},{2,34}... | collective-permute-start | bytes 1474568 | tf_op jit(solution)/shard_map/ppermute | solution.py:40
  59.2 0.4 collective-permute-start.23
  59.7 0.1 collective-permute-start.24
  59.8 0.8 copy-done
  60.6 0.4 collective-permute-start.4
  61.0 10.2 %collective-permute-done.3.refs_1_ = bf16[32,7680]{1,0:T(8,128)(2,1)} collective-permute-done((bf16[32,7680]{1,0:T(8,128)(2,1)}, bf16[32,7680]{1,0:T(8,128)(2,1)}, u32[]{:S(2)}, u32[]{:S(2)}) %collective-permute-start.3) | collective-permute-done | bytes 491552 | tf_op jit(solution)/shard_map/ppermute | solution.py:40
  71.2 4.0 %all-to-all-done = bf16[16,16,512]{2,1,0:T(8,128)(2,1)S(1)} async-done(((bf16[16,16,512]{2,1,0:T(8,128)(2,1)}), bf16[16,16,512]{2,1,0:T(8,128)(2,1)S(1)}, u32[]{:S(2)}, u32[]{:S(2)}) %all-to-all-start) | async-done | bytes 262176 | tf_op jit(solution)/shard_map/all_to_all | solution.py:633
  75.2 1.0 copy-done.1
  76.3 3.0 %attend_part.2.refs_4_ = f32[128,3584]{1,0:T(8,128)S(1)} custom-call(s32[5]{0:T(128)S(1)} %pad_add_fusion.where_ref, bf16[256,512]{1,0:T(8,128)(2,1)S(1)} %bitcast.15, bf16[32,7680]{1,0:T(8,128)(2,1)S(1)} %pack.2.refs_0_, bf16[32,7680]{1,0:T(8,128)(2,1)S(1)} %pack.3.refs_1_, bf16[32,7680]{1,0:T(8,128)(2,1)S(1)} %collective-permute-done.6.refs_2_, ...), custom_call_target="tpu_custom_call" | custom-call | flops 1409286144 | bytes 5505024 | tf_op jit(solution)/shard_map/attend_part/pallas_call | solution.py:278
  79.3 2.4 %attend_part.3 = (f32[32,3584]{1,0:T(8,128)S(1)}, bf16[32,3584]{1,0:T(8,128)(2,1)S(1)}, bf16[32,3584]{1,0:T(8,128)(2,1)S(1)}, bf16[32,1792]{1,0:T(8,128)(2,1)S(1)}, bf16[32,1792]{1,0:T(8,128)(2,1)S(1)}) custom-call(s32[5]{0:T(128)S(1)} %pad_add_fusion.where_ref, bf16[256,512]{1,0:T(8,128)(2,1)S(1)} %bitcast.16, ...), custom_call_target="tpu_custom_call" | custom-call | flops 469762048 | bytes 1835008 | tf_op jit(solution)/shard_map/attend_part/pallas_call | solution.py:278
  81.8 2.3 %collective-permute-start.16 = (bf16[32,1792]{1,0:T(8,128)(2,1)S(1)}, bf16[32,1792]{1,0:T(8,128)(2,1)S(1)}, u32[]{:S(2)}, u32[]{:S(2)}) collective-permute-start(bf16[32,1792]{1,0:T(8,128)(2,1)S(1)} %get-tuple-element.43), channel_id=1, source_target_pairs={{0,4},{2,6},{4,8},{6,10},{8,12},{10,14},{12,16},{14,18},{16,20},{1... | collective-permute-start | bytes 344072 | tf_op jit(solution)/shard_map/ppermute | solution.py:44
  84.1 1.9 collective-permute-start.17
  86.0 4.0 %collective-permute-done.16.refs_3_ = bf16[32,1792]{1,0:T(8,128)(2,1)S(1)} collective-permute-done((bf16[32,1792]{1,0:T(8,128)(2,1)S(1)}, bf16[32,1792]{1,0:T(8,128)(2,1)S(1)}, u32[]{:S(2)}, u32[]{:S(2)}) %collective-permute-start.16) | collective-permute-done | bytes 114720 | tf_op jit(solution)/shard_map/ppermute | solution.py:44
  90.0 2.0 collective-permute-start.15
  92.0 4.7 %collective-permute-done.14.refs_1_ = bf16[32,3584]{1,0:T(8,128)(2,1)S(1)} collective-permute-done((bf16[32,3584]{1,0:T(8,128)(2,1)S(1)}, bf16[32,3584]{1,0:T(8,128)(2,1)S(1)}, u32[]{:S(2)}, u32[]{:S(2)}) %collective-permute-start.14) | collective-permute-done | bytes 229408 | tf_op jit(solution)/shard_map/ppermute | solution.py:44
  96.8 5.9 %collective-permute-start.18 = (bf16[8,3584]{1,0:T(8,128)(2,1)S(1)}, bf16[8,3584]{1,0:T(8,128)(2,1)S(1)}, u32[]{:S(2)}, u32[]{:S(2)}) collective-permute-start(bf16[8,3584]{1,0:T(8,128)(2,1)S(1)} %get-tuple-element.46), channel_id=1, source_target_pairs={{0,8},{8,0},{16,24},{24,16},{1,9},{9,1},{17,25},{25,17},{2,10},{10... | collective-permute-start | bytes 172040 | tf_op jit(solution)/shard_map/ppermute | solution.py:48
  102.7 4.5 %collective-permute-start.19 = (bf16[8,3584]{1,0:T(8,128)(2,1)S(1)}, bf16[8,3584]{1,0:T(8,128)(2,1)S(1)}, u32[]{:S(2)}, u32[]{:S(2)}) collective-permute-start(bf16[8,3584]{1,0:T(8,128)(2,1)S(1)} %get-tuple-element.47), channel_id=1, source_target_pairs={{0,16},{8,24},{16,0},{24,8},{1,17},{9,25},{17,1},{25,9},{2,18},{10... | collective-permute-start | bytes 172040 | tf_op jit(solution)/shard_map/ppermute | solution.py:48
  107.2 2.8 %collective-permute-start.20 = (bf16[8,3584]{1,0:T(8,128)(2,1)S(1)}, bf16[8,3584]{1,0:T(8,128)(2,1)S(1)}, u32[]{:S(2)}, u32[]{:S(2)}) collective-permute-start(bf16[8,3584]{1,0:T(8,128)(2,1)S(1)} %get-tuple-element.48), channel_id=1, source_target_pairs={{0,24},{8,16},{16,8},{24,0},{1,25},{9,17},{17,9},{25,1},{2,26},{10... | collective-permute-start | bytes 172040 | tf_op jit(solution)/shard_map/ppermute | solution.py:48
  110.2 8.2 %collective-permute-done.19.two = bf16[8,3584]{1,0:T(8,128)(2,1)S(1)} collective-permute-done((bf16[8,3584]{1,0:T(8,128)(2,1)S(1)}, bf16[8,3584]{1,0:T(8,128)(2,1)S(1)}, u32[]{:S(2)}, u32[]{:S(2)}) %collective-permute-start.19) | collective-permute-done | bytes 57376 | tf_op jit(solution)/shard_map/ppermute | solution.py:48
  118.5 0.6 route.1
  119.1 33.2 %all_gather.3.tokens = bf16[128,3712]{1,0:T(8,128)(2,1)S(1)} all-gather(bf16[8,3712]{1,0:T(8,128)(2,1)S(1)} %get-tuple-element.50), channel_id=1, replica_groups=mesh['rep'=2,'x'=4,'zb'=4,'j'=4,'c'=2] {'zb','j'}, dimensions={0}, use_global_device_ids=true | all-gather | bytes 1009664 | tf_op jit(solution)/shard_map/all_gather | solution.py:657
  152.4 1.3 dispatch.1
  153.7 5.5 %collective-permute-start.26 = (bf16[32,7296]{1,0:T(8,128)(2,1)S(1)}, bf16[32,7296]{1,0:T(8,128)(2,1)S(1)}, u32[]{:S(2)}, u32[]{:S(2)}) collective-permute-start(bf16[32,7296]{1,0:T(8,128)(2,1)S(1)} %get-tuple-element.58), channel_id=1, source_target_pairs={{0,32},{32,0},{64,96},{96,64},{1,33},{33,1},{65,97},{97,65},{2,34}... | collective-permute-start | bytes 1400840 | tf_op jit(solution)/shard_map/ppermute | solution.py:40
  159.2 2.2 collective-permute-start.21
  161.4 4.2 %stage.1 = (bf16[7168,512]{1,0:T(8,128)(2,1)S(1)}, bf16[256,7168]{1,0:T(8,128)(2,1)S(1)}) custom-call(bf16[7168,128]{1,0:T(8,128)(2,1)} %gate_a.1, bf16[7168,128]{1,0:T(8,128)(2,1)} %collective-permute-done.22.gate_b, bf16[7168,128]{1,0:T(8,128)(2,1)} %up_a.1, bf16[7168,128]{1,0:T(8,128)(2,1)} %collective-permute-done.23.up_b, bf16[128,7168]{1,0:T(8,128)(2,1)} %down_a.1, ...), custom_call_target="tpu_custom_call" | custom-call | flops 3670016000 | bytes 11010048 | tf_op jit(solution)/shard_map/stage/pallas_call | solution.py:393
  165.6 0.8 collective-permute-done.26.refs_0_
  166.5 7.5 %collective-permute-done.27.refs_1_ = bf16[32,7296]{1,0:T(8,128)(2,1)S(1)} collective-permute-done((bf16[32,7296]{1,0:T(8,128)(2,1)S(1)}, bf16[32,7296]{1,0:T(8,128)(2,1)S(1)}, u32[]{:S(2)}, u32[]{:S(2)}) %collective-permute-start.27) | collective-permute-done | bytes 466976 | tf_op jit(solution)/shard_map/ppermute | solution.py:40
  173.9 2.7 %expert_part.3 = (bf16[24,7168]{1,0:T(8,128)(2,1)S(1)}, bf16[24,7168]{1,0:T(8,128)(2,1)S(1)}, bf16[8,7168]{1,0:T(8,128)(2,1)S(1)}, bf16[8,7168]{1,0:T(8,128)(2,1)S(1)}) custom-call(s32[5]{0:T(128)S(1)} %pad_add_fusion.where_ref, bf16[32,7296]{1,0:T(8,128)(2,1)S(1)} %collective-permute-done.26.refs_0_, bf16[32,7296]{1,0:T(8,128)(2,1)S(1)} %collective-permute-done.27.refs_1_, ...), custom_call_target="tpu_custom_call" | custom-call | flops 1409286144 | bytes 917504 | tf_op jit(solution)/shard_map/expert_part/pallas_call | solution.py:442
  176.6 0.1 collective-permute-start.31
  176.7 0.4 collective-permute-start.32
  177.1 2.7 %expert_part.2 = (bf16[24,7168]{1,0:T(8,128)(2,1)S(1)}, bf16[24,7168]{1,0:T(8,128)(2,1)S(1)}, bf16[8,7168]{1,0:T(8,128)(2,1)S(1)}, bf16[8,7168]{1,0:T(8,128)(2,1)S(1)}) custom-call(s32[5]{0:T(128)S(1)} %pad_add_fusion.where_ref, bf16[32,7296]{1,0:T(8,128)(2,1)S(1)} %get-tuple-element.52.refs_0_, bf16[32,7296]{1,0:T(8,128)(2,1)S(1)} %collective-permute-done.21.refs_1_, ...), custom_call_target="tpu_custom_call" | custom-call | flops 1409286144 | bytes 917504 | tf_op jit(solution)/shard_map/expert_part/pallas_call | solution.py:442
  179.8 3.8 %collective-permute-start.30 = (bf16[24,7168]{1,0:T(8,128)(2,1)S(1)}, bf16[24,7168]{1,0:T(8,128)(2,1)S(1)}, u32[]{:S(2)}, u32[]{:S(2)}) collective-permute-start(bf16[24,7168]{1,0:T(8,128)(2,1)S(1)} %get-tuple-element.64), channel_id=1, source_target_pairs={{0,64},{32,96},{64,0},{96,32},{1,65},{33,97},{65,1},{97,33},{2,66}... | collective-permute-start | bytes 1032200 | tf_op jit(solution)/shard_map/ppermute | solution.py:40
  183.6 0.9 plan.1
  184.5 0.5 collective-permute-start.28
  185.0 0.2 collective-permute-start.29
  185.2 5.0 %collective-permute-done.30.refs_1_ = bf16[24,7168]{1,0:T(8,128)(2,1)S(1)} collective-permute-done((bf16[24,7168]{1,0:T(8,128)(2,1)S(1)}, bf16[24,7168]{1,0:T(8,128)(2,1)S(1)}, u32[]{:S(2)}, u32[]{:S(2)}) %collective-permute-start.30) | collective-permute-done | bytes 344096 | tf_op jit(solution)/shard_map/ppermute | solution.py:40
  190.2 0.4 collect.1
  190.5 0.2 collective-permute-start.33
  190.7 1.9 collective-permute-start.34
  192.7 3.1 %collective-permute-start.25 = (bf16[8,7168]{1,0:T(8,128)(2,1)S(1)}, bf16[8,7168]{1,0:T(8,128)(2,1)S(1)}, u32[]{:S(2)}, u32[]{:S(2)}) collective-permute-start(bf16[8,7168]{1,0:T(8,128)(2,1)S(1)} %get-tuple-element.57), channel_id=1, source_target_pairs={{0,64},{32,96},{64,0},{96,32},{1,65},{33,97},{65,1},{97,33},{2,66}... | collective-permute-start | bytes 344072 | tf_op jit(solution)/shard_map/ppermute | solution.py:40
  195.8 1.7 collective-permute-start.35
  197.5 2.5 %collective-permute-start.36 = (bf16[32,1792]{1,0:T(8,128)(2,1)S(1)}, bf16[32,1792]{1,0:T(8,128)(2,1)S(1)}, u32[]{:S(2)}, u32[]{:S(2)}) collective-permute-start(bf16[32,1792]{1,0:T(8,128)(2,1)S(1)} %get-tuple-element.70), channel_id=1, source_target_pairs={{0,28},{2,30},{4,0},{6,2},{8,4},{10,6},{12,8},{14,10},{16,12},{18,... | collective-permute-start | bytes 344072 | tf_op jit(solution)/shard_map/ppermute | solution.py:44
  199.9 2.9 %collective-permute-done.35.refs_7_ = bf16[32,1792]{1,0:T(8,128)(2,1)S(1)} collective-permute-done((bf16[32,1792]{1,0:T(8,128)(2,1)S(1)}, bf16[32,1792]{1,0:T(8,128)(2,1)S(1)}, u32[]{:S(2)}, u32[]{:S(2)}) %collective-permute-start.35) | collective-permute-done | bytes 114720 | tf_op jit(solution)/shard_map/ppermute | solution.py:44
  202.8 2.6 %collective-permute-done.36.refs_8_ = bf16[32,1792]{1,0:T(8,128)(2,1)S(1)} collective-permute-done((bf16[32,1792]{1,0:T(8,128)(2,1)S(1)}, bf16[32,1792]{1,0:T(8,128)(2,1)S(1)}, u32[]{:S(2)}, u32[]{:S(2)}) %collective-permute-start.36) | collective-permute-done | bytes 114720 | tf_op jit(solution)/shard_map/ppermute | solution.py:44
  205.4 0.2 merge.3
  205.7 4.5 %collective-permute-start.37 = (bf16[8,3584]{1,0:T(8,128)(2,1)S(1)}, bf16[8,3584]{1,0:T(8,128)(2,1)S(1)}, u32[]{:S(2)}, u32[]{:S(2)}) collective-permute-start(bf16[8,3584]{1,0:T(8,128)(2,1)S(1)} %get-tuple-element.72), channel_id=1, source_target_pairs={{0,8},{8,0},{16,24},{24,16},{1,9},{9,1},{17,25},{25,17},{2,10},{10... | collective-permute-start | bytes 172040 | tf_op jit(solution)/shard_map/ppermute | solution.py:48
  210.2 7.5 %collective-permute-start.38 = (bf16[8,3584]{1,0:T(8,128)(2,1)S(1)}, bf16[8,3584]{1,0:T(8,128)(2,1)S(1)}, u32[]{:S(2)}, u32[]{:S(2)}) collective-permute-start(bf16[8,3584]{1,0:T(8,128)(2,1)S(1)} %get-tuple-element.73), channel_id=1, source_target_pairs={{0,16},{8,24},{16,0},{24,8},{1,17},{9,25},{17,1},{25,9},{2,18},{10... | collective-permute-start | bytes 172040 | tf_op jit(solution)/shard_map/ppermute | solution.py:48
  217.7 0.4 collective-permute-start.39
  218.1 5.0 %collective-permute-done.38.two = bf16[8,3584]{1,0:T(8,128)(2,1)S(1)} collective-permute-done((bf16[8,3584]{1,0:T(8,128)(2,1)S(1)}, bf16[8,3584]{1,0:T(8,128)(2,1)S(1)}, u32[]{:S(2)}, u32[]{:S(2)}) %collective-permute-start.38) | collective-permute-done | bytes 57376 | tf_op jit(solution)/shard_map/ppermute | solution.py:48
  223.1 3.2 %collective-permute-done.39.three = bf16[8,3584]{1,0:T(8,128)(2,1)S(1)} collective-permute-done((bf16[8,3584]{1,0:T(8,128)(2,1)S(1)}, bf16[8,3584]{1,0:T(8,128)(2,1)S(1)}, u32[]{:S(2)}, u32[]{:S(2)}) %collective-permute-start.39) | collective-permute-done | bytes 57376 | tf_op jit(solution)/shard_map/ppermute | solution.py:48
  226.4 0.7 finish.1
  (59 shorter events, 0.6 us)
Async XLA Ops:
  0.0 27.6 %copy-start.7 = (s32[2]{0:T(128)S(1)}, s32[2]{0:T(128)}, u32[]{:S(2)}) copy-start(s32[2]{0:T(128)} %param.17) | copy-start | bytes 28
  1.1 13.2 %collective-permute-start.11 = (bf16[32,7680]{1,0:T(8,128)(2,1)S(1)}, bf16[32,7680]{1,0:T(8,128)(2,1)S(1)}, u32[]{:S(2)}, u32[]{:S(2)}) collective-permute-start(bf16[32,7680]{1,0:T(8,128)(2,1)S(1)} %pack.2.refs_0_), channel_id=1, source_target_pairs={{0,96},{32,64},{64,32},{96,0},{1,97},{33,65},{65,33},{97,1},{2,98}... | collective-permute-start | bytes 1474568 | tf_op jit(solution)/shard_map/ppermute | solution.py:40
  1.6 13.0 %collective-permute-start.6 = (bf16[32,7680]{1,0:T(8,128)(2,1)S(1)}, bf16[32,7680]{1,0:T(8,128)(2,1)S(1)}, u32[]{:S(2)}, u32[]{:S(2)}) collective-permute-start(bf16[32,7680]{1,0:T(8,128)(2,1)S(1)} %pack.2.refs_0_), channel_id=1, source_target_pairs={{0,1},{1,0},{2,3},{3,2},{4,5},{5,4},{6,7},{7,6},{8,9},{9,8},{10,11... | collective-permute-start | bytes 1474568 | tf_op jit(solution)/shard_map/ppermute | solution.py:52
  1.6 14.1 %collective-permute-start = (bf16[32,7680]{1,0:T(8,128)(2,1)S(1)}, bf16[32,7680]{1,0:T(8,128)(2,1)S(1)}, u32[]{:S(2)}, u32[]{:S(2)}) collective-permute-start(bf16[32,7680]{1,0:T(8,128)(2,1)S(1)} %pack.2.refs_0_), channel_id=1, source_target_pairs={{0,32},{32,0},{64,96},{96,64},{1,33},{33,1},{65,97},{97,65},{2,34}... | collective-permute-start | bytes 1474568 | tf_op jit(solution)/shard_map/ppermute | solution.py:40
  3.9 21.9 %collective-permute-start.8 = (bf16[32,7680]{1,0:T(8,128)(2,1)S(1)}, bf16[32,7680]{1,0:T(8,128)(2,1)S(1)}, u32[]{:S(2)}, u32[]{:S(2)}) collective-permute-start(bf16[32,7680]{1,0:T(8,128)(2,1)S(1)} %pack.3.refs_1_), channel_id=1, source_target_pairs={{0,32},{32,0},{64,96},{96,64},{1,33},{33,1},{65,97},{97,65},{2,34}... | collective-permute-start | bytes 1474568 | tf_op jit(solution)/shard_map/ppermute | solution.py:40
  4.8 22.8 %collective-permute-start.7 = (bf16[32,7680]{1,0:T(8,128)(2,1)S(1)}, bf16[32,7680]{1,0:T(8,128)(2,1)}, u32[]{:S(2)}, u32[]{:S(2)}) collective-permute-start(bf16[32,7680]{1,0:T(8,128)(2,1)S(1)} %pack.3.refs_1_), channel_id=1, source_target_pairs={{0,1},{1,0},{2,3},{3,2},{4,5},{5,4},{6,7},{7,6},{8,9},{9,8},{10,11... | collective-permute-start | bytes 1474568 | tf_op jit(solution)/shard_map/ppermute | solution.py:52
  14.2 42.3 %collective-permute-start.2 = (bf16[32,7680]{1,0:T(8,128)(2,1)S(1)}, bf16[32,7680]{1,0:T(8,128)(2,1)}, u32[]{:S(2)}, u32[]{:S(2)}) collective-permute-start(bf16[32,7680]{1,0:T(8,128)(2,1)S(1)} %pack.3.refs_1_), channel_id=1, source_target_pairs={{0,96},{32,64},{64,32},{96,0},{1,97},{33,65},{65,33},{97,1},{2,98}... | collective-permute-start | bytes 1474568 | tf_op jit(solution)/shard_map/ppermute | solution.py:40
  14.6 42.0 %collective-permute-start.12 = (bf16[32,7680]{1,0:T(8,128)(2,1)S(1)}, bf16[32,7680]{1,0:T(8,128)(2,1)}, u32[]{:S(2)}, u32[]{:S(2)}) collective-permute-start(bf16[32,7680]{1,0:T(8,128)(2,1)S(1)} %collective-permute-done.11.refs_8_), channel_id=1, source_target_pairs={{0,1},{1,0},{2,3},{3,2},{4,5},{5,4},{6,7},{7,6},{8,9},{9,8},{10,11... | collective-permute-start | bytes 1474568 | tf_op jit(solution)/shard_map/ppermute | solution.py:52
  15.7 43.5 %collective-permute-start.9 = (bf16[32,7680]{1,0:T(8,128)(2,1)S(1)}, bf16[32,7680]{1,0:T(8,128)(2,1)}, u32[]{:S(2)}, u32[]{:S(2)}) collective-permute-start(bf16[32,7680]{1,0:T(8,128)(2,1)S(1)} %collective-permute-done.refs_4_), channel_id=1, source_target_pairs={{0,1},{1,0},{2,3},{3,2},{4,5},{5,4},{6,7},{7,6},{8,9},{9,8},{10,11... | collective-permute-start | bytes 1474568 | tf_op jit(solution)/shard_map/ppermute | solution.py:52
  25.8 33.5 %collective-permute-start.1 = (bf16[32,7680]{1,0:T(8,128)(2,1)S(1)}, bf16[32,7680]{1,0:T(8,128)(2,1)}, u32[]{:S(2)}, u32[]{:S(2)}) collective-permute-start(bf16[32,7680]{1,0:T(8,128)(2,1)S(1)} %collective-permute-done.refs_4_), channel_id=1, source_target_pairs={{0,96},{32,64},{64,32},{96,0},{1,97},{33,65},{65,33},{97,1},{2,98}... | collective-permute-start | bytes 1474568 | tf_op jit(solution)/shard_map/ppermute | solution.py:40
  27.6 32.1 %collective-permute-start.10 = (bf16[32,7680]{1,0:T(8,128)(2,1)S(1)}, bf16[32,7680]{1,0:T(8,128)(2,1)}, u32[]{:S(2)}, u32[]{:S(2)}) collective-permute-start(bf16[32,7680]{1,0:T(8,128)(2,1)S(1)} %collective-permute-done.8.refs_5_), channel_id=1, source_target_pairs={{0,1},{1,0},{2,3},{3,2},{4,5},{5,4},{6,7},{7,6},{8,9},{9,8},{10,11... | collective-permute-start | bytes 1474568 | tf_op jit(solution)/shard_map/ppermute | solution.py:52
  33.6 41.7 %all-to-all-start = ((bf16[16,16,512]{2,1,0:T(8,128)(2,1)}), bf16[16,16,512]{2,1,0:T(8,128)(2,1)S(1)}, u32[]{:S(2)}, u32[]{:S(2)}) async-start(bf16[16,16,512]{2,1,0:T(8,128)(2,1)} %bitcast.4), calls=%async_computation | async-start | bytes 524288 | tf_op jit(solution)/shard_map/all_to_all | solution.py:633
  56.5 3.3 %collective-permute-start.13 = (bf16[32,7680]{1,0:T(8,128)(2,1)}, bf16[32,7680]{1,0:T(8,128)(2,1)S(1)}, u32[]{:S(2)}, u32[]{:S(2)}) collective-permute-start(bf16[32,7680]{1,0:T(8,128)(2,1)} %collective-permute-done.2.refs_9_), channel_id=1, source_target_pairs={{0,1},{1,0},{2,3},{3,2},{4,5},{5,4},{6,7},{7,6},{8,9},{9,8},{10,11... | collective-permute-start | bytes 1474568 | tf_op jit(solution)/shard_map/ppermute | solution.py:52
  56.7 14.5 %collective-permute-start.3 = (bf16[32,7680]{1,0:T(8,128)(2,1)}, bf16[32,7680]{1,0:T(8,128)(2,1)}, u32[]{:S(2)}, u32[]{:S(2)}) collective-permute-start(bf16[32,7680]{1,0:T(8,128)(2,1)} %collective-permute-done.2.refs_9_), channel_id=1, source_target_pairs={{0,32},{32,0},{64,96},{96,64},{1,33},{33,1},{65,97},{97,65},{2,34}... | collective-permute-start | bytes 1474568 | tf_op jit(solution)/shard_map/ppermute | solution.py:40
  59.1 100.0 %collective-permute-start.22 = (bf16[7168,128]{1,0:T(8,128)(2,1)}, bf16[7168,128]{1,0:T(8,128)(2,1)}, u32[]{:S(2)}, u32[]{:S(2)}) collective-permute-start(bf16[7168,128]{1,0:T(8,128)(2,1)} %gate_a.1), channel_id=1, source_target_pairs={{0,1},{1,0},{2,3},{3,2},{4,5},{5,4},{6,7},{7,6},{8,9},{9,8},{10,11... | collective-permute-start | bytes 5505032 | tf_op jit(solution)/shard_map/ppermute | solution.py:52
  59.2 102.2 %collective-permute-start.23 = (bf16[7168,128]{1,0:T(8,128)(2,1)}, bf16[7168,128]{1,0:T(8,128)(2,1)}, u32[]{:S(2)}, u32[]{:S(2)}) collective-permute-start(bf16[7168,128]{1,0:T(8,128)(2,1)} %up_a.1), channel_id=1, source_target_pairs={{0,1},{1,0},{2,3},{3,2},{4,5},{5,4},{6,7},{7,6},{8,9},{9,8},{10,11... | collective-permute-start | bytes 5505032 | tf_op jit(solution)/shard_map/ppermute | solution.py:52
  59.7 101.7 %collective-permute-start.24 = (bf16[128,7168]{1,0:T(8,128)(2,1)}, bf16[128,7168]{1,0:T(8,128)(2,1)}, u32[]{:S(2)}, u32[]{:S(2)}) collective-permute-start(bf16[128,7168]{1,0:T(8,128)(2,1)} %down_a.1), channel_id=1, source_target_pairs={{0,1},{1,0},{2,3},{3,2},{4,5},{5,4},{6,7},{7,6},{8,9},{9,8},{10,11... | collective-permute-start | bytes 5505032 | tf_op jit(solution)/shard_map/ppermute | solution.py:52
  59.8 0.8 copy-start
  60.6 18.8 %collective-permute-start.4 = (bf16[32,7680]{1,0:T(8,128)(2,1)}, bf16[32,7680]{1,0:T(8,128)(2,1)}, u32[]{:S(2)}, u32[]{:S(2)}) collective-permute-start(bf16[32,7680]{1,0:T(8,128)(2,1)} %collective-permute-done.1.refs_0_), channel_id=1, source_target_pairs={{0,1},{1,0},{2,3},{3,2},{4,5},{5,4},{6,7},{7,6},{8,9},{9,8},{10,11... | collective-permute-start | bytes 1474568 | tf_op jit(solution)/shard_map/ppermute | solution.py:52
  71.2 8.2 %collective-permute-start.5 = (bf16[32,7680]{1,0:T(8,128)(2,1)}, bf16[32,7680]{1,0:T(8,128)(2,1)}, u32[]{:S(2)}, u32[]{:S(2)}) collective-permute-start(bf16[32,7680]{1,0:T(8,128)(2,1)} %collective-permute-done.3.refs_1_), channel_id=1, source_target_pairs={{0,1},{1,0},{2,3},{3,2},{4,5},{5,4},{6,7},{7,6},{8,9},{9,8},{10,11... | collective-permute-start | bytes 1474568 | tf_op jit(solution)/shard_map/ppermute | solution.py:52
  75.2 1.0 copy-start.1
  79.3 30.7 %copy-start.4 = (bf16[7168]{0:T(1024)(128)(2,1)S(1)}, bf16[7168]{0:T(1024)(128)(2,1)}, u32[]{:S(2)}) copy-start(bf16[7168]{0:T(1024)(128)(2,1)} %param.21) | copy-start | bytes 43012
  79.3 30.7 %copy-start.3 = (bf16[2,2,7168]{2,1,0:T(2,128)(2,1)S(1)}, bf16[2,2,7168]{2,1,0:T(2,128)(2,1)}, u32[]{:S(2)}) copy-start(bf16[2,2,7168]{2,1,0:T(2,128)(2,1)} %param.18) | copy-start | bytes 172036
  81.8 36.7 %copy-start.5 = (s32[2,2,8]{2,1,0:T(2,128)S(1)}, s32[2,2,8]{2,1,0:T(2,128)}, u32[]{:S(2)}) copy-start(s32[2,2,8]{2,1,0:T(2,128)} %param.23) | copy-start | bytes 388
  81.8 36.7 %copy-start.6 = (s32[2,2,8]{2,1,0:T(2,128)S(1)}, s32[2,2,8]{2,1,0:T(2,128)}, u32[]{:S(2)}) copy-start(s32[2,2,8]{2,1,0:T(2,128)} %param.24) | copy-start | bytes 388
  81.8 36.7 %copy-start.2 = (bf16[7168,16]{0,1:T(8,128)(2,1)S(1)}, bf16[7168,16]{0,1:T(8,128)(2,1)}, u32[]{:S(2)}) copy-start(bf16[7168,16]{0,1:T(8,128)(2,1)} %param.22) | copy-start | bytes 688132
  81.8 8.2 %collective-permute-start.16 = (bf16[32,1792]{1,0:T(8,128)(2,1)S(1)}, bf16[32,1792]{1,0:T(8,128)(2,1)S(1)}, u32[]{:S(2)}, u32[]{:S(2)}) collective-permute-start(bf16[32,1792]{1,0:T(8,128)(2,1)S(1)} %get-tuple-element.43), channel_id=1, source_target_pairs={{0,4},{2,6},{4,8},{6,10},{8,12},{10,14},{12,16},{14,18},{16,20},{1... | collective-permute-start | bytes 344072 | tf_op jit(solution)/shard_map/ppermute | solution.py:44
  84.1 5.9 %collective-permute-start.17 = (bf16[32,1792]{1,0:T(8,128)(2,1)S(1)}, bf16[32,1792]{1,0:T(8,128)(2,1)S(1)}, u32[]{:S(2)}, u32[]{:S(2)}) collective-permute-start(bf16[32,1792]{1,0:T(8,128)(2,1)S(1)} %get-tuple-element.44), channel_id=1, source_target_pairs={{0,28},{2,30},{4,0},{6,2},{8,4},{10,6},{12,8},{14,10},{16,12},{18,... | collective-permute-start | bytes 344072 | tf_op jit(solution)/shard_map/ppermute | solution.py:44
  90.0 6.7 %collective-permute-start.14 = (bf16[32,3584]{1,0:T(8,128)(2,1)S(1)}, bf16[32,3584]{1,0:T(8,128)(2,1)S(1)}, u32[]{:S(2)}, u32[]{:S(2)}) collective-permute-start(bf16[32,3584]{1,0:T(8,128)(2,1)S(1)} %get-tuple-element.41), channel_id=1, source_target_pairs={{0,2},{2,4},{4,6},{6,8},{8,10},{10,12},{12,14},{14,16},{16,18},{18... | collective-permute-start | bytes 688136 | tf_op jit(solution)/shard_map/ppermute | solution.py:44
  90.0 6.7 %collective-permute-start.15 = (bf16[32,3584]{1,0:T(8,128)(2,1)S(1)}, bf16[32,3584]{1,0:T(8,128)(2,1)S(1)}, u32[]{:S(2)}, u32[]{:S(2)}) collective-permute-start(bf16[32,3584]{1,0:T(8,128)(2,1)S(1)} %get-tuple-element.42), channel_id=1, source_target_pairs={{0,30},{2,0},{4,2},{6,4},{8,6},{10,8},{12,10},{14,12},{16,14},{18,... | collective-permute-start | bytes 688136 | tf_op jit(solution)/shard_map/ppermute | solution.py:44
  96.8 10.4 %collective-permute-start.18 = (bf16[8,3584]{1,0:T(8,128)(2,1)S(1)}, bf16[8,3584]{1,0:T(8,128)(2,1)S(1)}, u32[]{:S(2)}, u32[]{:S(2)}) collective-permute-start(bf16[8,3584]{1,0:T(8,128)(2,1)S(1)} %get-tuple-element.46), channel_id=1, source_target_pairs={{0,8},{8,0},{16,24},{24,16},{1,9},{9,1},{17,25},{25,17},{2,10},{10... | collective-permute-start | bytes 172040 | tf_op jit(solution)/shard_map/ppermute | solution.py:48
  102.7 15.8 %collective-permute-start.19 = (bf16[8,3584]{1,0:T(8,128)(2,1)S(1)}, bf16[8,3584]{1,0:T(8,128)(2,1)S(1)}, u32[]{:S(2)}, u32[]{:S(2)}) collective-permute-start(bf16[8,3584]{1,0:T(8,128)(2,1)S(1)} %get-tuple-element.47), channel_id=1, source_target_pairs={{0,16},{8,24},{16,0},{24,8},{1,17},{9,25},{17,1},{25,9},{2,18},{10... | collective-permute-start | bytes 172040 | tf_op jit(solution)/shard_map/ppermute | solution.py:48
  107.2 11.2 %collective-permute-start.20 = (bf16[8,3584]{1,0:T(8,128)(2,1)S(1)}, bf16[8,3584]{1,0:T(8,128)(2,1)S(1)}, u32[]{:S(2)}, u32[]{:S(2)}) collective-permute-start(bf16[8,3584]{1,0:T(8,128)(2,1)S(1)} %get-tuple-element.48), channel_id=1, source_target_pairs={{0,24},{8,16},{16,8},{24,0},{1,25},{9,17},{17,9},{25,1},{2,26},{10... | collective-permute-start | bytes 172040 | tf_op jit(solution)/shard_map/ppermute | solution.py:48
  153.7 12.8 %collective-permute-start.26 = (bf16[32,7296]{1,0:T(8,128)(2,1)S(1)}, bf16[32,7296]{1,0:T(8,128)(2,1)S(1)}, u32[]{:S(2)}, u32[]{:S(2)}) collective-permute-start(bf16[32,7296]{1,0:T(8,128)(2,1)S(1)} %get-tuple-element.58), channel_id=1, source_target_pairs={{0,32},{32,0},{64,96},{96,64},{1,33},{33,1},{65,97},{97,65},{2,34}... | collective-permute-start | bytes 1400840 | tf_op jit(solution)/shard_map/ppermute | solution.py:40
  159.2 14.8 %collective-permute-start.27 = (bf16[32,7296]{1,0:T(8,128)(2,1)S(1)}, bf16[32,7296]{1,0:T(8,128)(2,1)S(1)}, u32[]{:S(2)}, u32[]{:S(2)}) collective-permute-start(bf16[32,7296]{1,0:T(8,128)(2,1)S(1)} %get-tuple-element.59), channel_id=1, source_target_pairs={{0,96},{32,64},{64,32},{96,0},{1,97},{33,65},{65,33},{97,1},{2,98}... | collective-permute-start | bytes 1400840 | tf_op jit(solution)/shard_map/ppermute | solution.py:40
  159.2 17.9 %collective-permute-start.21 = (bf16[32,7296]{1,0:T(8,128)(2,1)S(1)}, bf16[32,7296]{1,0:T(8,128)(2,1)S(1)}, u32[]{:S(2)}, u32[]{:S(2)}) collective-permute-start(bf16[32,7296]{1,0:T(8,128)(2,1)S(1)} %get-tuple-element.53), channel_id=1, source_target_pairs={{0,64},{32,96},{64,0},{96,32},{1,65},{33,97},{65,1},{97,33},{2,66}... | collective-permute-start | bytes 1400840 | tf_op jit(solution)/shard_map/ppermute | solution.py:40
  176.6 8.6 %collective-permute-start.31 = (bf16[24,7168]{1,0:T(8,128)(2,1)S(1)}, bf16[24,7168]{1,0:T(8,128)(2,1)S(1)}, u32[]{:S(2)}, u32[]{:S(2)}) collective-permute-start(bf16[24,7168]{1,0:T(8,128)(2,1)S(1)} %get-tuple-element.65), channel_id=1, source_target_pairs={{0,32},{32,0},{64,96},{96,64},{1,33},{33,1},{65,97},{97,65},{2,34}... | collective-permute-start | bytes 1032200 | tf_op jit(solution)/shard_map/ppermute | solution.py:40
  176.7 8.5 %collective-permute-start.32 = (bf16[24,7168]{1,0:T(8,128)(2,1)S(1)}, bf16[24,7168]{1,0:T(8,128)(2,1)S(1)}, u32[]{:S(2)}, u32[]{:S(2)}) collective-permute-start(bf16[24,7168]{1,0:T(8,128)(2,1)S(1)} %get-tuple-element.66), channel_id=1, source_target_pairs={{0,96},{32,64},{64,32},{96,0},{1,97},{33,65},{65,33},{97,1},{2,98}... | collective-permute-start | bytes 1032200 | tf_op jit(solution)/shard_map/ppermute | solution.py:40
  179.8 10.4 %collective-permute-start.30 = (bf16[24,7168]{1,0:T(8,128)(2,1)S(1)}, bf16[24,7168]{1,0:T(8,128)(2,1)S(1)}, u32[]{:S(2)}, u32[]{:S(2)}) collective-permute-start(bf16[24,7168]{1,0:T(8,128)(2,1)S(1)} %get-tuple-element.64), channel_id=1, source_target_pairs={{0,64},{32,96},{64,0},{96,32},{1,65},{33,97},{65,1},{97,33},{2,66}... | collective-permute-start | bytes 1032200 | tf_op jit(solution)/shard_map/ppermute | solution.py:40
  184.5 11.3 %collective-permute-start.28 = (bf16[8,7168]{1,0:T(8,128)(2,1)S(1)}, bf16[8,7168]{1,0:T(8,128)(2,1)S(1)}, u32[]{:S(2)}, u32[]{:S(2)}) collective-permute-start(bf16[8,7168]{1,0:T(8,128)(2,1)S(1)} %get-tuple-element.60), channel_id=1, source_target_pairs={{0,32},{32,0},{64,96},{96,64},{1,33},{33,1},{65,97},{97,65},{2,34}... | collective-permute-start | bytes 344072 | tf_op jit(solution)/shard_map/ppermute | solution.py:40
  185.0 12.5 %collective-permute-start.29 = (bf16[8,7168]{1,0:T(8,128)(2,1)S(1)}, bf16[8,7168]{1,0:T(8,128)(2,1)S(1)}, u32[]{:S(2)}, u32[]{:S(2)}) collective-permute-start(bf16[8,7168]{1,0:T(8,128)(2,1)S(1)} %get-tuple-element.61), channel_id=1, source_target_pairs={{0,96},{32,64},{64,32},{96,0},{1,97},{33,65},{65,33},{97,1},{2,98}... | collective-permute-start | bytes 344072 | tf_op jit(solution)/shard_map/ppermute | solution.py:40
  190.5 14.9 %collective-permute-start.33 = (bf16[32,3584]{1,0:T(8,128)(2,1)S(1)}, bf16[32,3584]{1,0:T(8,128)(2,1)S(1)}, u32[]{:S(2)}, u32[]{:S(2)}) collective-permute-start(bf16[32,3584]{1,0:T(8,128)(2,1)S(1)} %get-tuple-element.67), channel_id=1, source_target_pairs={{0,2},{2,4},{4,6},{6,8},{8,10},{10,12},{12,14},{14,16},{16,18},{18... | collective-permute-start | bytes 688136 | tf_op jit(solution)/shard_map/ppermute | solution.py:44
  190.7 14.7 %collective-permute-start.34 = (bf16[32,3584]{1,0:T(8,128)(2,1)S(1)}, bf16[32,3584]{1,0:T(8,128)(2,1)S(1)}, u32[]{:S(2)}, u32[]{:S(2)}) collective-permute-start(bf16[32,3584]{1,0:T(8,128)(2,1)S(1)} %get-tuple-element.68), channel_id=1, source_target_pairs={{0,30},{2,0},{4,2},{6,4},{8,6},{10,8},{12,10},{14,12},{16,14},{18,... | collective-permute-start | bytes 688136 | tf_op jit(solution)/shard_map/ppermute | solution.py:44
  192.7 7.3 %collective-permute-start.25 = (bf16[8,7168]{1,0:T(8,128)(2,1)S(1)}, bf16[8,7168]{1,0:T(8,128)(2,1)S(1)}, u32[]{:S(2)}, u32[]{:S(2)}) collective-permute-start(bf16[8,7168]{1,0:T(8,128)(2,1)S(1)} %get-tuple-element.57), channel_id=1, source_target_pairs={{0,64},{32,96},{64,0},{96,32},{1,65},{33,97},{65,1},{97,33},{2,66}... | collective-permute-start | bytes 344072 | tf_op jit(solution)/shard_map/ppermute | solution.py:40
  195.8 7.0 %collective-permute-start.35 = (bf16[32,1792]{1,0:T(8,128)(2,1)S(1)}, bf16[32,1792]{1,0:T(8,128)(2,1)S(1)}, u32[]{:S(2)}, u32[]{:S(2)}) collective-permute-start(bf16[32,1792]{1,0:T(8,128)(2,1)S(1)} %get-tuple-element.69), channel_id=1, source_target_pairs={{0,4},{2,6},{4,8},{6,10},{8,12},{10,14},{12,16},{14,18},{16,20},{1... | collective-permute-start | bytes 344072 | tf_op jit(solution)/shard_map/ppermute | solution.py:44
  197.5 8.0 %collective-permute-start.36 = (bf16[32,1792]{1,0:T(8,128)(2,1)S(1)}, bf16[32,1792]{1,0:T(8,128)(2,1)S(1)}, u32[]{:S(2)}, u32[]{:S(2)}) collective-permute-start(bf16[32,1792]{1,0:T(8,128)(2,1)S(1)} %get-tuple-element.70), channel_id=1, source_target_pairs={{0,28},{2,30},{4,0},{6,2},{8,4},{10,6},{12,8},{14,10},{16,12},{18,... | collective-permute-start | bytes 344072 | tf_op jit(solution)/shard_map/ppermute | solution.py:44
  205.7 12.5 %collective-permute-start.37 = (bf16[8,3584]{1,0:T(8,128)(2,1)S(1)}, bf16[8,3584]{1,0:T(8,128)(2,1)S(1)}, u32[]{:S(2)}, u32[]{:S(2)}) collective-permute-start(bf16[8,3584]{1,0:T(8,128)(2,1)S(1)} %get-tuple-element.72), channel_id=1, source_target_pairs={{0,8},{8,0},{16,24},{24,16},{1,9},{9,1},{17,25},{25,17},{2,10},{10... | collective-permute-start | bytes 172040 | tf_op jit(solution)/shard_map/ppermute | solution.py:48
  210.2 12.9 %collective-permute-start.38 = (bf16[8,3584]{1,0:T(8,128)(2,1)S(1)}, bf16[8,3584]{1,0:T(8,128)(2,1)S(1)}, u32[]{:S(2)}, u32[]{:S(2)}) collective-permute-start(bf16[8,3584]{1,0:T(8,128)(2,1)S(1)} %get-tuple-element.73), channel_id=1, source_target_pairs={{0,16},{8,24},{16,0},{24,8},{1,17},{9,25},{17,1},{25,9},{2,18},{10... | collective-permute-start | bytes 172040 | tf_op jit(solution)/shard_map/ppermute | solution.py:48
  217.7 8.7 %collective-permute-start.39 = (bf16[8,3584]{1,0:T(8,128)(2,1)S(1)}, bf16[8,3584]{1,0:T(8,128)(2,1)S(1)}, u32[]{:S(2)}, u32[]{:S(2)}) collective-permute-start(bf16[8,3584]{1,0:T(8,128)(2,1)S(1)} %get-tuple-element.74), channel_id=1, source_target_pairs={{0,24},{8,16},{16,8},{24,0},{1,25},{9,17},{17,9},{25,1},{2,26},{10... | collective-permute-start | bytes 172040 | tf_op jit(solution)/shard_map/ppermute | solution.py:48

commit v3 on v1

--- a/solution.py
+++ b/solution.py
@@ -60,11 +60,15 @@
     return jnp.where(mask, 1.0, 0.0).astype(bf16)
 
 
-COLUMNS = (0, 1, 3, 2)
-
-
 def column(index, x):
     return x ^ jnp.where(index == 2, 3, jnp.where(index == 3, 2, index))
+
+
+EXPERT_COLUMNS = (0, 2, 1, 3)
+
+
+def expert_column(index, x):
+    return x ^ jnp.where(index == 1, 2, jnp.where(index == 2, 1, index))
 
 
 STEPS = (0, 1, RING - 1, 2, RING - 2)
@@ -294,7 +298,7 @@
     table = tokens[:, pl.ds(half, EXTRA)]
     shape = (nx * CAP, EXTRA)
     row, place = iota(shape, 0), iota(shape, 1)
-    expert = FAR * column(row // CAP, where_ref[0]) + where_ref[1]
+    expert = FAR * expert_column(row // CAP, where_ref[0]) + where_ref[1]
     hot = one_hot(place == lax.rem(row, CAP) * EXPERTS + expert)
     got = lax.dot_general(hot, table, NT, preferred_element_type=f32)
     shape = (SLOTS, count)
@@ -460,7 +464,8 @@
 
 
 def merge_kernel(count, *refs):
-    mine, (right, left, ahead, behind, first), rest = refs[:count], refs[count : count + 5], refs[count + 5 :]
+    mine, (right, left, ahead, behind), outs = refs[:count], refs[count : count + 4], refs[count + 4 :]
+    first, one, upper, lower, three = outs
     block = first.shape[0]
     tiles = first.shape[1] // TILE
     for n in range(tiles):
@@ -473,32 +478,55 @@
         total = total + right[:, cols].astype(f32) + left[:, cols].astype(f32)
         total = total + last[:, pl.ds(at, TILE)].astype(f32)
         first[:, cols] = total[:block]
-        for k, out in enumerate(rest):
-            out[:, cols] = total[(k + 1) * block : (k + 2) * block].astype(bf16)
+        one[:, cols] = total[block : 2 * block]
+        three[:, cols] = total[3 * block :]
+        last, at = (upper, n * TILE) if n < tiles // 2 else (lower, (n - tiles // 2) * TILE)
+        last[:, pl.ds(at, TILE)] = total[2 * block : 3 * block].astype(bf16)
 
 
 def merge(mine, others):
     size, width = others[0].shape
-    block = (size // FAR, width)
+    block = jax.ShapeDtypeStruct((size // FAR, width), f32)
+    part = jax.ShapeDtypeStruct((size // FAR, width // 2), bf16)
     return pl.pallas_call(
         functools.partial(merge_kernel, len(mine)),
-        out_shape=(jax.ShapeDtypeStruct(block, f32),) + (jax.ShapeDtypeStruct(block, bf16),) * (FAR - 1),
+        out_shape=(block, block, part, part, block),
         in_specs=[vmem()] * (len(mine) + 4),
-        out_specs=[vmem()] * FAR,
+        out_specs=[vmem()] * 5,
         compiler_params=params(4),
         cost_estimate=cost(4 * size * width, 12 * size * width),
         name="merge",
     )(*mine, *others)
 
 
+def relay_kernel(one, three, upper, lower, to_one, to_three):
+    half = upper.shape[1]
+    to_one[:, :half] = one[:, :half].astype(bf16)
+    to_one[:, half:] = (one[:, half:] + lower[...].astype(f32)).astype(bf16)
+    to_three[:, :half] = (three[:, :half] + upper[...].astype(f32)).astype(bf16)
+    to_three[:, half:] = three[:, half:].astype(bf16)
+
+
+def relay(one, three, upper, lower):
+    return pl.pallas_call(
+        relay_kernel,
+        out_shape=(jax.ShapeDtypeStruct(one.shape, bf16),) * 2,
+        in_specs=[vmem()] * 4,
+        out_specs=[vmem()] * 2,
+        compiler_params=params(4),
+        cost_estimate=cost(one.size, 14 * one.size),
+        name="relay",
+    )(one, three, upper, lower)
+
+
 def half_swap(a):
     middle = a.shape[0] // 2
     return jnp.concatenate([a[middle:], a[:middle]], axis=0)
 
 
-def route_kernel(first, one, two, three, rows, gain, router, ids, slots, hidden, payload):
+def route_kernel(first, one, three, rows, gain, router, ids, slots, hidden, payload):
     count, half = rows.shape
-    total = first[...] + one[...].astype(f32) + two[...].astype(f32) + three[...].astype(f32)
+    total = first[...] + one[...].astype(f32) + three[...].astype(f32)
     total = rows[...].astype(f32) + total
     hidden[...] = total
     square = jnp.sum(total * total, axis=1, keepdims=True)
@@ -538,7 +566,7 @@
             jax.ShapeDtypeStruct((count, half), f32),
             jax.ShapeDtypeStruct((count, half + EXTRA), bf16),
         ),
-        in_specs=[vmem()] * 9,
+        in_specs=[vmem()] * 8,
         out_specs=[vmem()] * 2,
         compiler_params=params(4),
         cost_estimate=cost(4 * count * half * EXPERTS, 20 * count * half),
@@ -546,10 +574,10 @@
     )(*added, rows, gain, router, ids, slots)
 
 
-def finish_kernel(hidden, first, one, two, three, out):
+def finish_kernel(hidden, first, one, three, out):
     seqs, steps, _ = out.shape
     half = hidden.shape[1]
-    total = first[...] + one[...].astype(f32) + two[...].astype(f32) + three[...].astype(f32)
+    total = first[...] + one[...].astype(f32) + three[...].astype(f32)
     total = (hidden[...] + total).astype(bf16)
     for c in range(HALVES):
         for b in range(seqs):
@@ -561,18 +589,20 @@
     return pl.pallas_call(
         finish_kernel,
         out_shape=jax.ShapeDtypeStruct(shape, bf16),
-        in_specs=[vmem()] * 5,
+        in_specs=[vmem()] * 4,
         out_specs=vmem(),
         compiler_params=params(4),
-        cost_estimate=cost(5 * hidden.size, 14 * hidden.size),
+        cost_estimate=cost(4 * hidden.size, 12 * hidden.size),
         name="finish",
     )(hidden, *added)
 
 
 def reduce_z(mine, right, left, ahead, behind):
     others = shift_z(right, 1), shift_z(left, -1), shift_z(ahead, 2), shift_z(behind, -2)
-    first, *sent = merge(mine, others)
-    others = [swap_far(rows, k + 1) for k, rows in enumerate(sent)]
+    first, one, upper, lower, three = merge(mine, others)
+    upper, lower = swap_far(upper, 1), swap_far(lower, 3)
+    one, three = relay(one, three, upper, lower)
+    others = swap_far(one, 1), swap_far(three, 3)
     return first, *others
 
 
@@ -631,13 +661,16 @@
 
     ring = lax.all_gather(payload, ZAX, axis=0, tiled=True)
     *sent, early, late = dispatch(where, nx, ring, tok)
-    got = [swap_x(sent[i], COLUMNS[i]) for i in range(1, nx)]
-    done = expert_part(where, (sent[0], *got[: nx - 2]), weights)
-    done = [list(done[: nx - 1]), list(done[nx - 1 :])]
-    for rows, last in zip(done, expert_part(where, got[nx - 2 :], weights)):
-        rows.append(last)
-    first = [done[0][0]] + [swap_x(done[0][i], COLUMNS[i]) for i in range(1, nx)]
-    second = [done[1][0]] + [swap_x(done[1][i], COLUMNS[i]) for i in range(1, nx)]
+    far = swap_x(sent[1], EXPERT_COLUMNS[1])
+    near = [swap_x(sent[i], EXPERT_COLUMNS[i]) for i in range(2, nx)]
+    done = [[], []]
+    for groups in ((sent[0], far), tuple(near)):
+        rows = expert_part(where, groups, weights)
+        done[0] += rows[: len(groups)]
+        done[1] += rows[len(groups) :]
+    first = [done[0][0], swap_x(done[0][1], EXPERT_COLUMNS[1])]
+    first += [swap_x(done[0][i], EXPERT_COLUMNS[i]) for i in range(2, nx)]
+    second = [done[1][0]] + [swap_x(done[1][i], EXPERT_COLUMNS[i]) for i in range(1, nx)]
     added = reduce_z((late, *second), *collect(early, first))
     return finish(hidden, added, resid.shape)
 

time: 232 us -> 238 us (1.026)
  starting transfers between devices: 88.7 us -> 94.7 us
    ppermute x6 -> x8, starting transfers between devices: 24.1 us -> 30.2 us  [swap_far(): return lax.ppermute(a, 'zb', [(i, i ^ bits) for i in range(FAR)])]
    ppermute x8, waiting for transfers between devices: 15.5 us -> 12.6 us  [shift_z(): return lax.ppermute(a, ZAX, [(i, (i + step) % RING) for i in range(RING)])]
    ppermute x6 -> x8, waiting for transfers between devices: 12.7 us -> 14.9 us  [swap_far(): return lax.ppermute(a, 'zb', [(i, i ^ bits) for i in range(FAR)])]
  transfers between devices with their start and end apart: 41 -> 43, of which waited for: 15 -> 19; matrix products, arithmetic and copies ran while one was open for 0% -> 0% of each run, Pallas kernels for 10% -> 10%
where the time goes in v3:
time: 238 us
  starting transfers between devices  94.7 us (40%)
  waiting for transfers between devices  79.1 us (33%)
  blocking collectives  35.7 us (15%)
  Pallas kernels  25.4 us (11%)
    ppermute x15, waiting for transfers between devices, swap_x(): lax.ppermute(a, 'x', [(i, i ^ bits) for i in range(lax.axis_size('x'))])  47 us
    ppermute x15, starting transfers between devices, swap_x(): lax.ppermute(a, 'x', [(i, i ^ bits) for i in range(lax.axis_size('x'))])  41 us
    all_gather x1, blocking collectives, layer(): ring = lax.all_gather(payload, ZAX, axis=0, tiled=True)  35.7 us
    ppermute x8, starting transfers between devices, swap_far(): return lax.ppermute(a, 'zb', [(i, i ^ bits) for i in range(FAR)])  30.2 us
    ppermute x8, starting transfers between devices, shift_z(): return lax.ppermute(a, ZAX, [(i, (i + step) % RING) for i in range(RING)])  16.3 us
    ppermute x8, waiting for transfers between devices, swap_far(): return lax.ppermute(a, 'zb', [(i, i ^ bits) for i in range(FAR)])  14.9 us
    ppermute x8, waiting for transfers between devices, shift_z(): return lax.ppermute(a, ZAX, [(i, (i + step) % RING) for i in range(RING)])  12.6 us
    pallas_call x1, Pallas kernels, context_rows(): pl.pallas_call(functools.partial(context_kernel, nx), grid=(seqs,), out_s...  5.87 us
  transfers between devices with their start and end apart: 43, of which 19 were waited for; matrix products, arithmetic and copies ran while one was open for 0% of the time, Pallas kernels for 10%

profile of v3, /device:TPU:34, one launch (start us, length us, event | category | flops | bytes accessed | tf_op | source)
XLA Modules:
  0.0 237.9 jit_solution(11846495494162005019)
XLA Ops:
  0.0 1.2 pack.1
  1.2 1.7 collective-permute-start.11
  3.0 18.1 %collective-permute-start = (bf16[32,7680]{1,0:T(8,128)(2,1)S(1)}, bf16[32,7680]{1,0:T(8,128)(2,1)S(1)}, u32[]{:S(2)}, u32[]{:S(2)}) collective-permute-start(bf16[32,7680]{1,0:T(8,128)(2,1)S(1)} %get-tuple-element.48.refs_0_), channel_id=1, source_target_pairs={{0,32},{32,0},{64,96},{96,64},{1,33},{33,1},{65,97},{97,65},{2,34}... | collective-permute-start | bytes 1474568 | tf_op jit(solution)/shard_map/ppermute | solution.py:40
  21.2 2.4 %collective-permute-start.2 = (bf16[32,7680]{1,0:T(8,128)(2,1)S(1)}, bf16[32,7680]{1,0:T(8,128)(2,1)}, u32[]{:S(2)}, u32[]{:S(2)}) collective-permute-start(bf16[32,7680]{1,0:T(8,128)(2,1)S(1)} %get-tuple-element.49.refs_1_), channel_id=1, source_target_pairs={{0,96},{32,64},{64,32},{96,0},{1,97},{33,65},{65,33},{97,1},{2,98}... | collective-permute-start | bytes 1474568 | tf_op jit(solution)/shard_map/ppermute | solution.py:40
  23.6 9.5 %collective-permute-done.refs_4_ = bf16[32,7680]{1,0:T(8,128)(2,1)S(1)} collective-permute-done((bf16[32,7680]{1,0:T(8,128)(2,1)S(1)}, bf16[32,7680]{1,0:T(8,128)(2,1)S(1)}, u32[]{:S(2)}, u32[]{:S(2)}) %collective-permute-start) | collective-permute-done | bytes 491552 | tf_op jit(solution)/shard_map/ppermute | solution.py:40
  33.1 10.2 %collective-permute-done.8.refs_5_ = bf16[32,7680]{1,0:T(8,128)(2,1)S(1)} collective-permute-done((bf16[32,7680]{1,0:T(8,128)(2,1)S(1)}, bf16[32,7680]{1,0:T(8,128)(2,1)S(1)}, u32[]{:S(2)}, u32[]{:S(2)}) %collective-permute-start.8) | collective-permute-done | bytes 491552 | tf_op jit(solution)/shard_map/ppermute | solution.py:40
  43.3 2.5 %collective-permute-start.1 = (bf16[32,7680]{1,0:T(8,128)(2,1)S(1)}, bf16[32,7680]{1,0:T(8,128)(2,1)}, u32[]{:S(2)}, u32[]{:S(2)}) collective-permute-start(bf16[32,7680]{1,0:T(8,128)(2,1)S(1)} %collective-permute-done.refs_4_), channel_id=1, source_target_pairs={{0,96},{32,64},{64,32},{96,0},{1,97},{33,65},{65,33},{97,1},{2,98}... | collective-permute-start | bytes 1474568 | tf_op jit(solution)/shard_map/ppermute | solution.py:40
  45.8 0.7 pad_add_fusion.where_ref
  46.5 5.9 %context_rows.1 = bf16[256,512]{1,0:T(8,128)(2,1)} custom-call(s32[5]{0:T(128)S(1)} %pad_add_fusion.where_ref, bf16[2,576,2048]{2,1,0:T(8,128)(2,1)} %bitcast.20, bf16[2,2,64,576]{3,2,1,0:T(8,128)(2,1)} %queries.1, bf16[2,2,576]{2,1,0:T(2,128)(2,1)} %new.1), custom_call_target="tpu_custom_call" | custom-call | flops 1140850688 | bytes 4718592 | tf_op jit(solution)/shard_map/context_rows/pallas_call | solution.py:170
  52.4 5.7 %all-to-all-start = ((bf16[16,16,512]{2,1,0:T(8,128)(2,1)}), bf16[16,16,512]{2,1,0:T(8,128)(2,1)S(1)}, u32[]{:S(2)}, u32[]{:S(2)}) async-start(bf16[16,16,512]{2,1,0:T(8,128)(2,1)} %bitcast.4), calls=%async_computation | async-start | bytes 524288 | tf_op jit(solution)/shard_map/all_to_all | solution.py:638
  58.2 0.3 collective-permute-start.13
  58.5 1.7 collective-permute-start.3
  60.2 0.5 collective-permute-start.24
  60.8 0.8 copy-done
  61.7 0.4 collective-permute-start.4
  62.0 10.2 %collective-permute-done.3.refs_1_ = bf16[32,7680]{1,0:T(8,128)(2,1)} collective-permute-done((bf16[32,7680]{1,0:T(8,128)(2,1)}, bf16[32,7680]{1,0:T(8,128)(2,1)}, u32[]{:S(2)}, u32[]{:S(2)}) %collective-permute-start.3) | collective-permute-done | bytes 491552 | tf_op jit(solution)/shard_map/ppermute | solution.py:40
  72.2 4.5 %all-to-all-done = bf16[16,16,512]{2,1,0:T(8,128)(2,1)S(1)} async-done(((bf16[16,16,512]{2,1,0:T(8,128)(2,1)}), bf16[16,16,512]{2,1,0:T(8,128)(2,1)S(1)}, u32[]{:S(2)}, u32[]{:S(2)}) %all-to-all-start) | async-done | bytes 262176 | tf_op jit(solution)/shard_map/all_to_all | solution.py:638
  76.8 1.0 copy-done.1
  77.8 3.0 %attend_part.2.refs_4_ = f32[128,3584]{1,0:T(8,128)S(1)} custom-call(s32[5]{0:T(128)S(1)} %pad_add_fusion.where_ref, bf16[256,512]{1,0:T(8,128)(2,1)S(1)} %bitcast.15, bf16[32,7680]{1,0:T(8,128)(2,1)S(1)} %get-tuple-element.48.refs_0_, bf16[32,7680]{1,0:T(8,128)(2,1)S(1)} %get-tuple-element.49.refs_1_, bf16[32,7680]{1,0:T(8,128)(2,1)S(1)} %collective-permute-done.6.refs_2_, ...), custom_call_target="tpu_custom_call" | custom-call | flops 1409286144 | bytes 5505024 | tf_op jit(solution)/shard_map/attend_part/pallas_call | solution.py:280
  80.9 2.4 attend_part.3
  83.3 0.6 collective-permute-start.16
  83.9 3.6 %collective-permute-start.17 = (bf16[32,1792]{1,0:T(8,128)(2,1)S(1)}, bf16[32,1792]{1,0:T(8,128)(2,1)S(1)}, u32[]{:S(2)}, u32[]{:S(2)}) collective-permute-start(bf16[32,1792]{1,0:T(8,128)(2,1)S(1)} %get-tuple-element.54), channel_id=1, source_target_pairs={{0,28},{2,30},{4,0},{6,2},{8,4},{10,6},{12,8},{14,10},{16,12},{18,... | collective-permute-start | bytes 344072 | tf_op jit(solution)/shard_map/ppermute | solution.py:44
  87.5 2.8 %collective-permute-done.16.refs_3_ = bf16[32,1792]{1,0:T(8,128)(2,1)S(1)} collective-permute-done((bf16[32,1792]{1,0:T(8,128)(2,1)S(1)}, bf16[32,1792]{1,0:T(8,128)(2,1)S(1)}, u32[]{:S(2)}, u32[]{:S(2)}) %collective-permute-start.16) | collective-permute-done | bytes 114720 | tf_op jit(solution)/shard_map/ppermute | solution.py:44
  90.3 3.0 %collective-permute-start.14 = (bf16[32,3584]{1,0:T(8,128)(2,1)S(1)}, bf16[32,3584]{1,0:T(8,128)(2,1)S(1)}, u32[]{:S(2)}, u32[]{:S(2)}) collective-permute-start(bf16[32,3584]{1,0:T(8,128)(2,1)S(1)} %get-tuple-element.51), channel_id=1, source_target_pairs={{0,2},{2,4},{4,6},{6,8},{8,10},{10,12},{12,14},{14,16},{16,18},{18... | collective-permute-start | bytes 688136 | tf_op jit(solution)/shard_map/ppermute | solution.py:44
  93.3 1.6 collective-permute-start.15
  94.9 3.4 %collective-permute-done.14.refs_1_ = bf16[32,3584]{1,0:T(8,128)(2,1)S(1)} collective-permute-done((bf16[32,3584]{1,0:T(8,128)(2,1)S(1)}, bf16[32,3584]{1,0:T(8,128)(2,1)S(1)}, u32[]{:S(2)}, u32[]{:S(2)}) %collective-permute-start.14) | collective-permute-done | bytes 229408 | tf_op jit(solution)/shard_map/ppermute | solution.py:44
  98.3 1.5 collective-permute-done.15.refs_2_
  99.9 4.2 %collective-permute-start.18 = (bf16[8,1792]{1,0:T(8,128)(2,1)S(1)}, bf16[8,1792]{1,0:T(8,128)(2,1)S(1)}, u32[]{:S(2)}, u32[]{:S(2)}) collective-permute-start(bf16[8,1792]{1,0:T(8,128)(2,1)S(1)} %get-tuple-element.58), channel_id=1, source_target_pairs={{0,8},{8,0},{16,24},{24,16},{1,9},{9,1},{17,25},{25,17},{2,10},{10... | collective-permute-start | bytes 86024 | tf_op jit(solution)/shard_map/ppermute | solution.py:48
  104.1 4.0 %collective-permute-start.19 = (bf16[8,1792]{1,0:T(8,128)(2,1)S(1)}, bf16[8,1792]{1,0:T(8,128)(2,1)S(1)}, u32[]{:S(2)}, u32[]{:S(2)}) collective-permute-start(bf16[8,1792]{1,0:T(8,128)(2,1)S(1)} %get-tuple-element.59), channel_id=1, source_target_pairs={{0,24},{8,16},{16,8},{24,0},{1,25},{9,17},{17,9},{25,1},{2,26},{10... | collective-permute-start | bytes 86024 | tf_op jit(solution)/shard_map/ppermute | solution.py:48
  108.1 3.8 %collective-permute-done.19.lower = bf16[8,1792]{1,0:T(8,128)(2,1)S(1)} collective-permute-done((bf16[8,1792]{1,0:T(8,128)(2,1)S(1)}, bf16[8,1792]{1,0:T(8,128)(2,1)S(1)}, u32[]{:S(2)}, u32[]{:S(2)}) %collective-permute-start.19) | collective-permute-done | bytes 28704 | tf_op jit(solution)/shard_map/ppermute | solution.py:48
  111.9 2.2 collective-permute-start.20
  114.1 4.3 %collective-permute-start.21 = (bf16[8,3584]{1,0:T(8,128)(2,1)S(1)}, bf16[8,3584]{1,0:T(8,128)(2,1)S(1)}, u32[]{:S(2)}, u32[]{:S(2)}) collective-permute-start(bf16[8,3584]{1,0:T(8,128)(2,1)S(1)} %get-tuple-element.61), channel_id=1, source_target_pairs={{0,24},{8,16},{16,8},{24,0},{1,25},{9,17},{17,9},{25,1},{2,26},{10... | collective-permute-start | bytes 172040 | tf_op jit(solution)/shard_map/ppermute | solution.py:48
  118.6 1.5 collective-permute-done.20.one
  120.1 2.6 %collective-permute-done.21.three = bf16[8,3584]{1,0:T(8,128)(2,1)S(1)} collective-permute-done((bf16[8,3584]{1,0:T(8,128)(2,1)S(1)}, bf16[8,3584]{1,0:T(8,128)(2,1)S(1)}, u32[]{:S(2)}, u32[]{:S(2)}) %collective-permute-start.21) | collective-permute-done | bytes 57376 | tf_op jit(solution)/shard_map/ppermute | solution.py:48
  122.8 0.6 route.1
  123.4 35.7 %all_gather.3.tokens = bf16[128,3712]{1,0:T(8,128)(2,1)S(1)} all-gather(bf16[8,3712]{1,0:T(8,128)(2,1)S(1)} %get-tuple-element.63), channel_id=1, replica_groups=mesh['rep'=2,'x'=4,'zb'=4,'j'=4,'c'=2] {'zb','j'}, dimensions={0}, use_global_device_ids=true | all-gather | bytes 1009664 | tf_op jit(solution)/shard_map/all_gather | solution.py:662
  159.1 1.4 dispatch.1
  160.5 1.8 collective-permute-start.27
  162.3 2.5 %collective-permute-start.28 = (bf16[32,7296]{1,0:T(8,128)(2,1)S(1)}, bf16[32,7296]{1,0:T(8,128)(2,1)S(1)}, u32[]{:S(2)}, u32[]{:S(2)}) collective-permute-start(bf16[32,7296]{1,0:T(8,128)(2,1)S(1)} %get-tuple-element.72), channel_id=1, source_target_pairs={{0,96},{32,64},{64,32},{96,0},{1,97},{33,65},{65,33},{97,1},{2,98}... | collective-permute-start | bytes 1400840 | tf_op jit(solution)/shard_map/ppermute | solution.py:40
  164.8 4.3 %stage.1 = (bf16[7168,512]{1,0:T(8,128)(2,1)S(1)}, bf16[256,7168]{1,0:T(8,128)(2,1)S(1)}) custom-call(bf16[7168,128]{1,0:T(8,128)(2,1)} %gate_a.1, bf16[7168,128]{1,0:T(8,128)(2,1)} %collective-permute-done.23.gate_b, bf16[7168,128]{1,0:T(8,128)(2,1)} %up_a.1, bf16[7168,128]{1,0:T(8,128)(2,1)} %collective-permute-done.24.up_b, bf16[128,7168]{1,0:T(8,128)(2,1)} %down_a.1, ...), custom_call_target="tpu_custom_call" | custom-call | flops 3670016000 | bytes 11010048 | tf_op jit(solution)/shard_map/stage/pallas_call | solution.py:374
  169.0 0.4 collective-permute-done.27.refs_0_
  169.4 12.0 %collective-permute-done.28.refs_1_ = bf16[32,7296]{1,0:T(8,128)(2,1)S(1)} collective-permute-done((bf16[32,7296]{1,0:T(8,128)(2,1)S(1)}, bf16[32,7296]{1,0:T(8,128)(2,1)S(1)}, u32[]{:S(2)}, u32[]{:S(2)}) %collective-permute-start.28) | collective-permute-done | bytes 466976 | tf_op jit(solution)/shard_map/ppermute | solution.py:40
  181.4 2.7 %expert_part.3 = (bf16[24,7168]{1,0:T(8,128)(2,1)S(1)}, bf16[24,7168]{1,0:T(8,128)(2,1)S(1)}, bf16[8,7168]{1,0:T(8,128)(2,1)S(1)}, bf16[8,7168]{1,0:T(8,128)(2,1)S(1)}) custom-call(s32[5]{0:T(128)S(1)} %pad_add_fusion.where_ref, bf16[32,7296]{1,0:T(8,128)(2,1)S(1)} %collective-permute-done.27.refs_0_, bf16[32,7296]{1,0:T(8,128)(2,1)S(1)} %collective-permute-done.28.refs_1_, ...), custom_call_target="tpu_custom_call" | custom-call | flops 1409286144 | bytes 917504 | tf_op jit(solution)/shard_map/expert_part/pallas_call | solution.py:423
  184.0 0.4 collective-permute-start.32
  184.4 2.6 %collective-permute-start.33 = (bf16[24,7168]{1,0:T(8,128)(2,1)S(1)}, bf16[24,7168]{1,0:T(8,128)(2,1)S(1)}, u32[]{:S(2)}, u32[]{:S(2)}) collective-permute-start(bf16[24,7168]{1,0:T(8,128)(2,1)S(1)} %get-tuple-element.79), channel_id=1, source_target_pairs={{0,96},{32,64},{64,32},{96,0},{1,97},{33,65},{65,33},{97,1},{2,98}... | collective-permute-start | bytes 1032200 | tf_op jit(solution)/shard_map/ppermute | solution.py:40
  187.0 2.7 %expert_part.2 = (bf16[24,7168]{1,0:T(8,128)(2,1)S(1)}, bf16[24,7168]{1,0:T(8,128)(2,1)S(1)}, bf16[8,7168]{1,0:T(8,128)(2,1)S(1)}, bf16[8,7168]{1,0:T(8,128)(2,1)S(1)}) custom-call(s32[5]{0:T(128)S(1)} %pad_add_fusion.where_ref, bf16[32,7296]{1,0:T(8,128)(2,1)S(1)} %get-tuple-element.65.refs_0_, bf16[32,7296]{1,0:T(8,128)(2,1)S(1)} %collective-permute-done.22.refs_1_, ...), custom_call_target="tpu_custom_call" | custom-call | flops 1409286144 | bytes 917504 | tf_op jit(solution)/shard_map/expert_part/pallas_call | solution.py:423
  189.7 1.6 collective-permute-start.31
  191.3 1.2 collective-permute-start.29
  192.5 1.5 collective-permute-start.30
  193.9 4.8 %collective-permute-done.31.refs_1_ = bf16[24,7168]{1,0:T(8,128)(2,1)S(1)} collective-permute-done((bf16[24,7168]{1,0:T(8,128)(2,1)S(1)}, bf16[24,7168]{1,0:T(8,128)(2,1)S(1)}, u32[]{:S(2)}, u32[]{:S(2)}) %collective-permute-start.31) | collective-permute-done | bytes 344096 | tf_op jit(solution)/shard_map/ppermute | solution.py:40
  198.7 0.3 collect.1
  199.2 3.2 %collective-permute-start.35 = (bf16[32,3584]{1,0:T(8,128)(2,1)S(1)}, bf16[32,3584]{1,0:T(8,128)(2,1)S(1)}, u32[]{:S(2)}, u32[]{:S(2)}) collective-permute-start(bf16[32,3584]{1,0:T(8,128)(2,1)S(1)} %get-tuple-element.81), channel_id=1, source_target_pairs={{0,30},{2,0},{4,2},{6,4},{8,6},{10,8},{12,10},{14,12},{16,14},{18,... | collective-permute-start | bytes 688136 | tf_op jit(solution)/shard_map/ppermute | solution.py:44
  202.4 3.0 %collective-permute-start.26 = (bf16[8,7168]{1,0:T(8,128)(2,1)S(1)}, bf16[8,7168]{1,0:T(8,128)(2,1)S(1)}, u32[]{:S(2)}, u32[]{:S(2)}) collective-permute-start(bf16[8,7168]{1,0:T(8,128)(2,1)S(1)} %get-tuple-element.70), channel_id=1, source_target_pairs={{0,64},{32,96},{64,0},{96,32},{1,65},{33,97},{65,1},{97,33},{2,66}... | collective-permute-start | bytes 344072 | tf_op jit(solution)/shard_map/ppermute | solution.py:40
  205.4 4.1 %collective-permute-start.37 = (bf16[32,1792]{1,0:T(8,128)(2,1)S(1)}, bf16[32,1792]{1,0:T(8,128)(2,1)S(1)}, u32[]{:S(2)}, u32[]{:S(2)}) collective-permute-start(bf16[32,1792]{1,0:T(8,128)(2,1)S(1)} %get-tuple-element.83), channel_id=1, source_target_pairs={{0,28},{2,30},{4,0},{6,2},{8,4},{10,6},{12,8},{14,10},{16,12},{18,... | collective-permute-start | bytes 344072 | tf_op jit(solution)/shard_map/ppermute | solution.py:44
  209.6 2.8 %collective-permute-done.36.refs_7_ = bf16[32,1792]{1,0:T(8,128)(2,1)S(1)} collective-permute-done((bf16[32,1792]{1,0:T(8,128)(2,1)S(1)}, bf16[32,1792]{1,0:T(8,128)(2,1)S(1)}, u32[]{:S(2)}, u32[]{:S(2)}) %collective-permute-start.36) | collective-permute-done | bytes 114720 | tf_op jit(solution)/shard_map/ppermute | solution.py:44
  212.3 2.2 collective-permute-done.37.refs_8_
  214.6 0.2 merge.3
  214.9 7.7 %collective-permute-start.39 = (bf16[8,1792]{1,0:T(8,128)(2,1)S(1)}, bf16[8,1792]{1,0:T(8,128)(2,1)S(1)}, u32[]{:S(2)}, u32[]{:S(2)}) collective-permute-start(bf16[8,1792]{1,0:T(8,128)(2,1)S(1)} %get-tuple-element.88), channel_id=1, source_target_pairs={{0,24},{8,16},{16,8},{24,0},{1,25},{9,17},{17,9},{25,1},{2,26},{10... | collective-permute-start | bytes 86024 | tf_op jit(solution)/shard_map/ppermute | solution.py:48
  222.8 1.7 collective-permute-done.39.lower
  224.5 4.2 %collective-permute-start.40 = (bf16[8,3584]{1,0:T(8,128)(2,1)S(1)}, bf16[8,3584]{1,0:T(8,128)(2,1)S(1)}, u32[]{:S(2)}, u32[]{:S(2)}) collective-permute-start(bf16[8,3584]{1,0:T(8,128)(2,1)S(1)} %get-tuple-element.89), channel_id=1, source_target_pairs={{0,8},{8,0},{16,24},{24,16},{1,9},{9,1},{17,25},{25,17},{2,10},{10... | collective-permute-start | bytes 172040 | tf_op jit(solution)/shard_map/ppermute | solution.py:48
  228.8 3.4 %collective-permute-start.41 = (bf16[8,3584]{1,0:T(8,128)(2,1)S(1)}, bf16[8,3584]{1,0:T(8,128)(2,1)S(1)}, u32[]{:S(2)}, u32[]{:S(2)}) collective-permute-start(bf16[8,3584]{1,0:T(8,128)(2,1)S(1)} %get-tuple-element.90), channel_id=1, source_target_pairs={{0,24},{8,16},{16,8},{24,0},{1,25},{9,17},{17,9},{25,1},{2,26},{10... | collective-permute-start | bytes 172040 | tf_op jit(solution)/shard_map/ppermute | solution.py:48
  232.2 0.5 collective-permute-done.40.one
  232.7 4.5 %collective-permute-done.41.three = bf16[8,3584]{1,0:T(8,128)(2,1)S(1)} collective-permute-done((bf16[8,3584]{1,0:T(8,128)(2,1)S(1)}, bf16[8,3584]{1,0:T(8,128)(2,1)S(1)}, u32[]{:S(2)}, u32[]{:S(2)}) %collective-permute-start.41) | collective-permute-done | bytes 57376 | tf_op jit(solution)/shard_map/ppermute | solution.py:48
  237.3 0.7 finish.1
  (61 shorter events, 1.1 us)
Async XLA Ops:
  1.2 20.0 %collective-permute-start.11 = (bf16[32,7680]{1,0:T(8,128)(2,1)S(1)}, bf16[32,7680]{1,0:T(8,128)(2,1)S(1)}, u32[]{:S(2)}, u32[]{:S(2)}) collective-permute-start(bf16[32,7680]{1,0:T(8,128)(2,1)S(1)} %get-tuple-element.48.refs_0_), channel_id=1, source_target_pairs={{0,96},{32,64},{64,32},{96,0},{1,97},{33,65},{65,33},{97,1},{2,98}... | collective-permute-start | bytes 1474568 | tf_op jit(solution)/shard_map/ppermute | solution.py:40
  3.0 20.6 %collective-permute-start.6 = (bf16[32,7680]{1,0:T(8,128)(2,1)S(1)}, bf16[32,7680]{1,0:T(8,128)(2,1)S(1)}, u32[]{:S(2)}, u32[]{:S(2)}) collective-permute-start(bf16[32,7680]{1,0:T(8,128)(2,1)S(1)} %get-tuple-element.48.refs_0_), channel_id=1, source_target_pairs={{0,1},{1,0},{2,3},{3,2},{4,5},{5,4},{6,7},{7,6},{8,9},{9,8},{10,11... | collective-permute-start | bytes 1474568 | tf_op jit(solution)/shard_map/ppermute | solution.py:52
  3.0 30.1 %collective-permute-start = (bf16[32,7680]{1,0:T(8,128)(2,1)S(1)}, bf16[32,7680]{1,0:T(8,128)(2,1)S(1)}, u32[]{:S(2)}, u32[]{:S(2)}) collective-permute-start(bf16[32,7680]{1,0:T(8,128)(2,1)S(1)} %get-tuple-element.48.refs_0_), channel_id=1, source_target_pairs={{0,32},{32,0},{64,96},{96,64},{1,33},{33,1},{65,97},{97,65},{2,34}... | collective-permute-start | bytes 1474568 | tf_op jit(solution)/shard_map/ppermute | solution.py:40
  21.0 22.3 %collective-permute-start.8 = (bf16[32,7680]{1,0:T(8,128)(2,1)S(1)}, bf16[32,7680]{1,0:T(8,128)(2,1)S(1)}, u32[]{:S(2)}, u32[]{:S(2)}) collective-permute-start(bf16[32,7680]{1,0:T(8,128)(2,1)S(1)} %get-tuple-element.49.refs_1_), channel_id=1, source_target_pairs={{0,32},{32,0},{64,96},{96,64},{1,33},{33,1},{65,97},{97,65},{2,34}... | collective-permute-start | bytes 1474568 | tf_op jit(solution)/shard_map/ppermute | solution.py:40
  21.2 24.6 %collective-permute-start.7 = (bf16[32,7680]{1,0:T(8,128)(2,1)S(1)}, bf16[32,7680]{1,0:T(8,128)(2,1)}, u32[]{:S(2)}, u32[]{:S(2)}) collective-permute-start(bf16[32,7680]{1,0:T(8,128)(2,1)S(1)} %get-tuple-element.49.refs_1_), channel_id=1, source_target_pairs={{0,1},{1,0},{2,3},{3,2},{4,5},{5,4},{6,7},{7,6},{8,9},{9,8},{10,11... | collective-permute-start | bytes 1474568 | tf_op jit(solution)/shard_map/ppermute | solution.py:52
  21.2 37.0 %collective-permute-start.2 = (bf16[32,7680]{1,0:T(8,128)(2,1)S(1)}, bf16[32,7680]{1,0:T(8,128)(2,1)}, u32[]{:S(2)}, u32[]{:S(2)}) collective-permute-start(bf16[32,7680]{1,0:T(8,128)(2,1)S(1)} %get-tuple-element.49.refs_1_), channel_id=1, source_target_pairs={{0,96},{32,64},{64,32},{96,0},{1,97},{33,65},{65,33},{97,1},{2,98}... | collective-permute-start | bytes 1474568 | tf_op jit(solution)/shard_map/ppermute | solution.py:40
  23.6 34.9 %collective-permute-start.12 = (bf16[32,7680]{1,0:T(8,128)(2,1)S(1)}, bf16[32,7680]{1,0:T(8,128)(2,1)}, u32[]{:S(2)}, u32[]{:S(2)}) collective-permute-start(bf16[32,7680]{1,0:T(8,128)(2,1)S(1)} %collective-permute-done.11.refs_8_), channel_id=1, source_target_pairs={{0,1},{1,0},{2,3},{3,2},{4,5},{5,4},{6,7},{7,6},{8,9},{9,8},{10,11... | collective-permute-start | bytes 1474568 | tf_op jit(solution)/shard_map/ppermute | solution.py:52
  33.1 27.1 %collective-permute-start.9 = (bf16[32,7680]{1,0:T(8,128)(2,1)S(1)}, bf16[32,7680]{1,0:T(8,128)(2,1)}, u32[]{:S(2)}, u32[]{:S(2)}) collective-permute-start(bf16[32,7680]{1,0:T(8,128)(2,1)S(1)} %collective-permute-done.refs_4_), channel_id=1, source_target_pairs={{0,1},{1,0},{2,3},{3,2},{4,5},{5,4},{6,7},{7,6},{8,9},{9,8},{10,11... | collective-permute-start | bytes 1474568 | tf_op jit(solution)/shard_map/ppermute | solution.py:52
  43.3 16.9 %collective-permute-start.1 = (bf16[32,7680]{1,0:T(8,128)(2,1)S(1)}, bf16[32,7680]{1,0:T(8,128)(2,1)}, u32[]{:S(2)}, u32[]{:S(2)}) collective-permute-start(bf16[32,7680]{1,0:T(8,128)(2,1)S(1)} %collective-permute-done.refs_4_), channel_id=1, source_target_pairs={{0,96},{32,64},{64,32},{96,0},{1,97},{33,65},{65,33},{97,1},{2,98}... | collective-permute-start | bytes 1474568 | tf_op jit(solution)/shard_map/ppermute | solution.py:40
  45.8 14.9 %collective-permute-start.10 = (bf16[32,7680]{1,0:T(8,128)(2,1)S(1)}, bf16[32,7680]{1,0:T(8,128)(2,1)}, u32[]{:S(2)}, u32[]{:S(2)}) collective-permute-start(bf16[32,7680]{1,0:T(8,128)(2,1)S(1)} %collective-permute-done.8.refs_5_), channel_id=1, source_target_pairs={{0,1},{1,0},{2,3},{3,2},{4,5},{5,4},{6,7},{7,6},{8,9},{9,8},{10,11... | collective-permute-start | bytes 1474568 | tf_op jit(solution)/shard_map/ppermute | solution.py:52
  52.4 24.4 %all-to-all-start = ((bf16[16,16,512]{2,1,0:T(8,128)(2,1)}), bf16[16,16,512]{2,1,0:T(8,128)(2,1)S(1)}, u32[]{:S(2)}, u32[]{:S(2)}) async-start(bf16[16,16,512]{2,1,0:T(8,128)(2,1)} %bitcast.4), calls=%async_computation | async-start | bytes 524288 | tf_op jit(solution)/shard_map/all_to_all | solution.py:638
  58.2 2.7 %collective-permute-start.13 = (bf16[32,7680]{1,0:T(8,128)(2,1)}, bf16[32,7680]{1,0:T(8,128)(2,1)S(1)}, u32[]{:S(2)}, u32[]{:S(2)}) collective-permute-start(bf16[32,7680]{1,0:T(8,128)(2,1)} %collective-permute-done.2.refs_9_), channel_id=1, source_target_pairs={{0,1},{1,0},{2,3},{3,2},{4,5},{5,4},{6,7},{7,6},{8,9},{9,8},{10,11... | collective-permute-start | bytes 1474568 | tf_op jit(solution)/shard_map/ppermute | solution.py:52
  58.5 13.7 %collective-permute-start.3 = (bf16[32,7680]{1,0:T(8,128)(2,1)}, bf16[32,7680]{1,0:T(8,128)(2,1)}, u32[]{:S(2)}, u32[]{:S(2)}) collective-permute-start(bf16[32,7680]{1,0:T(8,128)(2,1)} %collective-permute-done.2.refs_9_), channel_id=1, source_target_pairs={{0,32},{32,0},{64,96},{96,64},{1,33},{33,1},{65,97},{97,65},{2,34}... | collective-permute-start | bytes 1474568 | tf_op jit(solution)/shard_map/ppermute | solution.py:40
  60.2 104.5 %collective-permute-start.23 = (bf16[7168,128]{1,0:T(8,128)(2,1)}, bf16[7168,128]{1,0:T(8,128)(2,1)}, u32[]{:S(2)}, u32[]{:S(2)}) collective-permute-start(bf16[7168,128]{1,0:T(8,128)(2,1)} %gate_a.1), channel_id=1, source_target_pairs={{0,1},{1,0},{2,3},{3,2},{4,5},{5,4},{6,7},{7,6},{8,9},{9,8},{10,11... | collective-permute-start | bytes 5505032 | tf_op jit(solution)/shard_map/ppermute | solution.py:52
  60.2 104.5 %collective-permute-start.24 = (bf16[7168,128]{1,0:T(8,128)(2,1)}, bf16[7168,128]{1,0:T(8,128)(2,1)}, u32[]{:S(2)}, u32[]{:S(2)}) collective-permute-start(bf16[7168,128]{1,0:T(8,128)(2,1)} %up_a.1), channel_id=1, source_target_pairs={{0,1},{1,0},{2,3},{3,2},{4,5},{5,4},{6,7},{7,6},{8,9},{9,8},{10,11... | collective-permute-start | bytes 5505032 | tf_op jit(solution)/shard_map/ppermute | solution.py:52
  60.7 104.0 %collective-permute-start.25 = (bf16[128,7168]{1,0:T(8,128)(2,1)}, bf16[128,7168]{1,0:T(8,128)(2,1)}, u32[]{:S(2)}, u32[]{:S(2)}) collective-permute-start(bf16[128,7168]{1,0:T(8,128)(2,1)} %down_a.1), channel_id=1, source_target_pairs={{0,1},{1,0},{2,3},{3,2},{4,5},{5,4},{6,7},{7,6},{8,9},{9,8},{10,11... | collective-permute-start | bytes 5505032 | tf_op jit(solution)/shard_map/ppermute | solution.py:52
  60.8 0.8 copy-start
  61.7 19.2 %collective-permute-start.4 = (bf16[32,7680]{1,0:T(8,128)(2,1)}, bf16[32,7680]{1,0:T(8,128)(2,1)}, u32[]{:S(2)}, u32[]{:S(2)}) collective-permute-start(bf16[32,7680]{1,0:T(8,128)(2,1)} %collective-permute-done.1.refs_0_), channel_id=1, source_target_pairs={{0,1},{1,0},{2,3},{3,2},{4,5},{5,4},{6,7},{7,6},{8,9},{9,8},{10,11... | collective-permute-start | bytes 1474568 | tf_op jit(solution)/shard_map/ppermute | solution.py:52
  72.2 8.6 %collective-permute-start.5 = (bf16[32,7680]{1,0:T(8,128)(2,1)}, bf16[32,7680]{1,0:T(8,128)(2,1)}, u32[]{:S(2)}, u32[]{:S(2)}) collective-permute-start(bf16[32,7680]{1,0:T(8,128)(2,1)} %collective-permute-done.3.refs_1_), channel_id=1, source_target_pairs={{0,1},{1,0},{2,3},{3,2},{4,5},{5,4},{6,7},{7,6},{8,9},{9,8},{10,11... | collective-permute-start | bytes 1474568 | tf_op jit(solution)/shard_map/ppermute | solution.py:52
  76.8 1.0 copy-start.1
  80.8 37.5 %copy-start.4 = (bf16[7168]{0:T(1024)(128)(2,1)S(1)}, bf16[7168]{0:T(1024)(128)(2,1)}, u32[]{:S(2)}) copy-start(bf16[7168]{0:T(1024)(128)(2,1)} %param.21) | copy-start | bytes 43012
  80.8 37.5 %copy-start.3 = (bf16[2,2,7168]{2,1,0:T(2,128)(2,1)S(1)}, bf16[2,2,7168]{2,1,0:T(2,128)(2,1)}, u32[]{:S(2)}) copy-start(bf16[2,2,7168]{2,1,0:T(2,128)(2,1)} %param.18) | copy-start | bytes 172036
  83.2 39.5 %copy-start.5 = (s32[2,2,8]{2,1,0:T(2,128)S(1)}, s32[2,2,8]{2,1,0:T(2,128)}, u32[]{:S(2)}) copy-start(s32[2,2,8]{2,1,0:T(2,128)} %param.23) | copy-start | bytes 388
  83.3 39.5 %copy-start.6 = (s32[2,2,8]{2,1,0:T(2,128)S(1)}, s32[2,2,8]{2,1,0:T(2,128)}, u32[]{:S(2)}) copy-start(s32[2,2,8]{2,1,0:T(2,128)} %param.24) | copy-start | bytes 388
  83.3 39.5 %copy-start.2 = (bf16[7168,16]{0,1:T(8,128)(2,1)S(1)}, bf16[7168,16]{0,1:T(8,128)(2,1)}, u32[]{:S(2)}) copy-start(bf16[7168,16]{0,1:T(8,128)(2,1)} %param.22) | copy-start | bytes 688132
  83.3 7.0 %collective-permute-start.16 = (bf16[32,1792]{1,0:T(8,128)(2,1)S(1)}, bf16[32,1792]{1,0:T(8,128)(2,1)S(1)}, u32[]{:S(2)}, u32[]{:S(2)}) collective-permute-start(bf16[32,1792]{1,0:T(8,128)(2,1)S(1)} %get-tuple-element.53), channel_id=1, source_target_pairs={{0,4},{2,6},{4,8},{6,10},{8,12},{10,14},{12,16},{14,18},{16,20},{1... | collective-permute-start | bytes 344072 | tf_op jit(solution)/shard_map/ppermute | solution.py:44
  83.9 9.4 %collective-permute-start.17 = (bf16[32,1792]{1,0:T(8,128)(2,1)S(1)}, bf16[32,1792]{1,0:T(8,128)(2,1)S(1)}, u32[]{:S(2)}, u32[]{:S(2)}) collective-permute-start(bf16[32,1792]{1,0:T(8,128)(2,1)S(1)} %get-tuple-element.54), channel_id=1, source_target_pairs={{0,28},{2,30},{4,0},{6,2},{8,4},{10,6},{12,8},{14,10},{16,12},{18,... | collective-permute-start | bytes 344072 | tf_op jit(solution)/shard_map/ppermute | solution.py:44
  90.3 8.0 %collective-permute-start.14 = (bf16[32,3584]{1,0:T(8,128)(2,1)S(1)}, bf16[32,3584]{1,0:T(8,128)(2,1)S(1)}, u32[]{:S(2)}, u32[]{:S(2)}) collective-permute-start(bf16[32,3584]{1,0:T(8,128)(2,1)S(1)} %get-tuple-element.51), channel_id=1, source_target_pairs={{0,2},{2,4},{4,6},{6,8},{8,10},{10,12},{12,14},{14,16},{16,18},{18... | collective-permute-start | bytes 688136 | tf_op jit(solution)/shard_map/ppermute | solution.py:44
  93.3 6.4 %collective-permute-start.15 = (bf16[32,3584]{1,0:T(8,128)(2,1)S(1)}, bf16[32,3584]{1,0:T(8,128)(2,1)S(1)}, u32[]{:S(2)}, u32[]{:S(2)}) collective-permute-start(bf16[32,3584]{1,0:T(8,128)(2,1)S(1)} %get-tuple-element.52), channel_id=1, source_target_pairs={{0,30},{2,0},{4,2},{6,4},{8,6},{10,8},{12,10},{14,12},{16,14},{18,... | collective-permute-start | bytes 688136 | tf_op jit(solution)/shard_map/ppermute | solution.py:44
  99.9 8.2 %collective-permute-start.18 = (bf16[8,1792]{1,0:T(8,128)(2,1)S(1)}, bf16[8,1792]{1,0:T(8,128)(2,1)S(1)}, u32[]{:S(2)}, u32[]{:S(2)}) collective-permute-start(bf16[8,1792]{1,0:T(8,128)(2,1)S(1)} %get-tuple-element.58), channel_id=1, source_target_pairs={{0,8},{8,0},{16,24},{24,16},{1,9},{9,1},{17,25},{25,17},{2,10},{10... | collective-permute-start | bytes 86024 | tf_op jit(solution)/shard_map/ppermute | solution.py:48
  104.1 7.8 %collective-permute-start.19 = (bf16[8,1792]{1,0:T(8,128)(2,1)S(1)}, bf16[8,1792]{1,0:T(8,128)(2,1)S(1)}, u32[]{:S(2)}, u32[]{:S(2)}) collective-permute-start(bf16[8,1792]{1,0:T(8,128)(2,1)S(1)} %get-tuple-element.59), channel_id=1, source_target_pairs={{0,24},{8,16},{16,8},{24,0},{1,25},{9,17},{17,9},{25,1},{2,26},{10... | collective-permute-start | bytes 86024 | tf_op jit(solution)/shard_map/ppermute | solution.py:48
  111.9 8.2 %collective-permute-start.20 = (bf16[8,3584]{1,0:T(8,128)(2,1)S(1)}, bf16[8,3584]{1,0:T(8,128)(2,1)S(1)}, u32[]{:S(2)}, u32[]{:S(2)}) collective-permute-start(bf16[8,3584]{1,0:T(8,128)(2,1)S(1)} %get-tuple-element.60), channel_id=1, source_target_pairs={{0,8},{8,0},{16,24},{24,16},{1,9},{9,1},{17,25},{25,17},{2,10},{10... | collective-permute-start | bytes 172040 | tf_op jit(solution)/shard_map/ppermute | solution.py:48
  114.1 8.7 %collective-permute-start.21 = (bf16[8,3584]{1,0:T(8,128)(2,1)S(1)}, bf16[8,3584]{1,0:T(8,128)(2,1)S(1)}, u32[]{:S(2)}, u32[]{:S(2)}) collective-permute-start(bf16[8,3584]{1,0:T(8,128)(2,1)S(1)} %get-tuple-element.61), channel_id=1, source_target_pairs={{0,24},{8,16},{16,8},{24,0},{1,25},{9,17},{17,9},{25,1},{2,26},{10... | collective-permute-start | bytes 172040 | tf_op jit(solution)/shard_map/ppermute | solution.py:48
  160.5 8.9 %collective-permute-start.27 = (bf16[32,7296]{1,0:T(8,128)(2,1)S(1)}, bf16[32,7296]{1,0:T(8,128)(2,1)S(1)}, u32[]{:S(2)}, u32[]{:S(2)}) collective-permute-start(bf16[32,7296]{1,0:T(8,128)(2,1)S(1)} %get-tuple-element.71), channel_id=1, source_target_pairs={{0,32},{32,0},{64,96},{96,64},{1,33},{33,1},{65,97},{97,65},{2,34}... | collective-permute-start | bytes 1400840 | tf_op jit(solution)/shard_map/ppermute | solution.py:40
  162.3 19.1 %collective-permute-start.28 = (bf16[32,7296]{1,0:T(8,128)(2,1)S(1)}, bf16[32,7296]{1,0:T(8,128)(2,1)S(1)}, u32[]{:S(2)}, u32[]{:S(2)}) collective-permute-start(bf16[32,7296]{1,0:T(8,128)(2,1)S(1)} %get-tuple-element.72), channel_id=1, source_target_pairs={{0,96},{32,64},{64,32},{96,0},{1,97},{33,65},{65,33},{97,1},{2,98}... | collective-permute-start | bytes 1400840 | tf_op jit(solution)/shard_map/ppermute | solution.py:40
  164.7 22.3 %collective-permute-start.22 = (bf16[32,7296]{1,0:T(8,128)(2,1)S(1)}, bf16[32,7296]{1,0:T(8,128)(2,1)S(1)}, u32[]{:S(2)}, u32[]{:S(2)}) collective-permute-start(bf16[32,7296]{1,0:T(8,128)(2,1)S(1)} %get-tuple-element.66), channel_id=1, source_target_pairs={{0,64},{32,96},{64,0},{96,32},{1,65},{33,97},{65,1},{97,33},{2,66}... | collective-permute-start | bytes 1400840 | tf_op jit(solution)/shard_map/ppermute | solution.py:40
  184.0 9.9 %collective-permute-start.32 = (bf16[24,7168]{1,0:T(8,128)(2,1)S(1)}, bf16[24,7168]{1,0:T(8,128)(2,1)S(1)}, u32[]{:S(2)}, u32[]{:S(2)}) collective-permute-start(bf16[24,7168]{1,0:T(8,128)(2,1)S(1)} %get-tuple-element.78), channel_id=1, source_target_pairs={{0,32},{32,0},{64,96},{96,64},{1,33},{33,1},{65,97},{97,65},{2,34}... | collective-permute-start | bytes 1032200 | tf_op jit(solution)/shard_map/ppermute | solution.py:40
  184.4 9.5 %collective-permute-start.33 = (bf16[24,7168]{1,0:T(8,128)(2,1)S(1)}, bf16[24,7168]{1,0:T(8,128)(2,1)S(1)}, u32[]{:S(2)}, u32[]{:S(2)}) collective-permute-start(bf16[24,7168]{1,0:T(8,128)(2,1)S(1)} %get-tuple-element.79), channel_id=1, source_target_pairs={{0,96},{32,64},{64,32},{96,0},{1,97},{33,65},{65,33},{97,1},{2,98}... | collective-permute-start | bytes 1032200 | tf_op jit(solution)/shard_map/ppermute | solution.py:40
  189.7 9.0 %collective-permute-start.31 = (bf16[24,7168]{1,0:T(8,128)(2,1)S(1)}, bf16[24,7168]{1,0:T(8,128)(2,1)S(1)}, u32[]{:S(2)}, u32[]{:S(2)}) collective-permute-start(bf16[24,7168]{1,0:T(8,128)(2,1)S(1)} %get-tuple-element.77), channel_id=1, source_target_pairs={{0,64},{32,96},{64,0},{96,32},{1,65},{33,97},{65,1},{97,33},{2,66}... | collective-permute-start | bytes 1032200 | tf_op jit(solution)/shard_map/ppermute | solution.py:40
  191.3 14.1 %collective-permute-start.29 = (bf16[8,7168]{1,0:T(8,128)(2,1)S(1)}, bf16[8,7168]{1,0:T(8,128)(2,1)S(1)}, u32[]{:S(2)}, u32[]{:S(2)}) collective-permute-start(bf16[8,7168]{1,0:T(8,128)(2,1)S(1)} %get-tuple-element.73), channel_id=1, source_target_pairs={{0,32},{32,0},{64,96},{96,64},{1,33},{33,1},{65,97},{97,65},{2,34}... | collective-permute-start | bytes 344072 | tf_op jit(solution)/shard_map/ppermute | solution.py:40
  192.5 13.0 %collective-permute-start.30 = (bf16[8,7168]{1,0:T(8,128)(2,1)S(1)}, bf16[8,7168]{1,0:T(8,128)(2,1)S(1)}, u32[]{:S(2)}, u32[]{:S(2)}) collective-permute-start(bf16[8,7168]{1,0:T(8,128)(2,1)S(1)} %get-tuple-element.74), channel_id=1, source_target_pairs={{0,96},{32,64},{64,32},{96,0},{1,97},{33,65},{65,33},{97,1},{2,98}... | collective-permute-start | bytes 344072 | tf_op jit(solution)/shard_map/ppermute | solution.py:40
  199.0 15.5 %collective-permute-start.34 = (bf16[32,3584]{1,0:T(8,128)(2,1)S(1)}, bf16[32,3584]{1,0:T(8,128)(2,1)S(1)}, u32[]{:S(2)}, u32[]{:S(2)}) collective-permute-start(bf16[32,3584]{1,0:T(8,128)(2,1)S(1)} %get-tuple-element.80), channel_id=1, source_target_pairs={{0,2},{2,4},{4,6},{6,8},{8,10},{10,12},{12,14},{14,16},{16,18},{18... | collective-permute-start | bytes 688136 | tf_op jit(solution)/shard_map/ppermute | solution.py:44
  199.2 15.4 %collective-permute-start.35 = (bf16[32,3584]{1,0:T(8,128)(2,1)S(1)}, bf16[32,3584]{1,0:T(8,128)(2,1)S(1)}, u32[]{:S(2)}, u32[]{:S(2)}) collective-permute-start(bf16[32,3584]{1,0:T(8,128)(2,1)S(1)} %get-tuple-element.81), channel_id=1, source_target_pairs={{0,30},{2,0},{4,2},{6,4},{8,6},{10,8},{12,10},{14,12},{16,14},{18,... | collective-permute-start | bytes 688136 | tf_op jit(solution)/shard_map/ppermute | solution.py:44
  202.4 7.2 %collective-permute-start.26 = (bf16[8,7168]{1,0:T(8,128)(2,1)S(1)}, bf16[8,7168]{1,0:T(8,128)(2,1)S(1)}, u32[]{:S(2)}, u32[]{:S(2)}) collective-permute-start(bf16[8,7168]{1,0:T(8,128)(2,1)S(1)} %get-tuple-element.70), channel_id=1, source_target_pairs={{0,64},{32,96},{64,0},{96,32},{1,65},{33,97},{65,1},{97,33},{2,66}... | collective-permute-start | bytes 344072 | tf_op jit(solution)/shard_map/ppermute | solution.py:40
  205.4 6.9 %collective-permute-start.36 = (bf16[32,1792]{1,0:T(8,128)(2,1)S(1)}, bf16[32,1792]{1,0:T(8,128)(2,1)S(1)}, u32[]{:S(2)}, u32[]{:S(2)}) collective-permute-start(bf16[32,1792]{1,0:T(8,128)(2,1)S(1)} %get-tuple-element.82), channel_id=1, source_target_pairs={{0,4},{2,6},{4,8},{6,10},{8,12},{10,14},{12,16},{14,18},{16,20},{1... | collective-permute-start | bytes 344072 | tf_op jit(solution)/shard_map/ppermute | solution.py:44
  205.4 9.1 %collective-permute-start.37 = (bf16[32,1792]{1,0:T(8,128)(2,1)S(1)}, bf16[32,1792]{1,0:T(8,128)(2,1)S(1)}, u32[]{:S(2)}, u32[]{:S(2)}) collective-permute-start(bf16[32,1792]{1,0:T(8,128)(2,1)S(1)} %get-tuple-element.83), channel_id=1, source_target_pairs={{0,28},{2,30},{4,0},{6,2},{8,4},{10,6},{12,8},{14,10},{16,12},{18,... | collective-permute-start | bytes 344072 | tf_op jit(solution)/shard_map/ppermute | solution.py:44
  214.8 8.0 %collective-permute-start.38 = (bf16[8,1792]{1,0:T(8,128)(2,1)S(1)}, bf16[8,1792]{1,0:T(8,128)(2,1)S(1)}, u32[]{:S(2)}, u32[]{:S(2)}) collective-permute-start(bf16[8,1792]{1,0:T(8,128)(2,1)S(1)} %get-tuple-element.87), channel_id=1, source_target_pairs={{0,8},{8,0},{16,24},{24,16},{1,9},{9,1},{17,25},{25,17},{2,10},{10... | collective-permute-start | bytes 86024 | tf_op jit(solution)/shard_map/ppermute | solution.py:48
  214.9 9.6 %collective-permute-start.39 = (bf16[8,1792]{1,0:T(8,128)(2,1)S(1)}, bf16[8,1792]{1,0:T(8,128)(2,1)S(1)}, u32[]{:S(2)}, u32[]{:S(2)}) collective-permute-start(bf16[8,1792]{1,0:T(8,128)(2,1)S(1)} %get-tuple-element.88), channel_id=1, source_target_pairs={{0,24},{8,16},{16,8},{24,0},{1,25},{9,17},{17,9},{25,1},{2,26},{10... | collective-permute-start | bytes 86024 | tf_op jit(solution)/shard_map/ppermute | solution.py:48
  224.5 8.2 %collective-permute-start.40 = (bf16[8,3584]{1,0:T(8,128)(2,1)S(1)}, bf16[8,3584]{1,0:T(8,128)(2,1)S(1)}, u32[]{:S(2)}, u32[]{:S(2)}) collective-permute-start(bf16[8,3584]{1,0:T(8,128)(2,1)S(1)} %get-tuple-element.89), channel_id=1, source_target_pairs={{0,8},{8,0},{16,24},{24,16},{1,9},{9,1},{17,25},{25,17},{2,10},{10... | collective-permute-start | bytes 172040 | tf_op jit(solution)/shard_map/ppermute | solution.py:48
  228.8 8.5 %collective-permute-start.41 = (bf16[8,3584]{1,0:T(8,128)(2,1)S(1)}, bf16[8,3584]{1,0:T(8,128)(2,1)S(1)}, u32[]{:S(2)}, u32[]{:S(2)}) collective-permute-start(bf16[8,3584]{1,0:T(8,128)(2,1)S(1)} %get-tuple-element.90), channel_id=1, source_target_pairs={{0,24},{8,16},{16,8},{24,0},{1,25},{9,17},{17,9},{25,1},{2,26},{10... | collective-permute-start | bytes 172040 | tf_op jit(solution)/shard_map/ppermute | solution.py:48

commit v4 on v1

--- a/solution.py
+++ b/solution.py
@@ -60,11 +60,15 @@
     return jnp.where(mask, 1.0, 0.0).astype(bf16)
 
 
-COLUMNS = (0, 1, 3, 2)
-
-
 def column(index, x):
     return x ^ jnp.where(index == 2, 3, jnp.where(index == 3, 2, index))
+
+
+EXPERT_COLUMNS = (0, 2, 1, 3)
+
+
+def expert_column(index, x):
+    return x ^ jnp.where(index == 1, 2, jnp.where(index == 2, 1, index))
 
 
 STEPS = (0, 1, RING - 1, 2, RING - 2)
@@ -294,7 +298,7 @@
     table = tokens[:, pl.ds(half, EXTRA)]
     shape = (nx * CAP, EXTRA)
     row, place = iota(shape, 0), iota(shape, 1)
-    expert = FAR * column(row // CAP, where_ref[0]) + where_ref[1]
+    expert = FAR * expert_column(row // CAP, where_ref[0]) + where_ref[1]
     hot = one_hot(place == lax.rem(row, CAP) * EXPERTS + expert)
     got = lax.dot_general(hot, table, NT, preferred_element_type=f32)
     shape = (SLOTS, count)
@@ -631,13 +635,16 @@
 
     ring = lax.all_gather(payload, ZAX, axis=0, tiled=True)
     *sent, early, late = dispatch(where, nx, ring, tok)
-    got = [swap_x(sent[i], COLUMNS[i]) for i in range(1, nx)]
-    done = expert_part(where, (sent[0], *got[: nx - 2]), weights)
-    done = [list(done[: nx - 1]), list(done[nx - 1 :])]
-    for rows, last in zip(done, expert_part(where, got[nx - 2 :], weights)):
-        rows.append(last)
-    first = [done[0][0]] + [swap_x(done[0][i], COLUMNS[i]) for i in range(1, nx)]
-    second = [done[1][0]] + [swap_x(done[1][i], COLUMNS[i]) for i in range(1, nx)]
+    far = swap_x(sent[1], EXPERT_COLUMNS[1])
+    near = [swap_x(sent[i], EXPERT_COLUMNS[i]) for i in range(2, nx)]
+    done = [[], []]
+    for groups in ((sent[0], far), tuple(near)):
+        rows = expert_part(where, groups, weights)
+        done[0] += rows[: len(groups)]
+        done[1] += rows[len(groups) :]
+    first = [done[0][0], swap_x(done[0][1], EXPERT_COLUMNS[1])]
+    first += [swap_x(done[0][i], EXPERT_COLUMNS[i]) for i in range(2, nx)]
+    second = [done[1][0]] + [swap_x(done[1][i], EXPERT_COLUMNS[i]) for i in range(1, nx)]
     added = reduce_z((late, *second), *collect(early, first))
     return finish(hidden, added, resid.shape)
 

time: 232 us -> 230 us (level)
  the two profiles are of different devices: /device:TPU:34 before, /device:TPU:164 now
where the time goes in v4:
time: 230 us; the launch traced here: 228 us
  starting transfers between devices  85.5 us (37%)
  waiting for transfers between devices  80.6 us (35%)
  blocking collectives  33.3 us (14%)
  Pallas kernels  25.4 us (11%)
    ppermute x15, waiting for transfers between devices, swap_x(): lax.ppermute(a, 'x', [(i, i ^ bits) for i in range(lax.axis_size('x'))])  46.1 us
    all_gather x1, blocking collectives, layer(): ring = lax.all_gather(payload, ZAX, axis=0, tiled=True)  33.3 us
    ppermute x6, starting transfers between devices, swap_far(): return lax.ppermute(a, 'zb', [(i, i ^ bits) for i in range(FAR)])  25.9 us
    ppermute x15, starting transfers between devices, swap_x(): lax.ppermute(a, 'x', [(i, i ^ bits) for i in range(lax.axis_size('x'))])  23 us
    all_to_all x1, starting transfers between devices, layer(): lax.all_to_all(outgoing.reshape(RING, nx * tok, LAT), ZAX, split_axis=0,...  22.9 us
    ppermute x6, waiting for transfers between devices, swap_far(): return lax.ppermute(a, 'zb', [(i, i ^ bits) for i in range(FAR)])  16.4 us
    ppermute x8, waiting for transfers between devices, shift_z(): return lax.ppermute(a, ZAX, [(i, (i + step) % RING) for i in range(RING)])  13.9 us
    ppermute x8, starting transfers between devices, shift_z(): return lax.ppermute(a, ZAX, [(i, (i + step) % RING) for i in range(RING)])  12.5 us
  transfers between devices with their start and end apart: 41, of which 16 were waited for; matrix products, arithmetic and copies ran while one was open for 0% of the time, Pallas kernels for 10%

profile of v4, /device:TPU:164, one launch (start us, length us, event | category | flops | bytes accessed | tf_op | source)
XLA Modules:
  0.0 227.8 jit_solution(17266374532154918171)
XLA Ops:
  0.0 1.2 pack.1
  1.2 0.5 collective-permute-start.11
  1.7 1.2 collective-permute-start
  3.0 0.8 collective-permute-start.8
  3.8 10.6 %collective-permute-done.11.refs_8_ = bf16[32,7680]{1,0:T(8,128)(2,1)S(1)} collective-permute-done((bf16[32,7680]{1,0:T(8,128)(2,1)S(1)}, bf16[32,7680]{1,0:T(8,128)(2,1)S(1)}, u32[]{:S(2)}, u32[]{:S(2)}) %collective-permute-start.11) | collective-permute-done | bytes 491552 | tf_op jit(solution)/shard_map/ppermute | solution.py:40
  14.4 0.4 collective-permute-start.2
  14.8 1.1 collective-permute-done.refs_4_
  15.8 10.1 %collective-permute-done.8.refs_5_ = bf16[32,7680]{1,0:T(8,128)(2,1)S(1)} collective-permute-done((bf16[32,7680]{1,0:T(8,128)(2,1)S(1)}, bf16[32,7680]{1,0:T(8,128)(2,1)S(1)}, u32[]{:S(2)}, u32[]{:S(2)}) %collective-permute-start.8) | collective-permute-done | bytes 491552 | tf_op jit(solution)/shard_map/ppermute | solution.py:40
  25.9 1.8 collective-permute-start.1
  27.7 0.7 pad_add_fusion.where_ref
  28.5 5.9 %context_rows.1 = bf16[256,512]{1,0:T(8,128)(2,1)} custom-call(s32[5]{0:T(128)S(1)} %pad_add_fusion.where_ref, bf16[2,576,2048]{2,1,0:T(8,128)(2,1)} %bitcast.20, bf16[2,2,64,576]{3,2,1,0:T(8,128)(2,1)} %queries.1, bf16[2,2,576]{2,1,0:T(2,128)(2,1)} %new.1), custom_call_target="tpu_custom_call" | custom-call | flops 1140850688 | bytes 4718592 | tf_op jit(solution)/shard_map/context_rows/pallas_call | solution.py:170
  34.4 22.9 %all-to-all-start = ((bf16[16,16,512]{2,1,0:T(8,128)(2,1)}), bf16[16,16,512]{2,1,0:T(8,128)(2,1)S(1)}, u32[]{:S(2)}, u32[]{:S(2)}) async-start(bf16[16,16,512]{2,1,0:T(8,128)(2,1)} %bitcast.4), calls=%async_computation | async-start | bytes 524288 | tf_op jit(solution)/shard_map/all_to_all | solution.py:612
  57.3 0.1 collective-permute-start.13
  57.5 2.5 %collective-permute-start.3 = (bf16[32,7680]{1,0:T(8,128)(2,1)}, bf16[32,7680]{1,0:T(8,128)(2,1)}, u32[]{:S(2)}, u32[]{:S(2)}) collective-permute-start(bf16[32,7680]{1,0:T(8,128)(2,1)} %collective-permute-done.2.refs_9_), channel_id=1, source_target_pairs={{0,32},{32,0},{64,96},{96,64},{1,33},{33,1},{65,97},{97,65},{2,34}... | collective-permute-start | bytes 1474568 | tf_op jit(solution)/shard_map/ppermute | solution.py:40
  60.0 0.4 collective-permute-start.23
  60.4 0.1 collective-permute-start.24
  60.6 0.8 copy-done
  61.4 0.4 collective-permute-start.4
  61.8 10.2 %collective-permute-done.3.refs_1_ = bf16[32,7680]{1,0:T(8,128)(2,1)} collective-permute-done((bf16[32,7680]{1,0:T(8,128)(2,1)}, bf16[32,7680]{1,0:T(8,128)(2,1)}, u32[]{:S(2)}, u32[]{:S(2)}) %collective-permute-start.3) | collective-permute-done | bytes 491552 | tf_op jit(solution)/shard_map/ppermute | solution.py:40
  72.0 4.1 %all-to-all-done = bf16[16,16,512]{2,1,0:T(8,128)(2,1)S(1)} async-done(((bf16[16,16,512]{2,1,0:T(8,128)(2,1)}), bf16[16,16,512]{2,1,0:T(8,128)(2,1)S(1)}, u32[]{:S(2)}, u32[]{:S(2)}) %all-to-all-start) | async-done | bytes 262176 | tf_op jit(solution)/shard_map/all_to_all | solution.py:612
  76.0 1.0 copy-done.1
  77.1 3.0 %attend_part.2.refs_4_ = f32[128,3584]{1,0:T(8,128)S(1)} custom-call(s32[5]{0:T(128)S(1)} %pad_add_fusion.where_ref, bf16[256,512]{1,0:T(8,128)(2,1)S(1)} %bitcast.15, bf16[32,7680]{1,0:T(8,128)(2,1)S(1)} %get-tuple-element.42.refs_0_, bf16[32,7680]{1,0:T(8,128)(2,1)S(1)} %get-tuple-element.43.refs_1_, bf16[32,7680]{1,0:T(8,128)(2,1)S(1)} %collective-permute-done.6.refs_2_, ...), custom_call_target="tpu_custom_call" | custom-call | flops 1409286144 | bytes 5505024 | tf_op jit(solution)/shard_map/attend_part/pallas_call | solution.py:280
  80.2 2.4 %attend_part.3 = (f32[32,3584]{1,0:T(8,128)S(1)}, bf16[32,3584]{1,0:T(8,128)(2,1)S(1)}, bf16[32,3584]{1,0:T(8,128)(2,1)S(1)}, bf16[32,1792]{1,0:T(8,128)(2,1)S(1)}, bf16[32,1792]{1,0:T(8,128)(2,1)S(1)}) custom-call(s32[5]{0:T(128)S(1)} %pad_add_fusion.where_ref, bf16[256,512]{1,0:T(8,128)(2,1)S(1)} %bitcast.16, ...), custom_call_target="tpu_custom_call" | custom-call | flops 469762048 | bytes 1835008 | tf_op jit(solution)/shard_map/attend_part/pallas_call | solution.py:280
  82.6 2.3 %collective-permute-start.16 = (bf16[32,1792]{1,0:T(8,128)(2,1)S(1)}, bf16[32,1792]{1,0:T(8,128)(2,1)S(1)}, u32[]{:S(2)}, u32[]{:S(2)}) collective-permute-start(bf16[32,1792]{1,0:T(8,128)(2,1)S(1)} %get-tuple-element.47), channel_id=1, source_target_pairs={{0,4},{2,6},{4,8},{6,10},{8,12},{10,14},{12,16},{14,18},{16,20},{1... | collective-permute-start | bytes 344072 | tf_op jit(solution)/shard_map/ppermute | solution.py:44
  84.9 1.9 collective-permute-start.17
  86.8 4.0 %collective-permute-done.16.refs_3_ = bf16[32,1792]{1,0:T(8,128)(2,1)S(1)} collective-permute-done((bf16[32,1792]{1,0:T(8,128)(2,1)S(1)}, bf16[32,1792]{1,0:T(8,128)(2,1)S(1)}, u32[]{:S(2)}, u32[]{:S(2)}) %collective-permute-start.16) | collective-permute-done | bytes 114720 | tf_op jit(solution)/shard_map/ppermute | solution.py:44
  90.8 2.0 collective-permute-start.15
  92.8 4.7 %collective-permute-done.14.refs_1_ = bf16[32,3584]{1,0:T(8,128)(2,1)S(1)} collective-permute-done((bf16[32,3584]{1,0:T(8,128)(2,1)S(1)}, bf16[32,3584]{1,0:T(8,128)(2,1)S(1)}, u32[]{:S(2)}, u32[]{:S(2)}) %collective-permute-start.14) | collective-permute-done | bytes 229408 | tf_op jit(solution)/shard_map/ppermute | solution.py:44
  97.6 5.8 %collective-permute-start.18 = (bf16[8,3584]{1,0:T(8,128)(2,1)S(1)}, bf16[8,3584]{1,0:T(8,128)(2,1)S(1)}, u32[]{:S(2)}, u32[]{:S(2)}) collective-permute-start(bf16[8,3584]{1,0:T(8,128)(2,1)S(1)} %get-tuple-element.50), channel_id=1, source_target_pairs={{0,8},{8,0},{16,24},{24,16},{1,9},{9,1},{17,25},{25,17},{2,10},{10... | collective-permute-start | bytes 172040 | tf_op jit(solution)/shard_map/ppermute | solution.py:48
  103.4 4.6 %collective-permute-start.19 = (bf16[8,3584]{1,0:T(8,128)(2,1)S(1)}, bf16[8,3584]{1,0:T(8,128)(2,1)S(1)}, u32[]{:S(2)}, u32[]{:S(2)}) collective-permute-start(bf16[8,3584]{1,0:T(8,128)(2,1)S(1)} %get-tuple-element.51), channel_id=1, source_target_pairs={{0,16},{8,24},{16,0},{24,8},{1,17},{9,25},{17,1},{25,9},{2,18},{10... | collective-permute-start | bytes 172040 | tf_op jit(solution)/shard_map/ppermute | solution.py:48
  108.0 2.8 %collective-permute-start.20 = (bf16[8,3584]{1,0:T(8,128)(2,1)S(1)}, bf16[8,3584]{1,0:T(8,128)(2,1)S(1)}, u32[]{:S(2)}, u32[]{:S(2)}) collective-permute-start(bf16[8,3584]{1,0:T(8,128)(2,1)S(1)} %get-tuple-element.52), channel_id=1, source_target_pairs={{0,24},{8,16},{16,8},{24,0},{1,25},{9,17},{17,9},{25,1},{2,26},{10... | collective-permute-start | bytes 172040 | tf_op jit(solution)/shard_map/ppermute | solution.py:48
  111.0 8.1 %collective-permute-done.19.two = bf16[8,3584]{1,0:T(8,128)(2,1)S(1)} collective-permute-done((bf16[8,3584]{1,0:T(8,128)(2,1)S(1)}, bf16[8,3584]{1,0:T(8,128)(2,1)S(1)}, u32[]{:S(2)}, u32[]{:S(2)}) %collective-permute-start.19) | collective-permute-done | bytes 57376 | tf_op jit(solution)/shard_map/ppermute | solution.py:48
  119.2 0.6 route.1
  119.8 33.3 %all_gather.3.tokens = bf16[128,3712]{1,0:T(8,128)(2,1)S(1)} all-gather(bf16[8,3712]{1,0:T(8,128)(2,1)S(1)} %get-tuple-element.54), channel_id=1, replica_groups=mesh['rep'=2,'x'=4,'zb'=4,'j'=4,'c'=2] {'zb','j'}, dimensions={0}, use_global_device_ids=true | all-gather | bytes 1009664 | tf_op jit(solution)/shard_map/all_gather | solution.py:636
  153.2 1.4 dispatch.1
  154.5 5.4 %collective-permute-start.26 = (bf16[32,7296]{1,0:T(8,128)(2,1)S(1)}, bf16[32,7296]{1,0:T(8,128)(2,1)S(1)}, u32[]{:S(2)}, u32[]{:S(2)}) collective-permute-start(bf16[32,7296]{1,0:T(8,128)(2,1)S(1)} %get-tuple-element.62), channel_id=1, source_target_pairs={{0,32},{32,0},{64,96},{96,64},{1,33},{33,1},{65,97},{97,65},{2,34}... | collective-permute-start | bytes 1400840 | tf_op jit(solution)/shard_map/ppermute | solution.py:40
  160.0 2.2 collective-permute-start.21
  162.2 4.2 %stage.1 = (bf16[7168,512]{1,0:T(8,128)(2,1)S(1)}, bf16[256,7168]{1,0:T(8,128)(2,1)S(1)}) custom-call(bf16[7168,128]{1,0:T(8,128)(2,1)} %gate_a.1, bf16[7168,128]{1,0:T(8,128)(2,1)} %collective-permute-done.22.gate_b, bf16[7168,128]{1,0:T(8,128)(2,1)} %up_a.1, bf16[7168,128]{1,0:T(8,128)(2,1)} %collective-permute-done.23.up_b, bf16[128,7168]{1,0:T(8,128)(2,1)} %down_a.1, ...), custom_call_target="tpu_custom_call" | custom-call | flops 3670016000 | bytes 11010048 | tf_op jit(solution)/shard_map/stage/pallas_call | solution.py:374
  166.4 0.8 collective-permute-done.26.refs_0_
  167.3 7.5 %collective-permute-done.27.refs_1_ = bf16[32,7296]{1,0:T(8,128)(2,1)S(1)} collective-permute-done((bf16[32,7296]{1,0:T(8,128)(2,1)S(1)}, bf16[32,7296]{1,0:T(8,128)(2,1)S(1)}, u32[]{:S(2)}, u32[]{:S(2)}) %collective-permute-start.27) | collective-permute-done | bytes 466976 | tf_op jit(solution)/shard_map/ppermute | solution.py:40
  174.7 2.7 %expert_part.3 = (bf16[24,7168]{1,0:T(8,128)(2,1)S(1)}, bf16[24,7168]{1,0:T(8,128)(2,1)S(1)}, bf16[8,7168]{1,0:T(8,128)(2,1)S(1)}, bf16[8,7168]{1,0:T(8,128)(2,1)S(1)}) custom-call(s32[5]{0:T(128)S(1)} %pad_add_fusion.where_ref, bf16[32,7296]{1,0:T(8,128)(2,1)S(1)} %collective-permute-done.26.refs_0_, bf16[32,7296]{1,0:T(8,128)(2,1)S(1)} %collective-permute-done.27.refs_1_, ...), custom_call_target="tpu_custom_call" | custom-call | flops 1409286144 | bytes 917504 | tf_op jit(solution)/shard_map/expert_part/pallas_call | solution.py:423
  177.4 0.1 collective-permute-start.31
  177.6 0.4 collective-permute-start.32
  177.9 2.7 %expert_part.2 = (bf16[24,7168]{1,0:T(8,128)(2,1)S(1)}, bf16[24,7168]{1,0:T(8,128)(2,1)S(1)}, bf16[8,7168]{1,0:T(8,128)(2,1)S(1)}, bf16[8,7168]{1,0:T(8,128)(2,1)S(1)}) custom-call(s32[5]{0:T(128)S(1)} %pad_add_fusion.where_ref, bf16[32,7296]{1,0:T(8,128)(2,1)S(1)} %get-tuple-element.56.refs_0_, bf16[32,7296]{1,0:T(8,128)(2,1)S(1)} %collective-permute-done.21.refs_1_, ...), custom_call_target="tpu_custom_call" | custom-call | flops 1409286144 | bytes 917504 | tf_op jit(solution)/shard_map/expert_part/pallas_call | solution.py:423
  180.6 3.8 %collective-permute-start.30 = (bf16[24,7168]{1,0:T(8,128)(2,1)S(1)}, bf16[24,7168]{1,0:T(8,128)(2,1)S(1)}, u32[]{:S(2)}, u32[]{:S(2)}) collective-permute-start(bf16[24,7168]{1,0:T(8,128)(2,1)S(1)} %get-tuple-element.68), channel_id=1, source_target_pairs={{0,64},{32,96},{64,0},{96,32},{1,65},{33,97},{65,1},{97,33},{2,66}... | collective-permute-start | bytes 1032200 | tf_op jit(solution)/shard_map/ppermute | solution.py:40
  184.4 0.4 collective-permute-start.28
  184.8 0.3 collective-permute-start.29
  185.1 0.8 collective-permute-done.32.refs_3_
  185.9 5.0 %collective-permute-done.30.refs_1_ = bf16[24,7168]{1,0:T(8,128)(2,1)S(1)} collective-permute-done((bf16[24,7168]{1,0:T(8,128)(2,1)S(1)}, bf16[24,7168]{1,0:T(8,128)(2,1)S(1)}, u32[]{:S(2)}, u32[]{:S(2)}) %collective-permute-start.30) | collective-permute-done | bytes 344096 | tf_op jit(solution)/shard_map/ppermute | solution.py:40
  191.0 0.3 collect.1
  191.4 0.1 collective-permute-start.33
  191.5 2.0 collective-permute-start.34
  193.5 3.0 %collective-permute-start.25 = (bf16[8,7168]{1,0:T(8,128)(2,1)S(1)}, bf16[8,7168]{1,0:T(8,128)(2,1)S(1)}, u32[]{:S(2)}, u32[]{:S(2)}) collective-permute-start(bf16[8,7168]{1,0:T(8,128)(2,1)S(1)} %get-tuple-element.61), channel_id=1, source_target_pairs={{0,64},{32,96},{64,0},{96,32},{1,65},{33,97},{65,1},{97,33},{2,66}... | collective-permute-start | bytes 344072 | tf_op jit(solution)/shard_map/ppermute | solution.py:40
  196.5 1.8 collective-permute-start.35
  198.3 2.4 %collective-permute-start.36 = (bf16[32,1792]{1,0:T(8,128)(2,1)S(1)}, bf16[32,1792]{1,0:T(8,128)(2,1)S(1)}, u32[]{:S(2)}, u32[]{:S(2)}) collective-permute-start(bf16[32,1792]{1,0:T(8,128)(2,1)S(1)} %get-tuple-element.74), channel_id=1, source_target_pairs={{0,28},{2,30},{4,0},{6,2},{8,4},{10,6},{12,8},{14,10},{16,12},{18,... | collective-permute-start | bytes 344072 | tf_op jit(solution)/shard_map/ppermute | solution.py:44
  200.7 2.9 %collective-permute-done.35.refs_7_ = bf16[32,1792]{1,0:T(8,128)(2,1)S(1)} collective-permute-done((bf16[32,1792]{1,0:T(8,128)(2,1)S(1)}, bf16[32,1792]{1,0:T(8,128)(2,1)S(1)}, u32[]{:S(2)}, u32[]{:S(2)}) %collective-permute-start.35) | collective-permute-done | bytes 114720 | tf_op jit(solution)/shard_map/ppermute | solution.py:44
  203.5 2.5 %collective-permute-done.36.refs_8_ = bf16[32,1792]{1,0:T(8,128)(2,1)S(1)} collective-permute-done((bf16[32,1792]{1,0:T(8,128)(2,1)S(1)}, bf16[32,1792]{1,0:T(8,128)(2,1)S(1)}, u32[]{:S(2)}, u32[]{:S(2)}) %collective-permute-start.36) | collective-permute-done | bytes 114720 | tf_op jit(solution)/shard_map/ppermute | solution.py:44
  206.0 0.2 merge.3
  206.2 5.5 %collective-permute-start.37 = (bf16[8,3584]{1,0:T(8,128)(2,1)S(1)}, bf16[8,3584]{1,0:T(8,128)(2,1)S(1)}, u32[]{:S(2)}, u32[]{:S(2)}) collective-permute-start(bf16[8,3584]{1,0:T(8,128)(2,1)S(1)} %get-tuple-element.76), channel_id=1, source_target_pairs={{0,8},{8,0},{16,24},{24,16},{1,9},{9,1},{17,25},{25,17},{2,10},{10... | collective-permute-start | bytes 172040 | tf_op jit(solution)/shard_map/ppermute | solution.py:48
  211.8 6.7 %collective-permute-start.38 = (bf16[8,3584]{1,0:T(8,128)(2,1)S(1)}, bf16[8,3584]{1,0:T(8,128)(2,1)S(1)}, u32[]{:S(2)}, u32[]{:S(2)}) collective-permute-start(bf16[8,3584]{1,0:T(8,128)(2,1)S(1)} %get-tuple-element.77), channel_id=1, source_target_pairs={{0,16},{8,24},{16,0},{24,8},{1,17},{9,25},{17,1},{25,9},{2,18},{10... | collective-permute-start | bytes 172040 | tf_op jit(solution)/shard_map/ppermute | solution.py:48
  218.5 0.4 collective-permute-start.39
  218.9 6.0 %collective-permute-done.38.two = bf16[8,3584]{1,0:T(8,128)(2,1)S(1)} collective-permute-done((bf16[8,3584]{1,0:T(8,128)(2,1)S(1)}, bf16[8,3584]{1,0:T(8,128)(2,1)S(1)}, u32[]{:S(2)}, u32[]{:S(2)}) %collective-permute-start.38) | collective-permute-done | bytes 57376 | tf_op jit(solution)/shard_map/ppermute | solution.py:48
  224.9 2.3 %collective-permute-done.39.three = bf16[8,3584]{1,0:T(8,128)(2,1)S(1)} collective-permute-done((bf16[8,3584]{1,0:T(8,128)(2,1)S(1)}, bf16[8,3584]{1,0:T(8,128)(2,1)S(1)}, u32[]{:S(2)}, u32[]{:S(2)}) %collective-permute-start.39) | collective-permute-done | bytes 57376 | tf_op jit(solution)/shard_map/ppermute | solution.py:48
  227.2 0.7 finish.1
  (55 shorter events, 0.5 us)
Async XLA Ops:
  1.2 13.2 %collective-permute-start.11 = (bf16[32,7680]{1,0:T(8,128)(2,1)S(1)}, bf16[32,7680]{1,0:T(8,128)(2,1)S(1)}, u32[]{:S(2)}, u32[]{:S(2)}) collective-permute-start(bf16[32,7680]{1,0:T(8,128)(2,1)S(1)} %get-tuple-element.42.refs_0_), channel_id=1, source_target_pairs={{0,96},{32,64},{64,32},{96,0},{1,97},{33,65},{65,33},{97,1},{2,98}... | collective-permute-start | bytes 1474568 | tf_op jit(solution)/shard_map/ppermute | solution.py:40
  1.7 13.0 %collective-permute-start.6 = (bf16[32,7680]{1,0:T(8,128)(2,1)S(1)}, bf16[32,7680]{1,0:T(8,128)(2,1)S(1)}, u32[]{:S(2)}, u32[]{:S(2)}) collective-permute-start(bf16[32,7680]{1,0:T(8,128)(2,1)S(1)} %get-tuple-element.42.refs_0_), channel_id=1, source_target_pairs={{0,1},{1,0},{2,3},{3,2},{4,5},{5,4},{6,7},{7,6},{8,9},{9,8},{10,11... | collective-permute-start | bytes 1474568 | tf_op jit(solution)/shard_map/ppermute | solution.py:52
  1.7 14.1 %collective-permute-start = (bf16[32,7680]{1,0:T(8,128)(2,1)S(1)}, bf16[32,7680]{1,0:T(8,128)(2,1)S(1)}, u32[]{:S(2)}, u32[]{:S(2)}) collective-permute-start(bf16[32,7680]{1,0:T(8,128)(2,1)S(1)} %get-tuple-element.42.refs_0_), channel_id=1, source_target_pairs={{0,32},{32,0},{64,96},{96,64},{1,33},{33,1},{65,97},{97,65},{2,34}... | collective-permute-start | bytes 1474568 | tf_op jit(solution)/shard_map/ppermute | solution.py:40
  3.0 22.9 %collective-permute-start.8 = (bf16[32,7680]{1,0:T(8,128)(2,1)S(1)}, bf16[32,7680]{1,0:T(8,128)(2,1)S(1)}, u32[]{:S(2)}, u32[]{:S(2)}) collective-permute-start(bf16[32,7680]{1,0:T(8,128)(2,1)S(1)} %get-tuple-element.43.refs_1_), channel_id=1, source_target_pairs={{0,32},{32,0},{64,96},{96,64},{1,33},{33,1},{65,97},{97,65},{2,34}... | collective-permute-start | bytes 1474568 | tf_op jit(solution)/shard_map/ppermute | solution.py:40
  3.8 24.0 %collective-permute-start.7 = (bf16[32,7680]{1,0:T(8,128)(2,1)S(1)}, bf16[32,7680]{1,0:T(8,128)(2,1)}, u32[]{:S(2)}, u32[]{:S(2)}) collective-permute-start(bf16[32,7680]{1,0:T(8,128)(2,1)S(1)} %get-tuple-element.43.refs_1_), channel_id=1, source_target_pairs={{0,1},{1,0},{2,3},{3,2},{4,5},{5,4},{6,7},{7,6},{8,9},{9,8},{10,11... | collective-permute-start | bytes 1474568 | tf_op jit(solution)/shard_map/ppermute | solution.py:52
  14.4 42.9 %collective-permute-start.2 = (bf16[32,7680]{1,0:T(8,128)(2,1)S(1)}, bf16[32,7680]{1,0:T(8,128)(2,1)}, u32[]{:S(2)}, u32[]{:S(2)}) collective-permute-start(bf16[32,7680]{1,0:T(8,128)(2,1)S(1)} %get-tuple-element.43.refs_1_), channel_id=1, source_target_pairs={{0,96},{32,64},{64,32},{96,0},{1,97},{33,65},{65,33},{97,1},{2,98}... | collective-permute-start | bytes 1474568 | tf_op jit(solution)/shard_map/ppermute | solution.py:40
  14.8 42.7 %collective-permute-start.12 = (bf16[32,7680]{1,0:T(8,128)(2,1)S(1)}, bf16[32,7680]{1,0:T(8,128)(2,1)}, u32[]{:S(2)}, u32[]{:S(2)}) collective-permute-start(bf16[32,7680]{1,0:T(8,128)(2,1)S(1)} %collective-permute-done.11.refs_8_), channel_id=1, source_target_pairs={{0,1},{1,0},{2,3},{3,2},{4,5},{5,4},{6,7},{7,6},{8,9},{9,8},{10,11... | collective-permute-start | bytes 1474568 | tf_op jit(solution)/shard_map/ppermute | solution.py:52
  15.8 44.1 %collective-permute-start.9 = (bf16[32,7680]{1,0:T(8,128)(2,1)S(1)}, bf16[32,7680]{1,0:T(8,128)(2,1)}, u32[]{:S(2)}, u32[]{:S(2)}) collective-permute-start(bf16[32,7680]{1,0:T(8,128)(2,1)S(1)} %collective-permute-done.refs_4_), channel_id=1, source_target_pairs={{0,1},{1,0},{2,3},{3,2},{4,5},{5,4},{6,7},{7,6},{8,9},{9,8},{10,11... | collective-permute-start | bytes 1474568 | tf_op jit(solution)/shard_map/ppermute | solution.py:52
  25.9 34.1 %collective-permute-start.1 = (bf16[32,7680]{1,0:T(8,128)(2,1)S(1)}, bf16[32,7680]{1,0:T(8,128)(2,1)}, u32[]{:S(2)}, u32[]{:S(2)}) collective-permute-start(bf16[32,7680]{1,0:T(8,128)(2,1)S(1)} %collective-permute-done.refs_4_), channel_id=1, source_target_pairs={{0,96},{32,64},{64,32},{96,0},{1,97},{33,65},{65,33},{97,1},{2,98}... | collective-permute-start | bytes 1474568 | tf_op jit(solution)/shard_map/ppermute | solution.py:40
  27.7 32.7 %collective-permute-start.10 = (bf16[32,7680]{1,0:T(8,128)(2,1)S(1)}, bf16[32,7680]{1,0:T(8,128)(2,1)}, u32[]{:S(2)}, u32[]{:S(2)}) collective-permute-start(bf16[32,7680]{1,0:T(8,128)(2,1)S(1)} %collective-permute-done.8.refs_5_), channel_id=1, source_target_pairs={{0,1},{1,0},{2,3},{3,2},{4,5},{5,4},{6,7},{7,6},{8,9},{9,8},{10,11... | collective-permute-start | bytes 1474568 | tf_op jit(solution)/shard_map/ppermute | solution.py:52
  34.4 41.7 %all-to-all-start = ((bf16[16,16,512]{2,1,0:T(8,128)(2,1)}), bf16[16,16,512]{2,1,0:T(8,128)(2,1)S(1)}, u32[]{:S(2)}, u32[]{:S(2)}) async-start(bf16[16,16,512]{2,1,0:T(8,128)(2,1)} %bitcast.4), calls=%async_computation | async-start | bytes 524288 | tf_op jit(solution)/shard_map/all_to_all | solution.py:612
  57.3 3.3 %collective-permute-start.13 = (bf16[32,7680]{1,0:T(8,128)(2,1)}, bf16[32,7680]{1,0:T(8,128)(2,1)S(1)}, u32[]{:S(2)}, u32[]{:S(2)}) collective-permute-start(bf16[32,7680]{1,0:T(8,128)(2,1)} %collective-permute-done.2.refs_9_), channel_id=1, source_target_pairs={{0,1},{1,0},{2,3},{3,2},{4,5},{5,4},{6,7},{7,6},{8,9},{9,8},{10,11... | collective-permute-start | bytes 1474568 | tf_op jit(solution)/shard_map/ppermute | solution.py:52
  57.5 14.5 %collective-permute-start.3 = (bf16[32,7680]{1,0:T(8,128)(2,1)}, bf16[32,7680]{1,0:T(8,128)(2,1)}, u32[]{:S(2)}, u32[]{:S(2)}) collective-permute-start(bf16[32,7680]{1,0:T(8,128)(2,1)} %collective-permute-done.2.refs_9_), channel_id=1, source_target_pairs={{0,32},{32,0},{64,96},{96,64},{1,33},{33,1},{65,97},{97,65},{2,34}... | collective-permute-start | bytes 1474568 | tf_op jit(solution)/shard_map/ppermute | solution.py:40
  59.9 100.0 %collective-permute-start.22 = (bf16[7168,128]{1,0:T(8,128)(2,1)}, bf16[7168,128]{1,0:T(8,128)(2,1)}, u32[]{:S(2)}, u32[]{:S(2)}) collective-permute-start(bf16[7168,128]{1,0:T(8,128)(2,1)} %gate_a.1), channel_id=1, source_target_pairs={{0,1},{1,0},{2,3},{3,2},{4,5},{5,4},{6,7},{7,6},{8,9},{9,8},{10,11... | collective-permute-start | bytes 5505032 | tf_op jit(solution)/shard_map/ppermute | solution.py:52
  60.0 102.2 %collective-permute-start.23 = (bf16[7168,128]{1,0:T(8,128)(2,1)}, bf16[7168,128]{1,0:T(8,128)(2,1)}, u32[]{:S(2)}, u32[]{:S(2)}) collective-permute-start(bf16[7168,128]{1,0:T(8,128)(2,1)} %up_a.1), channel_id=1, source_target_pairs={{0,1},{1,0},{2,3},{3,2},{4,5},{5,4},{6,7},{7,6},{8,9},{9,8},{10,11... | collective-permute-start | bytes 5505032 | tf_op jit(solution)/shard_map/ppermute | solution.py:52
  60.4 101.7 %collective-permute-start.24 = (bf16[128,7168]{1,0:T(8,128)(2,1)}, bf16[128,7168]{1,0:T(8,128)(2,1)}, u32[]{:S(2)}, u32[]{:S(2)}) collective-permute-start(bf16[128,7168]{1,0:T(8,128)(2,1)} %down_a.1), channel_id=1, source_target_pairs={{0,1},{1,0},{2,3},{3,2},{4,5},{5,4},{6,7},{7,6},{8,9},{9,8},{10,11... | collective-permute-start | bytes 5505032 | tf_op jit(solution)/shard_map/ppermute | solution.py:52
  60.6 0.8 copy-start
  61.4 18.8 %collective-permute-start.4 = (bf16[32,7680]{1,0:T(8,128)(2,1)}, bf16[32,7680]{1,0:T(8,128)(2,1)}, u32[]{:S(2)}, u32[]{:S(2)}) collective-permute-start(bf16[32,7680]{1,0:T(8,128)(2,1)} %collective-permute-done.1.refs_0_), channel_id=1, source_target_pairs={{0,1},{1,0},{2,3},{3,2},{4,5},{5,4},{6,7},{7,6},{8,9},{9,8},{10,11... | collective-permute-start | bytes 1474568 | tf_op jit(solution)/shard_map/ppermute | solution.py:52
  72.0 8.2 %collective-permute-start.5 = (bf16[32,7680]{1,0:T(8,128)(2,1)}, bf16[32,7680]{1,0:T(8,128)(2,1)}, u32[]{:S(2)}, u32[]{:S(2)}) collective-permute-start(bf16[32,7680]{1,0:T(8,128)(2,1)} %collective-permute-done.3.refs_1_), channel_id=1, source_target_pairs={{0,1},{1,0},{2,3},{3,2},{4,5},{5,4},{6,7},{7,6},{8,9},{9,8},{10,11... | collective-permute-start | bytes 1474568 | tf_op jit(solution)/shard_map/ppermute | solution.py:52
  76.0 1.0 copy-start.1
  80.1 30.7 %copy-start.4 = (bf16[7168]{0:T(1024)(128)(2,1)S(1)}, bf16[7168]{0:T(1024)(128)(2,1)}, u32[]{:S(2)}) copy-start(bf16[7168]{0:T(1024)(128)(2,1)} %param.21) | copy-start | bytes 43012
  80.1 30.7 %copy-start.3 = (bf16[2,2,7168]{2,1,0:T(2,128)(2,1)S(1)}, bf16[2,2,7168]{2,1,0:T(2,128)(2,1)}, u32[]{:S(2)}) copy-start(bf16[2,2,7168]{2,1,0:T(2,128)(2,1)} %param.18) | copy-start | bytes 172036
  82.5 36.6 %copy-start.5 = (s32[2,2,8]{2,1,0:T(2,128)S(1)}, s32[2,2,8]{2,1,0:T(2,128)}, u32[]{:S(2)}) copy-start(s32[2,2,8]{2,1,0:T(2,128)} %param.23) | copy-start | bytes 388
  82.5 36.6 %copy-start.6 = (s32[2,2,8]{2,1,0:T(2,128)S(1)}, s32[2,2,8]{2,1,0:T(2,128)}, u32[]{:S(2)}) copy-start(s32[2,2,8]{2,1,0:T(2,128)} %param.24) | copy-start | bytes 388
  82.5 36.6 %copy-start.2 = (bf16[7168,16]{0,1:T(8,128)(2,1)S(1)}, bf16[7168,16]{0,1:T(8,128)(2,1)}, u32[]{:S(2)}) copy-start(bf16[7168,16]{0,1:T(8,128)(2,1)} %param.22) | copy-start | bytes 688132
  82.6 8.2 %collective-permute-start.16 = (bf16[32,1792]{1,0:T(8,128)(2,1)S(1)}, bf16[32,1792]{1,0:T(8,128)(2,1)S(1)}, u32[]{:S(2)}, u32[]{:S(2)}) collective-permute-start(bf16[32,1792]{1,0:T(8,128)(2,1)S(1)} %get-tuple-element.47), channel_id=1, source_target_pairs={{0,4},{2,6},{4,8},{6,10},{8,12},{10,14},{12,16},{14,18},{16,20},{1... | collective-permute-start | bytes 344072 | tf_op jit(solution)/shard_map/ppermute | solution.py:44
  84.9 5.9 %collective-permute-start.17 = (bf16[32,1792]{1,0:T(8,128)(2,1)S(1)}, bf16[32,1792]{1,0:T(8,128)(2,1)S(1)}, u32[]{:S(2)}, u32[]{:S(2)}) collective-permute-start(bf16[32,1792]{1,0:T(8,128)(2,1)S(1)} %get-tuple-element.48), channel_id=1, source_target_pairs={{0,28},{2,30},{4,0},{6,2},{8,4},{10,6},{12,8},{14,10},{16,12},{18,... | collective-permute-start | bytes 344072 | tf_op jit(solution)/shard_map/ppermute | solution.py:44
  90.8 6.7 %collective-permute-start.14 = (bf16[32,3584]{1,0:T(8,128)(2,1)S(1)}, bf16[32,3584]{1,0:T(8,128)(2,1)S(1)}, u32[]{:S(2)}, u32[]{:S(2)}) collective-permute-start(bf16[32,3584]{1,0:T(8,128)(2,1)S(1)} %get-tuple-element.45), channel_id=1, source_target_pairs={{0,2},{2,4},{4,6},{6,8},{8,10},{10,12},{12,14},{14,16},{16,18},{18... | collective-permute-start | bytes 688136 | tf_op jit(solution)/shard_map/ppermute | solution.py:44
  90.8 6.7 %collective-permute-start.15 = (bf16[32,3584]{1,0:T(8,128)(2,1)S(1)}, bf16[32,3584]{1,0:T(8,128)(2,1)S(1)}, u32[]{:S(2)}, u32[]{:S(2)}) collective-permute-start(bf16[32,3584]{1,0:T(8,128)(2,1)S(1)} %get-tuple-element.46), channel_id=1, source_target_pairs={{0,30},{2,0},{4,2},{6,4},{8,6},{10,8},{12,10},{14,12},{16,14},{18,... | collective-permute-start | bytes 688136 | tf_op jit(solution)/shard_map/ppermute | solution.py:44
  97.6 10.4 %collective-permute-start.18 = (bf16[8,3584]{1,0:T(8,128)(2,1)S(1)}, bf16[8,3584]{1,0:T(8,128)(2,1)S(1)}, u32[]{:S(2)}, u32[]{:S(2)}) collective-permute-start(bf16[8,3584]{1,0:T(8,128)(2,1)S(1)} %get-tuple-element.50), channel_id=1, source_target_pairs={{0,8},{8,0},{16,24},{24,16},{1,9},{9,1},{17,25},{25,17},{2,10},{10... | collective-permute-start | bytes 172040 | tf_op jit(solution)/shard_map/ppermute | solution.py:48
  103.4 15.7 %collective-permute-start.19 = (bf16[8,3584]{1,0:T(8,128)(2,1)S(1)}, bf16[8,3584]{1,0:T(8,128)(2,1)S(1)}, u32[]{:S(2)}, u32[]{:S(2)}) collective-permute-start(bf16[8,3584]{1,0:T(8,128)(2,1)S(1)} %get-tuple-element.51), channel_id=1, source_target_pairs={{0,16},{8,24},{16,0},{24,8},{1,17},{9,25},{17,1},{25,9},{2,18},{10... | collective-permute-start | bytes 172040 | tf_op jit(solution)/shard_map/ppermute | solution.py:48
  108.0 11.2 %collective-permute-start.20 = (bf16[8,3584]{1,0:T(8,128)(2,1)S(1)}, bf16[8,3584]{1,0:T(8,128)(2,1)S(1)}, u32[]{:S(2)}, u32[]{:S(2)}) collective-permute-start(bf16[8,3584]{1,0:T(8,128)(2,1)S(1)} %get-tuple-element.52), channel_id=1, source_target_pairs={{0,24},{8,16},{16,8},{24,0},{1,25},{9,17},{17,9},{25,1},{2,26},{10... | collective-permute-start | bytes 172040 | tf_op jit(solution)/shard_map/ppermute | solution.py:48
  154.5 12.7 %collective-permute-start.26 = (bf16[32,7296]{1,0:T(8,128)(2,1)S(1)}, bf16[32,7296]{1,0:T(8,128)(2,1)S(1)}, u32[]{:S(2)}, u32[]{:S(2)}) collective-permute-start(bf16[32,7296]{1,0:T(8,128)(2,1)S(1)} %get-tuple-element.62), channel_id=1, source_target_pairs={{0,32},{32,0},{64,96},{96,64},{1,33},{33,1},{65,97},{97,65},{2,34}... | collective-permute-start | bytes 1400840 | tf_op jit(solution)/shard_map/ppermute | solution.py:40
  160.0 14.8 %collective-permute-start.27 = (bf16[32,7296]{1,0:T(8,128)(2,1)S(1)}, bf16[32,7296]{1,0:T(8,128)(2,1)S(1)}, u32[]{:S(2)}, u32[]{:S(2)}) collective-permute-start(bf16[32,7296]{1,0:T(8,128)(2,1)S(1)} %get-tuple-element.63), channel_id=1, source_target_pairs={{0,96},{32,64},{64,32},{96,0},{1,97},{33,65},{65,33},{97,1},{2,98}... | collective-permute-start | bytes 1400840 | tf_op jit(solution)/shard_map/ppermute | solution.py:40
  160.0 18.0 %collective-permute-start.21 = (bf16[32,7296]{1,0:T(8,128)(2,1)S(1)}, bf16[32,7296]{1,0:T(8,128)(2,1)S(1)}, u32[]{:S(2)}, u32[]{:S(2)}) collective-permute-start(bf16[32,7296]{1,0:T(8,128)(2,1)S(1)} %get-tuple-element.57), channel_id=1, source_target_pairs={{0,64},{32,96},{64,0},{96,32},{1,65},{33,97},{65,1},{97,33},{2,66}... | collective-permute-start | bytes 1400840 | tf_op jit(solution)/shard_map/ppermute | solution.py:40
  177.4 7.7 %collective-permute-start.31 = (bf16[24,7168]{1,0:T(8,128)(2,1)S(1)}, bf16[24,7168]{1,0:T(8,128)(2,1)S(1)}, u32[]{:S(2)}, u32[]{:S(2)}) collective-permute-start(bf16[24,7168]{1,0:T(8,128)(2,1)S(1)} %get-tuple-element.69), channel_id=1, source_target_pairs={{0,32},{32,0},{64,96},{96,64},{1,33},{33,1},{65,97},{97,65},{2,34}... | collective-permute-start | bytes 1032200 | tf_op jit(solution)/shard_map/ppermute | solution.py:40
  177.6 8.4 %collective-permute-start.32 = (bf16[24,7168]{1,0:T(8,128)(2,1)S(1)}, bf16[24,7168]{1,0:T(8,128)(2,1)S(1)}, u32[]{:S(2)}, u32[]{:S(2)}) collective-permute-start(bf16[24,7168]{1,0:T(8,128)(2,1)S(1)} %get-tuple-element.70), channel_id=1, source_target_pairs={{0,96},{32,64},{64,32},{96,0},{1,97},{33,65},{65,33},{97,1},{2,98}... | collective-permute-start | bytes 1032200 | tf_op jit(solution)/shard_map/ppermute | solution.py:40
  180.6 10.4 %collective-permute-start.30 = (bf16[24,7168]{1,0:T(8,128)(2,1)S(1)}, bf16[24,7168]{1,0:T(8,128)(2,1)S(1)}, u32[]{:S(2)}, u32[]{:S(2)}) collective-permute-start(bf16[24,7168]{1,0:T(8,128)(2,1)S(1)} %get-tuple-element.68), channel_id=1, source_target_pairs={{0,64},{32,96},{64,0},{96,32},{1,65},{33,97},{65,1},{97,33},{2,66}... | collective-permute-start | bytes 1032200 | tf_op jit(solution)/shard_map/ppermute | solution.py:40
  184.4 12.1 %collective-permute-start.28 = (bf16[8,7168]{1,0:T(8,128)(2,1)S(1)}, bf16[8,7168]{1,0:T(8,128)(2,1)S(1)}, u32[]{:S(2)}, u32[]{:S(2)}) collective-permute-start(bf16[8,7168]{1,0:T(8,128)(2,1)S(1)} %get-tuple-element.64), channel_id=1, source_target_pairs={{0,32},{32,0},{64,96},{96,64},{1,33},{33,1},{65,97},{97,65},{2,34}... | collective-permute-start | bytes 344072 | tf_op jit(solution)/shard_map/ppermute | solution.py:40
  184.8 13.5 %collective-permute-start.29 = (bf16[8,7168]{1,0:T(8,128)(2,1)S(1)}, bf16[8,7168]{1,0:T(8,128)(2,1)S(1)}, u32[]{:S(2)}, u32[]{:S(2)}) collective-permute-start(bf16[8,7168]{1,0:T(8,128)(2,1)S(1)} %get-tuple-element.65), channel_id=1, source_target_pairs={{0,96},{32,64},{64,32},{96,0},{1,97},{33,65},{65,33},{97,1},{2,98}... | collective-permute-start | bytes 344072 | tf_op jit(solution)/shard_map/ppermute | solution.py:40
  191.4 14.6 %collective-permute-start.33 = (bf16[32,3584]{1,0:T(8,128)(2,1)S(1)}, bf16[32,3584]{1,0:T(8,128)(2,1)S(1)}, u32[]{:S(2)}, u32[]{:S(2)}) collective-permute-start(bf16[32,3584]{1,0:T(8,128)(2,1)S(1)} %get-tuple-element.71), channel_id=1, source_target_pairs={{0,2},{2,4},{4,6},{6,8},{8,10},{10,12},{12,14},{14,16},{16,18},{18... | collective-permute-start | bytes 688136 | tf_op jit(solution)/shard_map/ppermute | solution.py:44
  191.5 14.5 %collective-permute-start.34 = (bf16[32,3584]{1,0:T(8,128)(2,1)S(1)}, bf16[32,3584]{1,0:T(8,128)(2,1)S(1)}, u32[]{:S(2)}, u32[]{:S(2)}) collective-permute-start(bf16[32,3584]{1,0:T(8,128)(2,1)S(1)} %get-tuple-element.72), channel_id=1, source_target_pairs={{0,30},{2,0},{4,2},{6,4},{8,6},{10,8},{12,10},{14,12},{16,14},{18,... | collective-permute-start | bytes 688136 | tf_op jit(solution)/shard_map/ppermute | solution.py:44
  193.5 7.2 %collective-permute-start.25 = (bf16[8,7168]{1,0:T(8,128)(2,1)S(1)}, bf16[8,7168]{1,0:T(8,128)(2,1)S(1)}, u32[]{:S(2)}, u32[]{:S(2)}) collective-permute-start(bf16[8,7168]{1,0:T(8,128)(2,1)S(1)} %get-tuple-element.61), channel_id=1, source_target_pairs={{0,64},{32,96},{64,0},{96,32},{1,65},{33,97},{65,1},{97,33},{2,66}... | collective-permute-start | bytes 344072 | tf_op jit(solution)/shard_map/ppermute | solution.py:40
  196.5 7.0 %collective-permute-start.35 = (bf16[32,1792]{1,0:T(8,128)(2,1)S(1)}, bf16[32,1792]{1,0:T(8,128)(2,1)S(1)}, u32[]{:S(2)}, u32[]{:S(2)}) collective-permute-start(bf16[32,1792]{1,0:T(8,128)(2,1)S(1)} %get-tuple-element.73), channel_id=1, source_target_pairs={{0,4},{2,6},{4,8},{6,10},{8,12},{10,14},{12,16},{14,18},{16,20},{1... | collective-permute-start | bytes 344072 | tf_op jit(solution)/shard_map/ppermute | solution.py:44
  198.3 7.7 %collective-permute-start.36 = (bf16[32,1792]{1,0:T(8,128)(2,1)S(1)}, bf16[32,1792]{1,0:T(8,128)(2,1)S(1)}, u32[]{:S(2)}, u32[]{:S(2)}) collective-permute-start(bf16[32,1792]{1,0:T(8,128)(2,1)S(1)} %get-tuple-element.74), channel_id=1, source_target_pairs={{0,28},{2,30},{4,0},{6,2},{8,4},{10,6},{12,8},{14,10},{16,12},{18,... | collective-permute-start | bytes 344072 | tf_op jit(solution)/shard_map/ppermute | solution.py:44
  206.2 12.7 %collective-permute-start.37 = (bf16[8,3584]{1,0:T(8,128)(2,1)S(1)}, bf16[8,3584]{1,0:T(8,128)(2,1)S(1)}, u32[]{:S(2)}, u32[]{:S(2)}) collective-permute-start(bf16[8,3584]{1,0:T(8,128)(2,1)S(1)} %get-tuple-element.76), channel_id=1, source_target_pairs={{0,8},{8,0},{16,24},{24,16},{1,9},{9,1},{17,25},{25,17},{2,10},{10... | collective-permute-start | bytes 172040 | tf_op jit(solution)/shard_map/ppermute | solution.py:48
  211.8 13.1 %collective-permute-start.38 = (bf16[8,3584]{1,0:T(8,128)(2,1)S(1)}, bf16[8,3584]{1,0:T(8,128)(2,1)S(1)}, u32[]{:S(2)}, u32[]{:S(2)}) collective-permute-start(bf16[8,3584]{1,0:T(8,128)(2,1)S(1)} %get-tuple-element.77), channel_id=1, source_target_pairs={{0,16},{8,24},{16,0},{24,8},{1,17},{9,25},{17,1},{25,9},{2,18},{10... | collective-permute-start | bytes 172040 | tf_op jit(solution)/shard_map/ppermute | solution.py:48
  218.5 8.7 %collective-permute-start.39 = (bf16[8,3584]{1,0:T(8,128)(2,1)S(1)}, bf16[8,3584]{1,0:T(8,128)(2,1)S(1)}, u32[]{:S(2)}, u32[]{:S(2)}) collective-permute-start(bf16[8,3584]{1,0:T(8,128)(2,1)S(1)} %get-tuple-element.78), channel_id=1, source_target_pairs={{0,24},{8,16},{16,8},{24,0},{1,25},{9,17},{17,9},{25,1},{2,26},{10... | collective-permute-start | bytes 172040 | tf_op jit(solution)/shard_map/ppermute | solution.py:48
